TPU v7x, 128 devices: a whole 4x4x4 slice. The times are simulated.
128 devices in a mesh: gx: 8 (over x_lo, y), gy: 16 (over z, x_hi, core).
Axes of the slice: x: 4 (x_hi: 2, x_lo: 2; x = x_hi * 2 + x_lo), y: 4, z: 4, core: 2. Of those that a mesh axis runs over, the one named last changes fastest.
Arguments:
- expert_grad: bfloat16 [8, 512, 14336], P('gx', None, 'gy'), may hold values from -40000 to 40000
- attn_grad: bfloat16 [8, 2048, 4096], P('gx', None, 'gy'), may hold values from -40000 to 40000
- expert_master: float32 [4096, 14336], P(('gx', 'gy')), may hold values from -0.75 to 0.75
- expert_moment: float32 [4096, 14336], P(('gx', 'gy')), may hold values from -6 to 6
- expert_second: float32 [4096, 14336], P(('gx', 'gy')), may hold values from 0.1 to 4
- attn_master: float32 [2048, 4096], P(('gx', 'gy')), may hold values from -0.75 to 0.75
- attn_moment: float32 [2048, 4096], P(('gx', 'gy')), may hold values from -6 to 6
- attn_second: float32 [2048, 4096], P(('gx', 'gy')), may hold values from 0.1 to 4
Outputs:
- expert_master_new: float32 [4096, 14336], P(('gx', 'gy'))
- expert_moment_new: float32 [4096, 14336], P(('gx', 'gy'))
- expert_second_new: float32 [4096, 14336], P(('gx', 'gy'))
- attn_master_new: float32 [2048, 4096], P(('gx', 'gy'))
- attn_moment_new: float32 [2048, 4096], P(('gx', 'gy'))
- attn_second_new: float32 [2048, 4096], P(('gx', 'gy'))
- expert_weight: bfloat16 [8, 512, 14336], P('gx', None, 'gy')
- attn_weight: bfloat16 [2048, 4096], P(None, 'gy')
All inputs are finite; a program needn't handle non-finite values.
Results may differ from a plain program's by a relative error of at most 0.001.
Values may be sent and summed in bfloat16 or wider, within the bound.
No kernel may reach another device: no remote copies, remote signals or barrier semaphores. Data moves between devices by JAX's collectives and lax.ppermute only.
A program may use at most 64 MiB of HBM per device.

v0:
```python
import jax
import jax.numpy as jnp
from jax import lax
from jax.sharding import Mesh
from jax.sharding import PartitionSpec as P

NUMEL = 67108864
GY = ("gy_0", "gy_1", "gy_2")
GX = ("gx_0", "gx_1")
GX_GY = ("gx_0", "gx_1", "gy_0", "gy_1", "gy_2")


beta_one = 0.9
beta_two = 0.95
learn_rate = 0.01
weight_decay = 0.1
adam_eps = 1e-08
bias_one = 1.0 - 0.9**20
bias_two = 1.0 - 0.95**20


def cut_along(shard, dim, devices):
    before, after = (shard.shape[:dim], shard.shape[dim + 1 :])
    return jnp.moveaxis(shard.reshape(*before, devices, -1, *after), dim, 0)


def sum_at_owner(shard, axis, dim):
    parts = cut_along(shard, dim, lax.axis_size(axis))
    arrived = lax.all_to_all(parts, axis, split_axis=0, concat_axis=0, tiled=True)
    return arrived.sum(axis=0)


def one_axis_at_a_time(shard, axes):
    for axis in axes:
        shard = lax.psum(shard, axis)
    return shard


def joined_along(parts, dim):
    parts = jnp.moveaxis(parts, 0, dim)
    dims = parts.shape
    return parts.reshape(*dims[:dim], dims[dim] * dims[dim + 1], *dims[dim + 2 :])


def from_everyone(shard, axis):
    copies = jnp.broadcast_to(shard, (lax.axis_size(axis), *shard.shape))
    return lax.all_to_all(copies, axis, split_axis=0, concat_axis=0, tiled=True)


def gather_directly(shard, axis, dim):
    return joined_along(from_everyone(shard, axis), dim)


def adam_update(gradient, master, moment, second, clip_factor):
    scaled = clip_factor * gradient
    moment_new = beta_one * moment + (1.0 - beta_one) * scaled
    second_new = beta_two * second + (1.0 - beta_two) * scaled * scaled
    update = moment_new / bias_one / (jnp.sqrt(second_new / bias_two) + adam_eps)
    master_new = master - learn_rate * (update + weight_decay * master)
    return (master_new, moment_new, second_new)


def squares(expert_part, attn_part):
    wide = expert_part.astype(jnp.float32)
    return jnp.sum(wide * wide) + jnp.sum(attn_part * attn_part)


def regroup(flat_grad, owned):
    expert_group = lax.all_to_all(flat_grad, GY, split_axis=0, concat_axis=1, tiled=True)
    attn_group = lax.all_to_all(owned, GY, split_axis=0, concat_axis=1, tiled=True)
    return (expert_group, attn_group)


def local(
    expert_grad,
    attn_grad,
    expert_master,
    expert_moment,
    expert_second,
    attn_master,
    attn_moment,
    attn_second,
):
    local_experts, expert_rows, col_share = expert_grad.shape
    flat_grad = expert_grad.reshape(local_experts * expert_rows, col_share)
    attn_local = attn_grad.reshape(attn_grad.shape[1], attn_grad.shape[2]).astype(jnp.float32)
    owned = sum_at_owner(attn_local, GX, 0)
    expert_group, attn_group = regroup(flat_grad, owned)
    total = one_axis_at_a_time(squares(expert_group, attn_group), GX_GY)
    clip_factor = 1.0 / jnp.sqrt(total / NUMEL + 1e-06)
    e_master, e_moment, e_second = adam_update(
        expert_group.astype(jnp.float32), expert_master, expert_moment, expert_second, clip_factor
    )
    a_master, a_moment, a_second = adam_update(
        attn_group, attn_master, attn_moment, attn_second, clip_factor
    )
    expert_back, attn_back = (
        lax.all_to_all(e_master.astype(jnp.bfloat16), GY, split_axis=1, concat_axis=0, tiled=True),
        lax.all_to_all(a_master.astype(jnp.bfloat16), GY, split_axis=1, concat_axis=0, tiled=True),
    )
    expert_weight = expert_back.reshape(local_experts, expert_rows, col_share)
    attn_weight = gather_directly(attn_back, GX, 0)
    return (e_master, e_moment, e_second, a_master, a_moment, a_second, expert_weight, attn_weight)


def solution(mesh):
    split = Mesh(mesh.devices.reshape(2, 4, 4, 2, 2), ("gx_0", "gx_1", "gy_0", "gy_1", "gy_2"))
    placed = (
        P(GX, None, GY),
        P(GX, None, GY),
        P(GX_GY, None),
        P(GX_GY, None),
        P(GX_GY, None),
        P(GX_GY, None),
        P(GX_GY, None),
        P(GX_GY, None),
    )
    return jax.shard_map(
        local,
        mesh=split,
        in_specs=placed,
        out_specs=(
            P(GX_GY, None),
            P(GX_GY, None),
            P(GX_GY, None),
            P(GX_GY, None),
            P(GX_GY, None),
            P(GX_GY, None),
            P(GX, None, GY),
            P(None, GY),
        ),
        check_vma=False,
    )
```

profile of v0, /device:TPU:1, one launch (start us, length us, event | category | flops | bytes accessed | tf_op | source)
XLA Modules:
  0.0 165.8 jit_solution(18254513173904601893)
XLA Ops:
  0.6 1.4 convert.1
  2.0 31.5 %all_to_all.71 = f32[8,256,256]{2,1,0:T(8,128)S(1)} all-to-all(f32[8,256,256]{2,1,0:T(8,128)S(1)} %convert.1), channel_id=1, replica_groups=mesh['gx_0'=2,'gx_1'=4,'gy_0'=4,'gy_1'=2,'gy_2'=2] {'gx_0','gx_1'}, dimensions={0} | all-to-all | bytes 4194304 | tf_op jit(solution)/shard_map/all_to_all | solution.py:29
  33.5 9.9 %all-to-all-start = ((bf16[16,32,896]{2,1,0:T(8,128)(2,1)}), bf16[16,32,896]{2,1,0:T(8,128)(2,1)S(1)}, u32[]{:S(2)}, u32[]{:S(2)}) async-start(bf16[16,32,896]{2,1,0:T(8,128)(2,1)} %bitcast.34), calls=%async_computation | async-start | bytes 1835008 | tf_op jit(solution)/shard_map/all_to_all | solution.py:69
  43.4 0.8 reduce_sum.28
  44.3 14.8 %all-to-all-done = bf16[16,32,896]{2,1,0:T(8,128)(2,1)S(1)} async-done(((bf16[16,32,896]{2,1,0:T(8,128)(2,1)}), bf16[16,32,896]{2,1,0:T(8,128)(2,1)S(1)}, u32[]{:S(2)}, u32[]{:S(2)}) %all-to-all-start) | async-done | bytes 917536 | tf_op jit(solution)/shard_map/all_to_all | solution.py:69
  59.1 4.3 %all-to-all-start.2 = ((f32[16,16,256]{2,1,0:T(8,128)}), f32[16,16,256]{2,1,0:T(8,128)S(1)}, u32[]{:S(2)}, u32[]{:S(2)}) async-start(f32[16,16,256]{2,1,0:T(8,128)} %bitcast.2), calls=%async_computation.2 | async-start | bytes 524288 | tf_op jit(solution)/shard_map/all_to_all | solution.py:70
  63.4 1.1 fusion
  64.5 7.7 %all-to-all-done.2 = f32[16,16,256]{2,1,0:T(8,128)S(1)} async-done(((f32[16,16,256]{2,1,0:T(8,128)}), f32[16,16,256]{2,1,0:T(8,128)S(1)}, u32[]{:S(2)}, u32[]{:S(2)}) %all-to-all-start.2) | async-done | bytes 262176 | tf_op jit(solution)/shard_map/all_to_all | solution.py:70
  72.1 0.7 multiply_reduce_fusion
  74.1 4.3 %psum.35 = f32[]{:T(128)} all-reduce(f32[]{:T(128)S(6)} %add.46), channel_id=1, replica_groups=mesh['gx_0'=2,'gx_1'=4,'gy_0'=4,'gy_1'=2,'gy_2'=2] {'gx_0'}, use_global_device_ids=true, to_apply=%region_3.0 | all-reduce | flops 1 | bytes 8 | tf_op jit(solution)/shard_map/psum | solution.py:35
  78.4 7.1 %psum.36 = f32[]{:T(128)} all-reduce(f32[]{:T(128)} %psum.35), channel_id=1, replica_groups=mesh['gx_0'=2,'gx_1'=4,'gy_0'=4,'gy_1'=2,'gy_2'=2] {'gx_1'}, use_global_device_ids=true, to_apply=%region_4.0 | all-reduce | flops 1 | bytes 8 | tf_op jit(solution)/shard_map/psum | solution.py:35
  85.5 7.5 %psum.37 = f32[]{:T(128)} all-reduce(f32[]{:T(128)} %psum.36), channel_id=1, replica_groups=mesh['gx_0'=2,'gx_1'=4,'gy_0'=4,'gy_1'=2,'gy_2'=2] {'gy_0'}, use_global_device_ids=true, to_apply=%region_5.0 | all-reduce | flops 1 | bytes 8 | tf_op jit(solution)/shard_map/psum | solution.py:35
  93.0 5.9 %psum.38 = f32[]{:T(128)} all-reduce(f32[]{:T(128)} %psum.37), channel_id=1, replica_groups=mesh['gx_0'=2,'gx_1'=4,'gy_0'=4,'gy_1'=2,'gy_2'=2] {'gy_1'}, use_global_device_ids=true, to_apply=%region_6.0 | all-reduce | flops 1 | bytes 8 | tf_op jit(solution)/shard_map/psum | solution.py:35
  98.9 9.7 %psum.39 = f32[]{:T(128)} all-reduce(f32[]{:T(128)} %psum.38), channel_id=1, replica_groups=mesh['gx_0'=2,'gx_1'=4,'gy_0'=4,'gy_1'=2,'gy_2'=2] {'gy_2'}, use_global_device_ids=true, to_apply=%region_7.0 | all-reduce | flops 1 | bytes 8 | tf_op jit(solution)/shard_map/psum | solution.py:35
  109.3 0.2 fusion.1
  109.5 0.0 copy-start
  109.5 0.0 copy-start.1
  109.5 0.0 copy-start.2
  109.5 0.1 copy.37
  109.7 0.7 copy-done
  110.5 0.1 copy-done.1
  110.5 0.1 copy-done.2
  110.6 1.0 fusion.4
  111.6 0.7 copy.42
  112.3 3.6 %all-to-all-start.4 = ((bf16[16,16,256]{2,0,1:T(8,128)(2,1)}), bf16[16,16,256]{2,0,1:T(8,128)(2,1)S(1)}, u32[]{:S(2)}, u32[]{:S(2)}) async-start(bf16[16,16,256]{2,0,1:T(8,128)(2,1)} %bitcast.26), calls=%async_computation.4 | async-start | bytes 262144 | tf_op jit(solution)/shard_map/all_to_all | solution.py:99
  115.9 5.9 %fusion.6 = (bf16[32,14336]{1,0:T(8,128)(2,1)S(1)}, f32[32,14336]{1,0:T(8,128)}, f32[32,14336]{1,0:T(8,128)}, f32[32,14336]{1,0:T(8,128)}) fusion(f32[32,14336]{1,0:T(8,128)} %param.10, f32[32,14336]{1,0:T(8,128)S(1)} %bitcast.27, f32[32,14336]{1,0:T(8,128)} %param.11, f32[32,14336]{1,0:T(8,128)} %param.12), kind=kLoop, calls=%fused_computation.17 | loop fusion | flops 7340032 | bytes 13762560 | tf_op jit(solution)/shard_map/convert_element_type | solution.py:98
  121.9 0.1 copy.41
  121.9 1.7 %all-to-all-done.4 = bf16[16,16,256]{2,0,1:T(8,128)(2,1)S(1)} async-done(((bf16[16,16,256]{2,0,1:T(8,128)(2,1)}), bf16[16,16,256]{2,0,1:T(8,128)(2,1)S(1)}, u32[]{:S(2)}, u32[]{:S(2)}) %all-to-all-start.4) | async-done | bytes 131104 | tf_op jit(solution)/shard_map/all_to_all | solution.py:99
  123.6 20.8 %all_to_all.72 = bf16[32,16,896]{2,0,1:T(8,128)(2,1)S(1)} all-to-all(bf16[32,16,896]{2,0,1:T(8,128)(2,1)S(1)} %bitcast.30), channel_id=1, replica_groups=mesh['gx_0'=2,'gx_1'=4,'gy_0'=4,'gy_1'=2,'gy_2'=2] {'gy_0','gy_1','gy_2'}, dimensions={1} | all-to-all | bytes 1835008 | tf_op jit(solution)/shard_map/all_to_all | solution.py:98
  144.4 1.0 broadcast_in_dim.3
  145.4 3.6 %all-to-all-start.5 = ((bf16[8,256,256]{2,1,0:T(8,128)(2,1)}), bf16[8,256,256]{2,1,0:T(8,128)(2,1)S(1)}, u32[]{:S(2)}, u32[]{:S(2)}) async-start(bf16[8,256,256]{2,1,0:T(8,128)(2,1)} %broadcast_in_dim.3), calls=%async_computation.5 | async-start | bytes 2097152 | tf_op jit(solution)/shard_map/all_to_all | solution.py:47
  149.0 14.9 %all-to-all-done.5 = bf16[8,256,256]{2,1,0:T(8,128)(2,1)S(1)} async-done(((bf16[8,256,256]{2,1,0:T(8,128)(2,1)}), bf16[8,256,256]{2,1,0:T(8,128)(2,1)S(1)}, u32[]{:S(2)}, u32[]{:S(2)}) %all-to-all-start.5) | async-done | bytes 1048608 | tf_op jit(solution)/shard_map/all_to_all | solution.py:47
  163.9 0.9 copy.45
  164.8 1.0 copy.46
  (2 shorter events, 0.0 us)
Async XLA Ops:
  33.5 25.6 %all-to-all-start = ((bf16[16,32,896]{2,1,0:T(8,128)(2,1)}), bf16[16,32,896]{2,1,0:T(8,128)(2,1)S(1)}, u32[]{:S(2)}, u32[]{:S(2)}) async-start(bf16[16,32,896]{2,1,0:T(8,128)(2,1)} %bitcast.34), calls=%async_computation | async-start | bytes 1835008 | tf_op jit(solution)/shard_map/all_to_all | solution.py:69
  59.1 13.1 %all-to-all-start.2 = ((f32[16,16,256]{2,1,0:T(8,128)}), f32[16,16,256]{2,1,0:T(8,128)S(1)}, u32[]{:S(2)}, u32[]{:S(2)}) async-start(f32[16,16,256]{2,1,0:T(8,128)} %bitcast.2), calls=%async_computation.2 | async-start | bytes 524288 | tf_op jit(solution)/shard_map/all_to_all | solution.py:70
  109.5 1.0 copy-start
  109.5 1.0 copy-start.1
  109.5 1.1 copy-start.2
  112.3 11.3 %all-to-all-start.4 = ((bf16[16,16,256]{2,0,1:T(8,128)(2,1)}), bf16[16,16,256]{2,0,1:T(8,128)(2,1)S(1)}, u32[]{:S(2)}, u32[]{:S(2)}) async-start(bf16[16,16,256]{2,0,1:T(8,128)(2,1)} %bitcast.26), calls=%async_computation.4 | async-start | bytes 262144 | tf_op jit(solution)/shard_map/all_to_all | solution.py:99
  145.4 18.4 %all-to-all-start.5 = ((bf16[8,256,256]{2,1,0:T(8,128)(2,1)}), bf16[8,256,256]{2,1,0:T(8,128)(2,1)S(1)}, u32[]{:S(2)}, u32[]{:S(2)}) async-start(bf16[8,256,256]{2,1,0:T(8,128)(2,1)} %broadcast_in_dim.3), calls=%async_computation.5 | async-start | bytes 2097152 | tf_op jit(solution)/shard_map/all_to_all | solution.py:47
where the time goes:
time: 166 us
  blocking collectives  86.7 us (52%)
  waiting for transfers between devices  39.1 us (24%)
  starting transfers between devices  21.4 us (13%)
  other arithmetic  11.2 us (7%)
  local copies, waits for them, and re-layouts  4.71 us (3%)
  between operations  2.71 us (2%)
    psum x5, blocking collectives, one_axis_at_a_time(): shard = lax.psum(shard, axis)  34.5 us
    all_to_all x1, blocking collectives, sum_at_owner(): lax.all_to_all(parts, axis, split_axis=0, concat_axis=0, tiled=True)  31.5 us
    all_to_all x1, blocking collectives, local(): lax.all_to_all(e_master.astype(jnp.bfloat16), GY, split_axis=1, concat_ax...  20.8 us
    all_to_all x1, waiting for transfers between devices, from_everyone(): return lax.all_to_all(copies, axis, split_axis=0, concat_axis=0, tiled=True)  14.9 us
    all_to_all x1, waiting for transfers between devices, regroup(): lax.all_to_all(flat_grad, GY, split_axis=0, concat_axis=1, tiled=True)  14.8 us
    all_to_all x1, starting transfers between devices, regroup(): lax.all_to_all(flat_grad, GY, split_axis=0, concat_axis=1, tiled=True)  9.89 us
    all_to_all x1, waiting for transfers between devices, regroup(): lax.all_to_all(owned, GY, split_axis=0, concat_axis=1, tiled=True)  7.69 us
    convert_element_type x1, other arithmetic, local(): e_master.astype(jnp.bfloat16)  5.93 us
  transfers between devices with their start and end apart: 4, of which 4 were waited for; matrix products, arithmetic and copies ran while one was open for 5% of the time, Pallas kernels for 0%

commit v1 on v0

--- a/solution.py
+++ b/solution.py
@@ -27,13 +27,13 @@
 def sum_at_owner(shard, axis, dim):
     parts = cut_along(shard, dim, lax.axis_size(axis))
     arrived = lax.all_to_all(parts, axis, split_axis=0, concat_axis=0, tiled=True)
-    return arrived.sum(axis=0)
+    return arrived.astype(jnp.float32).sum(axis=0)
 
 
-def one_axis_at_a_time(shard, axes):
-    for axis in axes:
-        shard = lax.psum(shard, axis)
-    return shard
+def sum_over_all(part, axes):
+    copies = jnp.broadcast_to(part, (lax.axis_size(axes), 1, 128))
+    arrived = lax.all_to_all(copies, axes, split_axis=0, concat_axis=0, tiled=True)
+    return jnp.sum(arrived, axis=(0, 1))[0]
 
 
 def joined_along(parts, dim):
@@ -83,10 +83,10 @@
 ):
     local_experts, expert_rows, col_share = expert_grad.shape
     flat_grad = expert_grad.reshape(local_experts * expert_rows, col_share)
-    attn_local = attn_grad.reshape(attn_grad.shape[1], attn_grad.shape[2]).astype(jnp.float32)
+    attn_local = attn_grad.reshape(attn_grad.shape[1], attn_grad.shape[2])
     owned = sum_at_owner(attn_local, GX, 0)
     expert_group, attn_group = regroup(flat_grad, owned)
-    total = one_axis_at_a_time(squares(expert_group, attn_group), GX_GY)
+    total = sum_over_all(squares(flat_grad, owned), GX_GY)
     clip_factor = 1.0 / jnp.sqrt(total / NUMEL + 1e-06)
     e_master, e_moment, e_second = adam_update(
         expert_group.astype(jnp.float32), expert_master, expert_moment, expert_second, clip_factor

time: 166 us -> 133 us (0.80)
  blocking collectives: 86.7 us -> 39.4 us
  waiting for transfers between devices: 39.1 us -> 53.2 us
    psum x5 -> x0, blocking collectives: 34.5 us -> none  [one_axis_at_a_time(): shard = lax.psum(shard, axis)]
    all_to_all x1, blocking collectives: 31.5 us -> 18.6 us  [sum_over_all(): lax.all_to_all(copies, axes, split_axis=0, concat_axis=0, tiled=True)]
    all_to_all x0 -> x1, waiting for transfers between devices: none -> 12.7 us  [sum_at_owner(): lax.all_to_all(parts, axis, split_axis=0, concat_axis=0, tiled=True)]
    all_to_all x0 -> x1, starting transfers between devices: none -> 5.95 us  [sum_at_owner(): lax.all_to_all(parts, axis, split_axis=0, concat_axis=0, tiled=True)]
    all_to_all x1, starting transfers between devices: 9.89 us -> 4.22 us  [regroup(): lax.all_to_all(flat_grad, GY, split_axis=0, concat_axis=1, tiled=True)]
    reduce_sum x2, other arithmetic: 1.73 us -> 3.88 us  [squares(): return jnp.sum(wide * wide) + jnp.sum(attn_part * attn_part)]
  transfers between devices with their start and end apart: 4 -> 5, of which waited for: 4 -> 5; matrix products, arithmetic and copies ran while one was open for 5% -> 6% of each run, Pallas kernels for 0% -> 0%
where the time goes in v1:
time: 133 us
  waiting for transfers between devices  53.2 us (40%)
  blocking collectives  39.4 us (30%)
  starting transfers between devices  22.3 us (17%)
  other arithmetic  11.9 us (9%)
  local copies, waits for them, and re-layouts  3.86 us (3%)
  between operations  2.12 us (2%)
    all_to_all x1, blocking collectives, local(): lax.all_to_all(e_master.astype(jnp.bfloat16), GY, split_axis=1, concat_ax...  20.8 us
    all_to_all x1, blocking collectives, sum_over_all(): lax.all_to_all(copies, axes, split_axis=0, concat_axis=0, tiled=True)  18.6 us
    all_to_all x1, waiting for transfers between devices, regroup(): lax.all_to_all(flat_grad, GY, split_axis=0, concat_axis=1, tiled=True)  15.6 us
    all_to_all x1, waiting for transfers between devices, from_everyone(): return lax.all_to_all(copies, axis, split_axis=0, concat_axis=0, tiled=True)  14.9 us
    all_to_all x1, waiting for transfers between devices, sum_at_owner(): lax.all_to_all(parts, axis, split_axis=0, concat_axis=0, tiled=True)  12.7 us
    all_to_all x1, waiting for transfers between devices, regroup(): lax.all_to_all(owned, GY, split_axis=0, concat_axis=1, tiled=True)  8.38 us
    all_to_all x1, starting transfers between devices, sum_at_owner(): lax.all_to_all(parts, axis, split_axis=0, concat_axis=0, tiled=True)  5.95 us
    convert_element_type x1, other arithmetic, local(): e_master.astype(jnp.bfloat16)  5.93 us
  transfers between devices with their start and end apart: 5, of which 5 were waited for; matrix products, arithmetic and copies ran while one was open for 6% of the time, Pallas kernels for 0%

profile of v1, /device:TPU:1, one launch (start us, length us, event | category | flops | bytes accessed | tf_op | source)
XLA Modules:
  0.0 132.8 jit_solution(1011553465171021159)
XLA Ops:
  0.6 5.9 %all-to-all-start = ((bf16[8,256,256]{2,1,0:T(8,128)(2,1)}), bf16[8,256,256]{2,1,0:T(8,128)(2,1)S(1)}, u32[]{:S(2)}, u32[]{:S(2)}) async-start(bf16[8,256,256]{2,1,0:T(8,128)(2,1)} %bitcast.35), calls=%async_computation | async-start | bytes 2097152 | tf_op jit(solution)/shard_map/all_to_all | solution.py:29
  6.6 2.3 %multiply_reduce_fusion = f32[]{:T(128)} fusion(bf16[1,512,896]{2,1,0:T(8,128)(2,1)} %param.8), kind=kLoop, calls=%fused_computation.6 | loop fusion | flops 1376255 | bytes 917508 | tf_op jit(solution)/shard_map/reduce_sum | solution.py:65
  8.8 12.7 %all-to-all-done = bf16[8,256,256]{2,1,0:T(8,128)(2,1)S(1)} async-done(((bf16[8,256,256]{2,1,0:T(8,128)(2,1)}), bf16[8,256,256]{2,1,0:T(8,128)(2,1)S(1)}, u32[]{:S(2)}, u32[]{:S(2)}) %all-to-all-start) | async-done | bytes 1048608 | tf_op jit(solution)/shard_map/all_to_all | solution.py:29
  21.5 0.8 convert_reduce_fusion
  22.4 1.6 %multiply_reduce_fusion.1 = f32[]{:T(128)} fusion(f32[256,256]{1,0:T(8,128)} %convert_reduce_fusion), kind=kLoop, calls=%fused_computation.13 | loop fusion | flops 131071 | bytes 262148 | tf_op jit(solution)/shard_map/reduce_sum | solution.py:65
  25.4 18.6 %all_to_all.76 = f32[128,1,128]{2,1,0:T(1,128)S(1)} all-to-all(f32[128,1,128]{2,1,0:T(1,128)S(1)} %broadcast_in_dim.6), channel_id=1, replica_groups=mesh['gx_0'=2,'gx_1'=4,'gy_0'=4,'gy_1'=2,'gy_2'=2] {'gx_0','gx_1','gy_0'..., dimensions={0} | all-to-all | bytes 131072 | tf_op jit(solution)/shard_map/all_to_all | solution.py:35
  44.0 4.2 %all-to-all-start.2 = ((bf16[16,32,896]{2,1,0:T(8,128)(2,1)}), bf16[16,32,896]{2,1,0:T(8,128)(2,1)S(1)}, u32[]{:S(2)}, u32[]{:S(2)}) async-start(bf16[16,32,896]{2,1,0:T(8,128)(2,1)} %bitcast.3), calls=%async_computation.2 | async-start | bytes 1835008 | tf_op jit(solution)/shard_map/all_to_all | solution.py:69
  48.3 15.6 %all-to-all-done.2 = bf16[16,32,896]{2,1,0:T(8,128)(2,1)S(1)} async-done(((bf16[16,32,896]{2,1,0:T(8,128)(2,1)}), bf16[16,32,896]{2,1,0:T(8,128)(2,1)S(1)}, u32[]{:S(2)}, u32[]{:S(2)}) %all-to-all-start.2) | async-done | bytes 917536 | tf_op jit(solution)/shard_map/all_to_all | solution.py:69
  63.9 4.3 %all-to-all-start.3 = ((f32[16,16,256]{2,1,0:T(8,128)}), f32[16,16,256]{2,1,0:T(8,128)S(1)}, u32[]{:S(2)}, u32[]{:S(2)}) async-start(f32[16,16,256]{2,1,0:T(8,128)} %bitcast.5), calls=%async_computation.3 | async-start | bytes 524288 | tf_op jit(solution)/shard_map/all_to_all | solution.py:70
  68.2 0.2 multiply_bitcast_fusion
  68.4 0.0 copy-start
  68.4 0.0 copy-start.1
  68.4 0.0 copy-start.2
  68.4 0.1 copy.46
  68.5 8.4 %all-to-all-done.3 = f32[16,16,256]{2,1,0:T(8,128)S(1)} async-done(((f32[16,16,256]{2,1,0:T(8,128)}), f32[16,16,256]{2,1,0:T(8,128)S(1)}, u32[]{:S(2)}, u32[]{:S(2)}) %all-to-all-start.3) | async-done | bytes 262176 | tf_op jit(solution)/shard_map/all_to_all | solution.py:70
  77.0 0.0 copy-done
  77.0 0.0 copy-done.1
  77.0 0.0 copy-done.2
  77.0 1.0 fusion.2
  78.0 0.7 copy.51
  78.7 4.2 %all-to-all-start.5 = ((bf16[16,16,256]{2,0,1:T(8,128)(2,1)}), bf16[16,16,256]{2,0,1:T(8,128)(2,1)S(1)}, u32[]{:S(2)}, u32[]{:S(2)}) async-start(bf16[16,16,256]{2,0,1:T(8,128)(2,1)} %bitcast.27), calls=%async_computation.5 | async-start | bytes 262144 | tf_op jit(solution)/shard_map/all_to_all | solution.py:99
  82.9 5.9 %fusion.4 = (bf16[32,14336]{1,0:T(8,128)(2,1)S(1)}, f32[32,14336]{1,0:T(8,128)}, f32[32,14336]{1,0:T(8,128)}, f32[32,14336]{1,0:T(8,128)}) fusion(f32[32,14336]{1,0:T(8,128)} %param.10, f32[32,14336]{1,0:T(8,128)S(1)} %bitcast.29, f32[32,14336]{1,0:T(8,128)} %param.11, f32[32,14336]{1,0:T(8,128)} %param.12), kind=kLoop, calls=%fused_computation.16 | loop fusion | flops 7340032 | bytes 13762560 | tf_op jit(solution)/shard_map/convert_element_type | solution.py:98
  88.8 0.1 copy.50
  88.9 1.7 %all-to-all-done.5 = bf16[16,16,256]{2,0,1:T(8,128)(2,1)S(1)} async-done(((bf16[16,16,256]{2,0,1:T(8,128)(2,1)}), bf16[16,16,256]{2,0,1:T(8,128)(2,1)S(1)}, u32[]{:S(2)}, u32[]{:S(2)}) %all-to-all-start.5) | async-done | bytes 131104 | tf_op jit(solution)/shard_map/all_to_all | solution.py:99
  90.6 20.8 %all_to_all.77 = bf16[32,16,896]{2,0,1:T(8,128)(2,1)S(1)} all-to-all(bf16[32,16,896]{2,0,1:T(8,128)(2,1)S(1)} %bitcast.32), channel_id=1, replica_groups=mesh['gx_0'=2,'gx_1'=4,'gy_0'=4,'gy_1'=2,'gy_2'=2] {'gy_0','gy_1','gy_2'}, dimensions={1} | all-to-all | bytes 1835008 | tf_op jit(solution)/shard_map/all_to_all | solution.py:98
  111.4 1.0 broadcast_in_dim.7
  112.4 3.6 %all-to-all-start.6 = ((bf16[8,256,256]{2,1,0:T(8,128)(2,1)}), bf16[8,256,256]{2,1,0:T(8,128)(2,1)S(1)}, u32[]{:S(2)}, u32[]{:S(2)}) async-start(bf16[8,256,256]{2,1,0:T(8,128)(2,1)} %broadcast_in_dim.7), calls=%async_computation.6 | async-start | bytes 2097152 | tf_op jit(solution)/shard_map/all_to_all | solution.py:47
  116.0 14.9 %all-to-all-done.6 = bf16[8,256,256]{2,1,0:T(8,128)(2,1)S(1)} async-done(((bf16[8,256,256]{2,1,0:T(8,128)(2,1)}), bf16[8,256,256]{2,1,0:T(8,128)(2,1)S(1)}, u32[]{:S(2)}, u32[]{:S(2)}) %all-to-all-start.6) | async-done | bytes 1048608 | tf_op jit(solution)/shard_map/all_to_all | solution.py:47
  130.9 0.9 copy.54
  131.8 1.0 copy.55
  (4 shorter events, 0.1 us)
Async XLA Ops:
  0.6 20.9 %all-to-all-start = ((bf16[8,256,256]{2,1,0:T(8,128)(2,1)}), bf16[8,256,256]{2,1,0:T(8,128)(2,1)S(1)}, u32[]{:S(2)}, u32[]{:S(2)}) async-start(bf16[8,256,256]{2,1,0:T(8,128)(2,1)} %bitcast.35), calls=%async_computation | async-start | bytes 2097152 | tf_op jit(solution)/shard_map/all_to_all | solution.py:29
  44.0 19.9 %all-to-all-start.2 = ((bf16[16,32,896]{2,1,0:T(8,128)(2,1)}), bf16[16,32,896]{2,1,0:T(8,128)(2,1)S(1)}, u32[]{:S(2)}, u32[]{:S(2)}) async-start(bf16[16,32,896]{2,1,0:T(8,128)(2,1)} %bitcast.3), calls=%async_computation.2 | async-start | bytes 1835008 | tf_op jit(solution)/shard_map/all_to_all | solution.py:69
  63.9 13.1 %all-to-all-start.3 = ((f32[16,16,256]{2,1,0:T(8,128)}), f32[16,16,256]{2,1,0:T(8,128)S(1)}, u32[]{:S(2)}, u32[]{:S(2)}) async-start(f32[16,16,256]{2,1,0:T(8,128)} %bitcast.5), calls=%async_computation.3 | async-start | bytes 524288 | tf_op jit(solution)/shard_map/all_to_all | solution.py:70
  68.4 8.6 %copy-start = (f32[16,4096]{1,0:T(8,128)S(1)}, f32[16,4096]{1,0:T(8,128)}, u32[]{:S(2)}) copy-start(f32[16,4096]{1,0:T(8,128)} %param.13) | copy-start | bytes 786436
  68.4 8.6 %copy-start.1 = (f32[16,4096]{1,0:T(8,128)S(1)}, f32[16,4096]{1,0:T(8,128)}, u32[]{:S(2)}) copy-start(f32[16,4096]{1,0:T(8,128)} %param.14) | copy-start | bytes 786436
  68.4 8.6 %copy-start.2 = (f32[16,4096]{1,0:T(8,128)S(1)}, f32[16,4096]{1,0:T(8,128)}, u32[]{:S(2)}) copy-start(f32[16,4096]{1,0:T(8,128)} %param.15) | copy-start | bytes 786436
  78.7 12.0 %all-to-all-start.5 = ((bf16[16,16,256]{2,0,1:T(8,128)(2,1)}), bf16[16,16,256]{2,0,1:T(8,128)(2,1)S(1)}, u32[]{:S(2)}, u32[]{:S(2)}) async-start(bf16[16,16,256]{2,0,1:T(8,128)(2,1)} %bitcast.27), calls=%async_computation.5 | async-start | bytes 262144 | tf_op jit(solution)/shard_map/all_to_all | solution.py:99
  112.4 18.4 %all-to-all-start.6 = ((bf16[8,256,256]{2,1,0:T(8,128)(2,1)}), bf16[8,256,256]{2,1,0:T(8,128)(2,1)S(1)}, u32[]{:S(2)}, u32[]{:S(2)}) async-start(bf16[8,256,256]{2,1,0:T(8,128)(2,1)} %broadcast_in_dim.7), calls=%async_computation.6 | async-start | bytes 2097152 | tf_op jit(solution)/shard_map/all_to_all | solution.py:47

commit v2 on v1

v2 whole, which is shorter than its diff:
```python
import jax
import jax.numpy as jnp
from jax import lax
from jax.experimental import pallas as pl
from jax.experimental.pallas import tpu as pltpu
from jax.sharding import Mesh
from jax.sharding import PartitionSpec as P


NUMEL = 67108864
GY = ("gy_0", "gy_1", "gy_2")
GX = ("gx_0", "gx_1")
GX_GY = ("gx_0", "gx_1", "gy_0", "gy_1", "gy_2")
bf16 = jnp.bfloat16
f32 = jnp.float32

beta_one = 0.9
beta_two = 0.95
learn_rate = 0.01
weight_decay = 0.1
adam_eps = 1e-08
bias_one = 1.0 - 0.9**20
bias_two = 1.0 - 0.95**20

ROWS, COLS = 32, 896
AROWS, ACOLS = 16, 256
STATE = 3 * ACOLS
WIDE = COLS + STATE
BACK = COLS + ACOLS

CHIP_STEPS = ((1, 0), (3, 0), (2, 0), (0, 1), (1, 1), (3, 1), (2, 1))
REPLICA_STEPS = ((0, 1), (0, 3), (0, 2), (1, 0), (1, 1), (1, 3), (1, 2))


def call(kernel, out, flops, mib=12, **kw):
    return pl.pallas_call(
        kernel,
        out_shape=out,
        cost_estimate=pl.CostEstimate(flops=flops, bytes_accessed=4096, transcendentals=0),
        compiler_params=pltpu.CompilerParams(vmem_limit_bytes=mib * 2**20),
        **kw,
    )


def shape(dims, dtype):
    return jax.ShapeDtypeStruct(dims, dtype)


def halves(x):
    high = x.astype(bf16)
    return high, (x - high.astype(f32)).astype(bf16)


def adam_update(gradient, master, moment, second, clip_factor):
    scaled = clip_factor * gradient
    moment_new = beta_one * moment + (1.0 - beta_one) * scaled
    second_new = beta_two * second + (1.0 - beta_two) * scaled * scaled
    update = moment_new / bias_one / (jnp.sqrt(second_new / bias_two) + adam_eps)
    master_new = master - learn_rate * (update + weight_decay * master)
    return (master_new, moment_new, second_new)


def clip_of(sums_ref):
    total = jnp.sum(jnp.sum(sums_ref[...], axis=0, keepdims=True), axis=1, keepdims=True)
    return 1.0 / jnp.sqrt(total / NUMEL + 1e-06)


def fold_lanes(x):
    total = x[:, :128]
    for at in range(128, x.shape[1], 128):
        total = total + x[:, at : at + 128]
    return jnp.sum(total, axis=0, keepdims=True)


def pack_kernel(grad, master, moment, second, own, swap, part):
    core = lax.axis_index("gy_2")
    total = jnp.zeros((8, COLS), f32)
    for chip in range(8):
        for out, which in ((own, core), (swap, 1 - core)):
            rows = grad[2 * chip + which]
            out[chip, :, :COLS] = rows
            wide = rows.astype(f32)
            total = total + jnp.sum((wide * wide).reshape(ROWS // 8, 8, COLS), axis=0)
            cols = pl.ds(pl.multiple_of((2 * chip + which) * ACOLS, ACOLS), ACOLS)
            for n, state in enumerate((master, moment, second)):
                high, low = halves(state[:, cols])
                at = COLS + n * ACOLS
                out[chip, :AROWS, at : at + ACOLS] = high
                out[chip, AROWS:, at : at + ACOLS] = low
    part[...] = fold_lanes(total)


def route_kernel(own, swapped, *outs):
    z, x, core = (lax.axis_index(axis) for axis in GY)
    for (dz, dx), out in zip(((0, 0),) + CHIP_STEPS, outs):
        chip = lax.rem(z + dz, 4) * 2 + lax.rem(x + dx, 2)
        out[core] = own[chip]
        out[1 - core] = swapped[chip]


def sum_kernel(arrived, part, summed, partial):
    total = arrived[0].astype(f32)
    for replica in range(1, 8):
        total = total + arrived[replica].astype(f32)
    summed[...] = total
    squared = jnp.sum((total * total).reshape(32, 8, ACOLS), axis=0)
    partial[...] = part[...] + fold_lanes(squared)


def expert_weight_kernel(where, sums, grad, master, moment, second, attn, out):
    clip = clip_of(sums)
    for core in range(2):
        cols = slice(core * COLS, (core + 1) * COLS)
        new, _, _ = adam_update(
            grad[0, core].astype(f32), master[:, cols], moment[:, cols], second[:, cols], clip
        )
        out[core, :, :COLS] = new.astype(bf16)
        high, low = halves(attn[core * AROWS : (core + 1) * AROWS, :])
        out[core, :AROWS, COLS:] = high
        out[core, AROWS:, COLS:] = low


def expert_state_kernel(where, sums, grad, master, moment, second, master_new, moment_new, second_new):
    clip = clip_of(sums)
    for core in range(2):
        cols = slice(core * COLS, (core + 1) * COLS)
        master_new[:, cols], moment_new[:, cols], second_new[:, cols] = adam_update(
            grad[0, core].astype(f32), master[:, cols], moment[:, cols], second[:, cols], clip
        )


def attn_weight_kernel(sums, attn, *refs):
    arrived, out = refs[:-1], refs[-1]
    z, x = (lax.axis_index(axis) for axis in GY[:2])
    clip = clip_of(sums)
    for (dz, dx), block in zip(((0, 0),) + CHIP_STEPS, arrived):
        chip = lax.rem(z + 4 - dz, 4) * 2 + lax.rem(x + dx, 2)
        for core in range(2):
            rows = pl.ds(pl.multiple_of((chip * 2 + core) * AROWS, AROWS), AROWS)
            high = block[core, :AROWS, COLS:].astype(f32)
            low = block[core, AROWS:, COLS:].astype(f32)
            state = high + low
            new, _, _ = adam_update(
                attn[rows, :],
                state[:, :ACOLS],
                state[:, ACOLS : 2 * ACOLS],
                state[:, 2 * ACOLS :],
                clip,
            )
            out[rows, :] = new.astype(bf16)


def join_kernel(*refs):
    pieces, out = refs[:-1], refs[-1]
    x, y = (lax.axis_index(axis) for axis in GX)
    for (dx, dy), piece in zip(((0, 0),) + REPLICA_STEPS, pieces):
        out[lax.rem(x + dx, 2) * 4 + lax.rem(y + 4 - dy, 4)] = piece[...]


def finish_kernel(sums, arrived, master, moment, second, weight, master_new, moment_new, second_new):
    clip = clip_of(sums)
    for group in range(16):
        weight[group] = arrived[group, :, :COLS]
        cols = slice(group * ACOLS, (group + 1) * ACOLS)
        gradient = arrived[group, :AROWS, COLS:].astype(f32) + arrived[group, AROWS:, COLS:].astype(f32)
        master_new[:, cols], moment_new[:, cols], second_new[:, cols] = adam_update(
            gradient, master[:, cols], moment[:, cols], second[:, cols], clip
        )


def chip_pairs(dz, dx):
    return [(z * 2 + x, (z + dz) % 4 * 2 + (x + dx) % 2) for z in range(4) for x in range(2)]


def replica_pairs(dx, dy):
    return [(x * 4 + y, (x + dx) % 2 * 4 + (y + dy) % 4) for x in range(2) for y in range(4)]


def local(
    expert_grad,
    attn_grad,
    expert_master,
    expert_moment,
    expert_second,
    attn_master,
    attn_moment,
    attn_second,
):
    arrived = lax.all_to_all(
        attn_grad.reshape(8, 256, ACOLS), GX, split_axis=0, concat_axis=0, tiled=True
    )

    own, swap, part = call(
        pack_kernel,
        (shape((8, ROWS, WIDE), bf16), shape((8, ROWS, WIDE), bf16), shape((1, 128), f32)),
        4000000,
    )(expert_grad.reshape(16, ROWS, COLS), attn_master, attn_moment, attn_second)
    swapped = lax.ppermute(swap, "gy_2", [(0, 1), (1, 0)])
    routed = call(route_kernel, (shape((2, ROWS, WIDE), bf16),) * 8, 1000000)(own, swapped)
    blocks = [routed[0]]
    for n, step in enumerate(CHIP_STEPS):
        blocks.append(lax.ppermute(routed[n + 1], GY[:2], chip_pairs(*step)))

    attn_sum, partial = call(
        sum_kernel, (shape((256, ACOLS), f32), shape((1, 128), f32)), 2000000
    )(arrived, part)
    sums = lax.all_to_all(
        jnp.broadcast_to(partial, (128, 1, 128)), GX_GY, split_axis=0, concat_axis=0, tiled=True
    ).reshape(128, 128)

    order = {step: n for n, step in enumerate(((0, 0),) + CHIP_STEPS)}
    grads = jnp.stack([blocks[order[(n // 2, n % 2)]][:, :, :COLS] for n in range(8)])
    where = jnp.stack([lax.axis_index("gy_0"), lax.axis_index("gy_1")]).astype(jnp.int32)

    def source(n, at):
        return (lax.rem(at[0] + 4 - n // 2, 4) * 2 + lax.rem(at[1] + n, 2), 0, 0, 0)

    rows = pl.BlockSpec((ROWS, 2 * COLS), lambda n, at: (0, n))
    inputs = [
        pl.BlockSpec((128, 128), lambda n, at: (0, 0)),
        pl.BlockSpec((1, 2, ROWS, COLS), source),
        rows,
        rows,
        rows,
    ]
    state = (expert_master, expert_moment, expert_second)
    weights = call(
        expert_weight_kernel,
        shape((16, ROWS, BACK), bf16),
        4000000,
        grid_spec=pltpu.PrefetchScalarGridSpec(
            num_scalar_prefetch=1,
            grid=(8,),
            in_specs=inputs + [pl.BlockSpec((2 * AROWS, ACOLS), lambda n, at: (n, 0))],
            out_specs=pl.BlockSpec((2, ROWS, BACK), lambda n, at: (n, 0, 0)),
        ),
    )(where, sums, grads, *state, attn_sum)
    returned = lax.all_to_all(weights, GY, split_axis=0, concat_axis=0, tiled=True)
    attn_block = call(attn_weight_kernel, shape((256, ACOLS), bf16), 2000000)(
        sums, attn_sum, *blocks
    )
    pieces = [attn_block]
    for step in REPLICA_STEPS:
        pieces.append(lax.ppermute(attn_block, GX, replica_pairs(*step)))
    e_master, e_moment, e_second = call(
        expert_state_kernel,
        (shape((ROWS, 16 * COLS), f32),) * 3,
        8000000,
        grid_spec=pltpu.PrefetchScalarGridSpec(
            num_scalar_prefetch=1, grid=(8,), in_specs=inputs, out_specs=[rows] * 3
        ),
    )(where, sums, grads, *state)
    attn_weight = call(join_kernel, shape((8, 256, ACOLS), bf16), 1000000)(*pieces)
    expert_weight, a_master, a_moment, a_second = call(
        finish_kernel,
        (shape((16, ROWS, COLS), bf16),) + (shape((AROWS, 16 * ACOLS), f32),) * 3,
        2000000,
    )(sums, returned, attn_master, attn_moment, attn_second)
    return (
        e_master,
        e_moment,
        e_second,
        a_master,
        a_moment,
        a_second,
        expert_weight.reshape(1, 16 * ROWS, COLS),
        attn_weight.reshape(2048, ACOLS),
    )


def solution(mesh):
    split = Mesh(mesh.devices.reshape(2, 4, 4, 2, 2), GX_GY)
    placed = (P(GX, None, GY),) * 2 + (P(GX_GY, None),) * 6

    return jax.shard_map(
        local,
        mesh=split,
        in_specs=placed,
        out_specs=(P(GX_GY, None),) * 6 + (P(GX, None, GY), P(None, GY)),
        check_vma=False,
    )
```

time: 133 us -> 107 us (0.80); the launches traced: 133 us -> 105 us
  waiting for transfers between devices: 53.2 us -> 11.1 us
  blocking collectives: 39.4 us -> 0 us
  starting transfers between devices: 22.3 us -> 50.9 us
  local copies, waits for them, and re-layouts: 3.86 us -> 26 us
  Pallas kernels: 0 us -> 16.3 us
  other arithmetic: 11.9 us -> 0.07 us
  between operations: 2.12 us -> 0.79 us
    all_to_all x5 -> x3, waiting for transfers between devices: 53.2 us -> 1.94 us  [the longest x1 1.93 us: local(): lax.all_to_all(attn_grad.reshape(8, 256, ACOLS), GX, split_axis=0, concat...]
    all_to_all x2 -> x0, blocking collectives: 39.4 us -> none  [the longest x1 20.8 us: local(): lax.all_to_all(e_master.astype(jnp.bfloat16), GY, split_axis=1, concat_ax...]
    ppermute x0 -> x15, starting transfers between devices: none -> 28.3 us  [the longest x7 17.2 us: local(): blocks.append(lax.ppermute(routed[n + 1], GY[:2], chip_pairs(*step)))]
    unnamed x8 -> x57, local copies, waits for them, and re-layouts: 1.91 us -> 24.7 us
    pallas_call x0 -> x8, Pallas kernels: none -> 16.3 us  [the longest x1 5.5 us: local(): call(expert_state_kernel, (shape((ROWS, 16 * COLS), f32),) * 3, 8000000,...]
    ppermute x0 -> x15, waiting for transfers between devices: none -> 9.19 us  [the longest x7 9.17 us: local(): pieces.append(lax.ppermute(attn_block, GX, replica_pairs(*step)))]
    convert_element_type x2 -> x0, other arithmetic: 6.93 us -> none  [the longest x1 5.93 us: local(): e_master.astype(jnp.bfloat16)]
    reduce_sum x4 -> x0, other arithmetic: 4.75 us -> none  [the longest x2 3.88 us: squares(): return jnp.sum(wide * wide) + jnp.sum(attn_part * attn_part)]
  transfers between devices with their start and end apart: 5 -> 18, of which waited for: 5 -> 2; matrix products, arithmetic and copies ran while one was open for 6% -> 10% of each run, Pallas kernels for 0% -> 9%
where the time goes in v2:
time: 107 us; the launch traced here: 105 us
  starting transfers between devices  50.9 us (48%)
  local copies, waits for them, and re-layouts  26 us (24%)
  Pallas kernels  16.3 us (15%)
  waiting for transfers between devices  11.1 us (10%)
    unnamed x57, local copies, waits for them, and re-layouts  24.7 us
    ppermute x7, starting transfers between devices, local(): blocks.append(lax.ppermute(routed[n + 1], GY[:2], chip_pairs(*step)))  17.2 us
    all_to_all x1, starting transfers between devices, local(): lax.all_to_all(jnp.broadcast_to(partial, (128, 1, 128)), GX_GY, split_axi...  10 us
    ppermute x7, starting transfers between devices, local(): pieces.append(lax.ppermute(attn_block, GX, replica_pairs(*step)))  9.76 us
    ppermute x7, waiting for transfers between devices, local(): pieces.append(lax.ppermute(attn_block, GX, replica_pairs(*step)))  9.17 us
    all_to_all x1, starting transfers between devices, local(): lax.all_to_all(weights, GY, split_axis=0, concat_axis=0, tiled=True)  7.28 us
    pallas_call x1, Pallas kernels, local(): call(expert_state_kernel, (shape((ROWS, 16 * COLS), f32),) * 3, 8000000,...  5.5 us
    all_to_all x1, starting transfers between devices, local(): lax.all_to_all(attn_grad.reshape(8, 256, ACOLS), GX, split_axis=0, concat...  5.23 us
  transfers between devices with their start and end apart: 18, of which 2 were waited for; matrix products, arithmetic and copies ran while one was open for 10% of the time, Pallas kernels for 9%

profile of v2, /device:TPU:1, one launch (start us, length us, event | category | flops | bytes accessed | tf_op | source)
XLA Modules:
  0.0 105.2 jit_solution(10370950561193514713)
XLA Ops:
  0.6 0.0 copy-start.8
  0.6 0.9 copy-done.8
  1.6 0.9 copy-done.10
  2.5 0.9 copy-done.12
  3.5 1.2 %copy-done.14 = bf16[1,512,896]{2,1,0:T(8,128)(2,1)S(1)} copy-done((bf16[1,512,896]{2,1,0:T(8,128)(2,1)S(1)}, bf16[1,512,896]{2,1,0:T(8,128)(2,1)}, u32[]{:S(2)}) %copy-start.14) | copy-done | bytes 917528
  4.7 1.1 %shard_map.143 = (bf16[8,32,1664]{2,1,0:T(8,128)(2,1)S(1)}, bf16[8,32,1664]{2,1,0:T(8,128)(2,1)}, f32[1,128]{1,0:T(1,128)S(1)}) custom-call(bf16[16,32,896]{2,1,0:T(8,128)(2,1)S(1)} %bitcast.42, f32[16,4096]{1,0:T(8,128)S(1)} %copy-done.8, f32[16,4096]{1,0:T(8,128)S(1)} %copy-done.10, f32[16,4096]{1,0:T(8,128)S(1)} %copy-done.12), custom_call_target="tpu_custom_call" | custom-call | flops 4000000 | bytes 4096 | tf_op jit(solution)/shard_map/pallas_call | solution.py:193
  5.8 0.9 copy-done.15
  6.7 1.4 %collective-permute-start = (bf16[8,32,1664]{2,1,0:T(8,128)(2,1)}, bf16[8,32,1664]{2,1,0:T(8,128)(2,1)S(1)}, u32[]{:S(2)}, u32[]{:S(2)}) collective-permute-start(bf16[8,32,1664]{2,1,0:T(8,128)(2,1)} %get-tuple-element.31), channel_id=1, source_target_pairs={{0,1},{1,0},{2,3},{3,2},{4,5},{5,4},{6,7},{7,6},{8,9},{9,8},{10,11... | collective-permute-start | bytes 2555912 | tf_op jit(solution)/shard_map/ppermute | solution.py:198
  8.1 5.2 %all-to-all-start = ((bf16[8,256,256]{2,1,0:T(8,128)(2,1)}), bf16[8,256,256]{2,1,0:T(8,128)(2,1)S(1)}, u32[]{:S(2)}, u32[]{:S(2)}) async-start(bf16[8,256,256]{2,1,0:T(8,128)(2,1)} %bitcast.44), calls=%async_computation | async-start | bytes 2097152 | tf_op jit(solution)/shard_map/all_to_all | solution.py:189
  13.3 0.1 pad_add_fusion.where
  13.4 0.0 collective-permute-done.swapped
  13.4 1.1 %shard_map.145 = (bf16[2,32,1664]{2,1,0:T(8,128)(2,1)S(1)}, bf16[2,32,1664]{2,1,0:T(8,128)(2,1)}, bf16[2,32,1664]{2,1,0:T(8,128)(2,1)S(1)}, bf16[2,32,1664]{2,1,...) custom-call(bf16[8,32,1664]{2,1,0:T(8,128)(2,1)S(1)} %copy-done.16, ...), custom_call_target="tpu_custom_call" | custom-call | flops 1000000 | bytes 4096 | tf_op jit(solution)/shard_map/pallas_call | solution.py:199
  14.5 2.5 %collective-permute-start.1 = (bf16[2,32,1664]{2,1,0:T(8,128)(2,1)}, bf16[2,32,1664]{2,1,0:T(8,128)(2,1)}, u32[]{:S(2)}, u32[]{:S(2)}) collective-permute-start(bf16[2,32,1664]{2,1,0:T(8,128)(2,1)} %get-tuple-element.33), channel_id=1, source_target_pairs={{0,2},{2,0},{4,6},{6,4},{8,10},{10,8},{12,14},{14,12},{1,3},{3,1},... | collective-permute-start | bytes 638984 | tf_op jit(solution)/shard_map/ppermute | solution.py:202
  17.0 1.6 %collective-permute-start.2 = (bf16[2,32,1664]{2,1,0:T(8,128)(2,1)}, bf16[2,32,1664]{2,1,0:T(8,128)(2,1)}, u32[]{:S(2)}, u32[]{:S(2)}) collective-permute-start(bf16[2,32,1664]{2,1,0:T(8,128)(2,1)} %get-tuple-element.34), channel_id=1, source_target_pairs={{0,4},{2,6},{4,8},{6,10},{8,12},{10,14},{12,0},{14,2},{1,5},{3,7},... | collective-permute-start | bytes 638984 | tf_op jit(solution)/shard_map/ppermute | solution.py:202
  18.7 1.9 %collective-permute-start.3 = (bf16[2,32,1664]{2,1,0:T(8,128)(2,1)}, bf16[2,32,1664]{2,1,0:T(8,128)(2,1)}, u32[]{:S(2)}, u32[]{:S(2)}) collective-permute-start(bf16[2,32,1664]{2,1,0:T(8,128)(2,1)} %get-tuple-element.35), channel_id=1, source_target_pairs={{0,6},{2,4},{4,10},{6,8},{8,14},{10,12},{12,2},{14,0},{1,7},{3,5},... | collective-permute-start | bytes 638984 | tf_op jit(solution)/shard_map/ppermute | solution.py:202
  20.5 1.7 %collective-permute-start.4 = (bf16[2,32,1664]{2,1,0:T(8,128)(2,1)}, bf16[2,32,1664]{2,1,0:T(8,128)(2,1)}, u32[]{:S(2)}, u32[]{:S(2)}) collective-permute-start(bf16[2,32,1664]{2,1,0:T(8,128)(2,1)} %get-tuple-element.36), channel_id=1, source_target_pairs={{0,8},{2,10},{4,12},{6,14},{8,0},{10,2},{12,4},{14,6},{1,9},{3,11}... | collective-permute-start | bytes 638984 | tf_op jit(solution)/shard_map/ppermute | solution.py:202
  22.2 3.5 %collective-permute-start.5 = (bf16[2,32,1664]{2,1,0:T(8,128)(2,1)}, bf16[2,32,1664]{2,1,0:T(8,128)(2,1)}, u32[]{:S(2)}, u32[]{:S(2)}) collective-permute-start(bf16[2,32,1664]{2,1,0:T(8,128)(2,1)} %get-tuple-element.37), channel_id=1, source_target_pairs={{0,10},{2,8},{4,14},{6,12},{8,2},{10,0},{12,6},{14,4},{1,11},{3,9}... | collective-permute-start | bytes 638984 | tf_op jit(solution)/shard_map/ppermute | solution.py:202
  25.7 0.7 bitcast_dynamic-update-slice_fusion
  26.3 1.9 %all-to-all-done.arrived = bf16[8,256,256]{2,1,0:T(8,128)(2,1)S(1)} async-done(((bf16[8,256,256]{2,1,0:T(8,128)(2,1)}), bf16[8,256,256]{2,1,0:T(8,128)(2,1)S(1)}, u32[]{:S(2)}, u32[]{:S(2)}) %all-to-all-start) | async-done | bytes 1048608 | tf_op jit(solution)/shard_map/all_to_all | solution.py:189
  28.3 0.2 shard_map.144
  28.4 0.7 broadcast_in_dim.3
  29.1 10.0 %all-to-all-start.1 = ((f32[128,1,128]{2,1,0:T(1,128)}), f32[128,1,128]{2,1,0:T(1,128)S(1)}, u32[]{:S(2)}, u32[]{:S(2)}) async-start(f32[128,1,128]{2,1,0:T(1,128)} %broadcast_in_dim.3), calls=%async_computation.1 | async-start | bytes 131072 | tf_op jit(solution)/shard_map/all_to_all | solution.py:207
  39.1 0.0 collective-permute-done.1.refs_4_
  39.1 3.3 %collective-permute-start.6 = (bf16[2,32,1664]{2,1,0:T(8,128)(2,1)}, bf16[2,32,1664]{2,1,0:T(8,128)(2,1)S(1)}, u32[]{:S(2)}, u32[]{:S(2)}) collective-permute-start(bf16[2,32,1664]{2,1,0:T(8,128)(2,1)} %copy-done.24), channel_id=1, source_target_pairs={{0,12},{2,14},{4,0},{6,2},{8,4},{10,6},{12,8},{14,10},{1,13},{3,15... | collective-permute-start | bytes 638984 | tf_op jit(solution)/shard_map/ppermute | solution.py:202
  42.4 1.6 %fusion.6 = bf16[8,2,32,896]{3,2,1,0:T(8,128)(2,1)} fusion(bf16[8,2,32,896]{3,2,1,0:T(8,128)(2,1)} %bitcast_dynamic-update-slice_fusion, bf16[2,32,1664]{2,1,0:T(8,128)(2,1)} %collective-permute-done.1.refs_4_), kind=kLoop, calls=%fused_computation.13 | loop fusion | bytes 229376
  44.0 0.0 collective-permute-done.2.refs_1_
  44.0 2.7 %collective-permute-start.7 = (bf16[2,32,1664]{2,1,0:T(8,128)(2,1)}, bf16[2,32,1664]{2,1,0:T(8,128)(2,1)S(1)}, u32[]{:S(2)}, u32[]{:S(2)}) collective-permute-start(bf16[2,32,1664]{2,1,0:T(8,128)(2,1)} %copy-done.23), channel_id=1, source_target_pairs={{0,14},{2,12},{4,2},{6,0},{8,6},{10,4},{12,10},{14,8},{1,15},{3,13... | collective-permute-start | bytes 638984 | tf_op jit(solution)/shard_map/ppermute | solution.py:202
  46.7 1.6 %fusion.5 = bf16[8,2,32,896]{3,2,1,0:T(8,128)(2,1)} fusion(bf16[8,2,32,896]{3,2,1,0:T(8,128)(2,1)} %fusion.6, bf16[2,32,1664]{2,1,0:T(8,128)(2,1)} %collective-permute-done.2.refs_1_), kind=kLoop, calls=%fused_computation.11 | loop fusion | bytes 229376
  48.3 1.6 %fusion.4 = bf16[8,2,32,896]{3,2,1,0:T(8,128)(2,1)} fusion(bf16[8,2,32,896]{3,2,1,0:T(8,128)(2,1)} %fusion.5, bf16[2,32,1664]{2,1,0:T(8,128)(2,1)} %collective-permute-done.3.refs_5_), kind=kLoop, calls=%fused_computation.9 | loop fusion | bytes 229376
  49.8 1.6 %fusion.3 = bf16[8,2,32,896]{3,2,1,0:T(8,128)(2,1)} fusion(bf16[8,2,32,896]{3,2,1,0:T(8,128)(2,1)} %fusion.4, bf16[2,32,1664]{2,1,0:T(8,128)(2,1)} %collective-permute-done.4.refs_3_), kind=kLoop, calls=%fused_computation.7 | loop fusion | bytes 229376
  51.4 1.6 %fusion.2 = bf16[8,2,32,896]{3,2,1,0:T(8,128)(2,1)} fusion(bf16[8,2,32,896]{3,2,1,0:T(8,128)(2,1)} %fusion.3, bf16[2,32,1664]{2,1,0:T(8,128)(2,1)} %collective-permute-done.5.refs_7_), kind=kLoop, calls=%fused_computation.5 | loop fusion | bytes 229376
  53.0 0.7 fusion.1
  53.7 0.0 collective-permute-done.7.refs_6_
  53.7 0.0 copy-done.17
  53.7 0.7 fusion.grad
  54.3 0.7 copy-done.19
  55.0 0.0 all-to-all-done.1
  55.0 0.0 copy-start.1
  55.0 1.5 %copy-done.1 = f32[32,14336]{1,0:T(8,128)S(1)} copy-done((f32[32,14336]{1,0:T(8,128)S(1)}, f32[32,14336]{1,0:T(8,128)}, u32[]{:S(2)}) %copy-start.1) | copy-done | bytes 1835032
  56.5 1.5 %copy-done.3 = f32[32,14336]{1,0:T(8,128)S(1)} copy-done((f32[32,14336]{1,0:T(8,128)S(1)}, f32[32,14336]{1,0:T(8,128)}, u32[]{:S(2)}) %copy-start.3) | copy-done | bytes 1835032
  58.0 1.2 %copy-done.6 = bf16[8,2,32,896]{3,2,1,0:T(8,128)(2,1)S(1)} copy-done((bf16[8,2,32,896]{3,2,1,0:T(8,128)(2,1)S(1)}, bf16[8,2,32,896]{3,2,1,0:T(8,128)(2,1)}, u32[]{:S(2)}) %copy-start.6) | copy-done | bytes 917528
  59.2 4.0 %shard_map.147 = bf16[16,32,1152]{2,1,0:T(8,128)(2,1)S(1)} custom-call(s32[2]{0:T(128)S(1)} %pad_add_fusion.where, f32[128,128]{1,0:T(8,128)S(1)} %bitcast.38, bf16[8,2,32,896]{3,2,1,0:T(8,128)(2,1)S(1)} %copy-done.6, f32[32,14336]{1,0:T(8,128)S(1)} %copy-done, f32[32,14336]{1,0:T(8,128)S(1)} %copy-done.1, f32[32,14336]{1,0:T(8,128)S(1)} %copy-done.3, ...), custom_call_target="tpu_custom_call" | custom-call | flops 4000000 | bytes 4096 | tf_op jit(solution)/shard_map/pallas_call | solution.py:227
  63.2 1.1 %copy-done.5 = bf16[16,32,1152]{2,1,0:T(8,128)(2,1)} copy-done((bf16[16,32,1152]{2,1,0:T(8,128)(2,1)}, bf16[16,32,1152]{2,1,0:T(8,128)(2,1)S(1)}, u32[]{:S(2)}) %copy-start.5) | copy-done | bytes 1179672
  64.3 7.3 %all-to-all-start.2 = ((bf16[16,32,1152]{2,1,0:T(8,128)(2,1)}), bf16[16,32,1152]{2,1,0:T(8,128)(2,1)S(1)}, u32[]{:S(2)}, u32[]{:S(2)}) async-start(bf16[16,32,1152]{2,1,0:T(8,128)(2,1)} %copy-done.5), calls=%async_computation.2 | async-start | bytes 2359296 | tf_op jit(solution)/shard_map/all_to_all | solution.py:238
  71.6 0.9 copy-done.18
  72.5 0.9 copy-done.20
  73.4 1.8 %shard_map.149.refs_0_ = bf16[256,256]{1,0:T(8,128)(2,1)S(1)} custom-call(f32[128,128]{1,0:T(8,128)S(1)} %bitcast.39, f32[256,256]{1,0:T(8,128)S(1)} %get-tuple-element.43.attn, bf16[2,32,1664]{2,1,0:T(8,128)(2,1)S(1)} %get-tuple-element.32.refs_0_, bf16[2,32,1664]{2,1,0:T(8,128)(2,1)} %collective-permute-done.2.refs_1_, ...), custom_call_target="tpu_custom_call" | custom-call | flops 2000000 | bytes 4096 | tf_op jit(solution)/shard_map/pallas_call | solution.py:239
  75.2 2.8 %collective-permute-start.14 = (bf16[256,256]{1,0:T(8,128)(2,1)S(1)}, bf16[256,256]{1,0:T(8,128)(2,1)S(1)}, u32[]{:S(2)}, u32[]{:S(2)}) collective-permute-start(bf16[256,256]{1,0:T(8,128)(2,1)S(1)} %shard_map.149.refs_0_), channel_id=1, source_target_pairs={{0,96},{16,112},{32,64},{48,80},{64,32},{80,48},{96,0},{112,16},{1... | collective-permute-start | bytes 393224 | tf_op jit(solution)/shard_map/ppermute | solution.py:244
  78.0 1.7 %collective-permute-start.13 = (bf16[256,256]{1,0:T(8,128)(2,1)S(1)}, bf16[256,256]{1,0:T(8,128)(2,1)S(1)}, u32[]{:S(2)}, u32[]{:S(2)}) collective-permute-start(bf16[256,256]{1,0:T(8,128)(2,1)S(1)} %shard_map.149.refs_0_), channel_id=1, source_target_pairs={{0,112},{16,64},{32,80},{48,96},{64,48},{80,0},{96,16},{112,32},{1... | collective-permute-start | bytes 393224 | tf_op jit(solution)/shard_map/ppermute | solution.py:244
  79.7 0.6 collective-permute-start.12
  80.4 1.2 %collective-permute-start.11 = (bf16[256,256]{1,0:T(8,128)(2,1)S(1)}, bf16[256,256]{1,0:T(8,128)(2,1)S(1)}, u32[]{:S(2)}, u32[]{:S(2)}) collective-permute-start(bf16[256,256]{1,0:T(8,128)(2,1)S(1)} %shard_map.149.refs_0_), channel_id=1, source_target_pairs={{0,64},{16,80},{32,96},{48,112},{64,0},{80,16},{96,32},{112,48},{1... | collective-permute-start | bytes 393224 | tf_op jit(solution)/shard_map/ppermute | solution.py:244
  81.5 0.3 collective-permute-start.10
  81.8 9.2 %collective-permute-done.14.refs_7_ = bf16[256,256]{1,0:T(8,128)(2,1)S(1)} collective-permute-done((bf16[256,256]{1,0:T(8,128)(2,1)S(1)}, bf16[256,256]{1,0:T(8,128)(2,1)S(1)}, u32[]{:S(2)}, u32[]{:S(2)}) %collective-permute-start.14) | collective-permute-done | bytes 131104 | tf_op jit(solution)/shard_map/ppermute | solution.py:244
  91.0 1.3 %collective-permute-start.9 = (bf16[256,256]{1,0:T(8,128)(2,1)S(1)}, bf16[256,256]{1,0:T(8,128)(2,1)S(1)}, u32[]{:S(2)}, u32[]{:S(2)}) collective-permute-start(bf16[256,256]{1,0:T(8,128)(2,1)S(1)} %shard_map.149.refs_0_), channel_id=1, source_target_pairs={{0,48},{16,0},{32,16},{48,32},{64,112},{80,64},{96,80},{112,96},{1... | collective-permute-start | bytes 393224 | tf_op jit(solution)/shard_map/ppermute | solution.py:244
  92.3 0.0 collective-permute-done.13.refs_6_
  92.3 1.9 %collective-permute-start.8 = (bf16[256,256]{1,0:T(8,128)(2,1)S(1)}, bf16[256,256]{1,0:T(8,128)(2,1)S(1)}, u32[]{:S(2)}, u32[]{:S(2)}) collective-permute-start(bf16[256,256]{1,0:T(8,128)(2,1)S(1)} %shard_map.149.refs_0_), channel_id=1, source_target_pairs={{0,16},{16,32},{32,48},{48,0},{64,80},{80,96},{96,112},{112,64},{1... | collective-permute-start | bytes 393224 | tf_op jit(solution)/shard_map/ppermute | solution.py:244
  94.2 1.5 %copy-done.4 = f32[32,14336]{1,0:T(8,128)S(1)} copy-done((f32[32,14336]{1,0:T(8,128)S(1)}, f32[32,14336]{1,0:T(8,128)}, u32[]{:S(2)}) %copy-start.4) | copy-done | bytes 1835032
  95.7 1.2 %copy-done.7 = bf16[8,2,32,896]{3,2,1,0:T(8,128)(2,1)S(1)} copy-done((bf16[8,2,32,896]{3,2,1,0:T(8,128)(2,1)S(1)}, bf16[8,2,32,896]{3,2,1,0:T(8,128)(2,1)}, u32[]{:S(2)}) %copy-start.7) | copy-done | bytes 917528
  96.8 5.5 %shard_map.146 = (f32[32,14336]{1,0:T(8,128)}, f32[32,14336]{1,0:T(8,128)}, f32[32,14336]{1,0:T(8,128)}) custom-call(s32[2]{0:T(128)S(1)} %copy-done.22, f32[128,128]{1,0:T(8,128)S(1)} %bitcast.40, bf16[8,2,32,896]{3,2,1,0:T(8,128)(2,1)S(1)} %copy-done.7, f32[32,14336]{1,0:T(8,128)S(1)} %copy-done, f32[32,14336]{1,0:T(8,128)S(1)} %copy-done.2, ...), custom_call_target="tpu_custom_call" | custom-call | flops 8000000 | bytes 4096 | tf_op jit(solution)/shard_map/pallas_call | solution.py:245
  102.4 0.0 collective-permute-done.12.refs_5_
  102.4 0.0 collective-permute-done.9.refs_2_
  102.4 1.1 %shard_map.150 = bf16[8,256,256]{2,1,0:T(8,128)(2,1)} custom-call(bf16[256,256]{1,0:T(8,128)(2,1)S(1)} %shard_map.149.refs_0_, bf16[256,256]{1,0:T(8,128)(2,1)S(1)} %collective-permute-done.8.refs_1_, bf16[256,256]{1,0:T(8,128)(2,1)S(1)} %collective-permute-done.9.refs_2_, bf16[256,256]{1,0:T(8,128)(2,1)S(1)} %collective-permute-done.10.refs_3_, ...), custom_call_target="tpu_custom_call" | custom-call | flops 1000000 | bytes 4096 | tf_op jit(solution)/shard_map/pallas_call | solution.py:253
  103.5 0.1 copy-done.13
  103.6 1.6 %shard_map.148 = (bf16[16,32,896]{2,1,0:T(8,128)(2,1)}, f32[16,4096]{1,0:T(8,128)}, f32[16,4096]{1,0:T(8,128)}, f32[16,4096]{1,0:T(8,128)}) custom-call(f32[128,128]{1,0:T(8,128)S(1)} %bitcast.41, bf16[16,32,1152]{2,1,0:T(8,128)(2,1)S(1)} %all-to-all-done.2.arrived, f32[16,4096]{1,0:T(8,128)S(1)} %copy-done.9, f32[16,4096]{1,0:T(8,128)S(1)} %copy-done.11, ...), custom_call_target="tpu_custom_call" | custom-call | flops 2000000 | bytes 4096 | tf_op jit(solution)/shard_map/pallas_call | solution.py:254
  (40 shorter events, 0.1 us)
Async XLA Ops:
  0.6 1.0 copy-start.8
  1.6 0.9 copy-start.10
  2.5 0.9 copy-start.12
  3.5 1.2 %copy-start.14 = (bf16[1,512,896]{2,1,0:T(8,128)(2,1)S(1)}, bf16[1,512,896]{2,1,0:T(8,128)(2,1)}, u32[]{:S(2)}) copy-start(bf16[1,512,896]{2,1,0:T(8,128)(2,1)} %param.8) | copy-start | bytes 2752516
  5.8 0.9 copy-start.15
  6.7 6.7 %copy-start.16 = (bf16[8,32,1664]{2,1,0:T(8,128)(2,1)S(1)}, bf16[8,32,1664]{2,1,0:T(8,128)(2,1)}, u32[]{:S(2)}) copy-start(bf16[8,32,1664]{2,1,0:T(8,128)(2,1)} %copy-done.15) | copy-start | bytes 2555908
  6.7 6.7 %collective-permute-start = (bf16[8,32,1664]{2,1,0:T(8,128)(2,1)}, bf16[8,32,1664]{2,1,0:T(8,128)(2,1)S(1)}, u32[]{:S(2)}, u32[]{:S(2)}) collective-permute-start(bf16[8,32,1664]{2,1,0:T(8,128)(2,1)} %get-tuple-element.31), channel_id=1, source_target_pairs={{0,1},{1,0},{2,3},{3,2},{4,5},{5,4},{6,7},{7,6},{8,9},{9,8},{10,11... | collective-permute-start | bytes 2555912 | tf_op jit(solution)/shard_map/ppermute | solution.py:198
  8.1 20.2 %all-to-all-start = ((bf16[8,256,256]{2,1,0:T(8,128)(2,1)}), bf16[8,256,256]{2,1,0:T(8,128)(2,1)S(1)}, u32[]{:S(2)}, u32[]{:S(2)}) async-start(bf16[8,256,256]{2,1,0:T(8,128)(2,1)} %bitcast.44), calls=%async_computation | async-start | bytes 2097152 | tf_op jit(solution)/shard_map/all_to_all | solution.py:189
  13.4 41.6 %copy-start.21 = (s32[2]{0:T(128)}, s32[2]{0:T(128)S(1)}, u32[]{:S(2)}) copy-start(s32[2]{0:T(128)S(1)} %pad_add_fusion.where) | copy-start | bytes 28
  14.5 11.2 %copy-start.23 = (bf16[2,32,1664]{2,1,0:T(8,128)(2,1)}, bf16[2,32,1664]{2,1,0:T(8,128)(2,1)S(1)}, u32[]{:S(2)}) copy-start(bf16[2,32,1664]{2,1,0:T(8,128)(2,1)S(1)} %get-tuple-element.39) | copy-start | bytes 638980
  14.5 11.2 %copy-start.24 = (bf16[2,32,1664]{2,1,0:T(8,128)(2,1)}, bf16[2,32,1664]{2,1,0:T(8,128)(2,1)S(1)}, u32[]{:S(2)}) copy-start(bf16[2,32,1664]{2,1,0:T(8,128)(2,1)S(1)} %get-tuple-element.38) | copy-start | bytes 638980
  14.5 40.5 %copy-start = (f32[32,14336]{1,0:T(8,128)S(1)}, f32[32,14336]{1,0:T(8,128)}, u32[]{:S(2)}) copy-start(f32[32,14336]{1,0:T(8,128)} %master.6) | copy-start | bytes 5505028
  14.5 24.6 %collective-permute-start.1 = (bf16[2,32,1664]{2,1,0:T(8,128)(2,1)}, bf16[2,32,1664]{2,1,0:T(8,128)(2,1)}, u32[]{:S(2)}, u32[]{:S(2)}) collective-permute-start(bf16[2,32,1664]{2,1,0:T(8,128)(2,1)} %get-tuple-element.33), channel_id=1, source_target_pairs={{0,2},{2,0},{4,6},{6,4},{8,10},{10,8},{12,14},{14,12},{1,3},{3,1},... | collective-permute-start | bytes 638984 | tf_op jit(solution)/shard_map/ppermute | solution.py:202
  17.0 27.0 %collective-permute-start.2 = (bf16[2,32,1664]{2,1,0:T(8,128)(2,1)}, bf16[2,32,1664]{2,1,0:T(8,128)(2,1)}, u32[]{:S(2)}, u32[]{:S(2)}) collective-permute-start(bf16[2,32,1664]{2,1,0:T(8,128)(2,1)} %get-tuple-element.34), channel_id=1, source_target_pairs={{0,4},{2,6},{4,8},{6,10},{8,12},{10,14},{12,0},{14,2},{1,5},{3,7},... | collective-permute-start | bytes 638984 | tf_op jit(solution)/shard_map/ppermute | solution.py:202
  18.7 29.6 %collective-permute-start.3 = (bf16[2,32,1664]{2,1,0:T(8,128)(2,1)}, bf16[2,32,1664]{2,1,0:T(8,128)(2,1)}, u32[]{:S(2)}, u32[]{:S(2)}) collective-permute-start(bf16[2,32,1664]{2,1,0:T(8,128)(2,1)} %get-tuple-element.35), channel_id=1, source_target_pairs={{0,6},{2,4},{4,10},{6,8},{8,14},{10,12},{12,2},{14,0},{1,7},{3,5},... | collective-permute-start | bytes 638984 | tf_op jit(solution)/shard_map/ppermute | solution.py:202
  20.5 29.3 %collective-permute-start.4 = (bf16[2,32,1664]{2,1,0:T(8,128)(2,1)}, bf16[2,32,1664]{2,1,0:T(8,128)(2,1)}, u32[]{:S(2)}, u32[]{:S(2)}) collective-permute-start(bf16[2,32,1664]{2,1,0:T(8,128)(2,1)} %get-tuple-element.36), channel_id=1, source_target_pairs={{0,8},{2,10},{4,12},{6,14},{8,0},{10,2},{12,4},{14,6},{1,9},{3,11}... | collective-permute-start | bytes 638984 | tf_op jit(solution)/shard_map/ppermute | solution.py:202
  22.2 29.2 %collective-permute-start.5 = (bf16[2,32,1664]{2,1,0:T(8,128)(2,1)}, bf16[2,32,1664]{2,1,0:T(8,128)(2,1)}, u32[]{:S(2)}, u32[]{:S(2)}) collective-permute-start(bf16[2,32,1664]{2,1,0:T(8,128)(2,1)} %get-tuple-element.37), channel_id=1, source_target_pairs={{0,10},{2,8},{4,14},{6,12},{8,2},{10,0},{12,6},{14,4},{1,11},{3,9}... | collective-permute-start | bytes 638984 | tf_op jit(solution)/shard_map/ppermute | solution.py:202
  29.1 25.9 %all-to-all-start.1 = ((f32[128,1,128]{2,1,0:T(1,128)}), f32[128,1,128]{2,1,0:T(1,128)S(1)}, u32[]{:S(2)}, u32[]{:S(2)}) async-start(f32[128,1,128]{2,1,0:T(1,128)} %broadcast_in_dim.3), calls=%async_computation.1 | async-start | bytes 131072 | tf_op jit(solution)/shard_map/all_to_all | solution.py:207
  39.1 13.8 %collective-permute-start.6 = (bf16[2,32,1664]{2,1,0:T(8,128)(2,1)}, bf16[2,32,1664]{2,1,0:T(8,128)(2,1)S(1)}, u32[]{:S(2)}, u32[]{:S(2)}) collective-permute-start(bf16[2,32,1664]{2,1,0:T(8,128)(2,1)} %copy-done.24), channel_id=1, source_target_pairs={{0,12},{2,14},{4,0},{6,2},{8,4},{10,6},{12,8},{14,10},{1,13},{3,15... | collective-permute-start | bytes 638984 | tf_op jit(solution)/shard_map/ppermute | solution.py:202
  44.0 9.7 %collective-permute-start.7 = (bf16[2,32,1664]{2,1,0:T(8,128)(2,1)}, bf16[2,32,1664]{2,1,0:T(8,128)(2,1)S(1)}, u32[]{:S(2)}, u32[]{:S(2)}) collective-permute-start(bf16[2,32,1664]{2,1,0:T(8,128)(2,1)} %copy-done.23), channel_id=1, source_target_pairs={{0,14},{2,12},{4,2},{6,0},{8,6},{10,4},{12,10},{14,8},{1,15},{3,13... | collective-permute-start | bytes 638984 | tf_op jit(solution)/shard_map/ppermute | solution.py:202
  52.9 0.7 copy-start.17
  54.3 0.7 copy-start.19
  55.0 1.5 %copy-start.1 = (f32[32,14336]{1,0:T(8,128)S(1)}, f32[32,14336]{1,0:T(8,128)}, u32[]{:S(2)}) copy-start(f32[32,14336]{1,0:T(8,128)} %moment.6) | copy-start | bytes 5505028
  56.5 1.5 %copy-start.3 = (f32[32,14336]{1,0:T(8,128)S(1)}, f32[32,14336]{1,0:T(8,128)}, u32[]{:S(2)}) copy-start(f32[32,14336]{1,0:T(8,128)} %second.6) | copy-start | bytes 5505028
  58.0 1.2 %copy-start.6 = (bf16[8,2,32,896]{3,2,1,0:T(8,128)(2,1)S(1)}, bf16[8,2,32,896]{3,2,1,0:T(8,128)(2,1)}, u32[]{:S(2)}) copy-start(bf16[8,2,32,896]{3,2,1,0:T(8,128)(2,1)} %fusion.grad) | copy-start | bytes 2752516
  63.2 1.1 %copy-start.5 = (bf16[16,32,1152]{2,1,0:T(8,128)(2,1)}, bf16[16,32,1152]{2,1,0:T(8,128)(2,1)S(1)}, u32[]{:S(2)}) copy-start(bf16[16,32,1152]{2,1,0:T(8,128)(2,1)S(1)} %shard_map.147) | copy-start | bytes 3538948
  64.3 39.2 %all-to-all-start.2 = ((bf16[16,32,1152]{2,1,0:T(8,128)(2,1)}), bf16[16,32,1152]{2,1,0:T(8,128)(2,1)S(1)}, u32[]{:S(2)}, u32[]{:S(2)}) async-start(bf16[16,32,1152]{2,1,0:T(8,128)(2,1)} %copy-done.5), calls=%async_computation.2 | async-start | bytes 2359296 | tf_op jit(solution)/shard_map/all_to_all | solution.py:238
  71.6 0.9 copy-start.18
  72.5 0.9 copy-start.20
  73.4 20.7 %copy-start.2 = (f32[32,14336]{1,0:T(8,128)S(1)}, f32[32,14336]{1,0:T(8,128)}, u32[]{:S(2)}) copy-start(f32[32,14336]{1,0:T(8,128)} %moment.6) | copy-start | bytes 5505028
  73.4 20.7 %copy-start.22 = (s32[2]{0:T(128)S(1)}, s32[2]{0:T(128)}, u32[]{:S(2)}) copy-start(s32[2]{0:T(128)} %copy-done.21) | copy-start | bytes 28
  75.2 15.8 %collective-permute-start.14 = (bf16[256,256]{1,0:T(8,128)(2,1)S(1)}, bf16[256,256]{1,0:T(8,128)(2,1)S(1)}, u32[]{:S(2)}, u32[]{:S(2)}) collective-permute-start(bf16[256,256]{1,0:T(8,128)(2,1)S(1)} %shard_map.149.refs_0_), channel_id=1, source_target_pairs={{0,96},{16,112},{32,64},{48,80},{64,32},{80,48},{96,0},{112,16},{1... | collective-permute-start | bytes 393224 | tf_op jit(solution)/shard_map/ppermute | solution.py:244
  78.0 14.3 %collective-permute-start.13 = (bf16[256,256]{1,0:T(8,128)(2,1)S(1)}, bf16[256,256]{1,0:T(8,128)(2,1)S(1)}, u32[]{:S(2)}, u32[]{:S(2)}) collective-permute-start(bf16[256,256]{1,0:T(8,128)(2,1)S(1)} %shard_map.149.refs_0_), channel_id=1, source_target_pairs={{0,112},{16,64},{32,80},{48,96},{64,48},{80,0},{96,16},{112,32},{1... | collective-permute-start | bytes 393224 | tf_op jit(solution)/shard_map/ppermute | solution.py:244
  79.7 22.6 %collective-permute-start.12 = (bf16[256,256]{1,0:T(8,128)(2,1)S(1)}, bf16[256,256]{1,0:T(8,128)(2,1)S(1)}, u32[]{:S(2)}, u32[]{:S(2)}) collective-permute-start(bf16[256,256]{1,0:T(8,128)(2,1)S(1)} %shard_map.149.refs_0_), channel_id=1, source_target_pairs={{0,80},{16,96},{32,112},{48,64},{64,16},{80,32},{96,48},{112,0},{1... | collective-permute-start | bytes 393224 | tf_op jit(solution)/shard_map/ppermute | solution.py:244
  80.4 22.0 %collective-permute-start.11 = (bf16[256,256]{1,0:T(8,128)(2,1)S(1)}, bf16[256,256]{1,0:T(8,128)(2,1)S(1)}, u32[]{:S(2)}, u32[]{:S(2)}) collective-permute-start(bf16[256,256]{1,0:T(8,128)(2,1)S(1)} %shard_map.149.refs_0_), channel_id=1, source_target_pairs={{0,64},{16,80},{32,96},{48,112},{64,0},{80,16},{96,32},{112,48},{1... | collective-permute-start | bytes 393224 | tf_op jit(solution)/shard_map/ppermute | solution.py:244
  81.5 20.8 %collective-permute-start.10 = (bf16[256,256]{1,0:T(8,128)(2,1)S(1)}, bf16[256,256]{1,0:T(8,128)(2,1)S(1)}, u32[]{:S(2)}, u32[]{:S(2)}) collective-permute-start(bf16[256,256]{1,0:T(8,128)(2,1)S(1)} %shard_map.149.refs_0_), channel_id=1, source_target_pairs={{0,32},{16,48},{32,0},{48,16},{64,96},{80,112},{96,64},{112,80},{1... | collective-permute-start | bytes 393224 | tf_op jit(solution)/shard_map/ppermute | solution.py:244
  91.0 11.4 %collective-permute-start.9 = (bf16[256,256]{1,0:T(8,128)(2,1)S(1)}, bf16[256,256]{1,0:T(8,128)(2,1)S(1)}, u32[]{:S(2)}, u32[]{:S(2)}) collective-permute-start(bf16[256,256]{1,0:T(8,128)(2,1)S(1)} %shard_map.149.refs_0_), channel_id=1, source_target_pairs={{0,48},{16,0},{32,16},{48,32},{64,112},{80,64},{96,80},{112,96},{1... | collective-permute-start | bytes 393224 | tf_op jit(solution)/shard_map/ppermute | solution.py:244
  92.3 10.1 %collective-permute-start.8 = (bf16[256,256]{1,0:T(8,128)(2,1)S(1)}, bf16[256,256]{1,0:T(8,128)(2,1)S(1)}, u32[]{:S(2)}, u32[]{:S(2)}) collective-permute-start(bf16[256,256]{1,0:T(8,128)(2,1)S(1)} %shard_map.149.refs_0_), channel_id=1, source_target_pairs={{0,16},{16,32},{32,48},{48,0},{64,80},{80,96},{96,112},{112,64},{1... | collective-permute-start | bytes 393224 | tf_op jit(solution)/shard_map/ppermute | solution.py:244
  94.2 1.5 %copy-start.4 = (f32[32,14336]{1,0:T(8,128)S(1)}, f32[32,14336]{1,0:T(8,128)}, u32[]{:S(2)}) copy-start(f32[32,14336]{1,0:T(8,128)} %second.6) | copy-start | bytes 5505028
  95.7 1.2 %copy-start.7 = (bf16[8,2,32,896]{3,2,1,0:T(8,128)(2,1)S(1)}, bf16[8,2,32,896]{3,2,1,0:T(8,128)(2,1)}, u32[]{:S(2)}) copy-start(bf16[8,2,32,896]{3,2,1,0:T(8,128)(2,1)} %fusion.grad) | copy-start | bytes 2752516
  102.3 1.1 %copy-start.9 = (f32[16,4096]{1,0:T(8,128)S(1)}, f32[16,4096]{1,0:T(8,128)}, u32[]{:S(2)}) copy-start(f32[16,4096]{1,0:T(8,128)} %master.7) | copy-start | bytes 786436
  102.3 1.1 %copy-start.11 = (f32[16,4096]{1,0:T(8,128)S(1)}, f32[16,4096]{1,0:T(8,128)}, u32[]{:S(2)}) copy-start(f32[16,4096]{1,0:T(8,128)} %moment.7) | copy-start | bytes 786436
  102.3 1.3 %copy-start.13 = (f32[16,4096]{1,0:T(8,128)S(1)}, f32[16,4096]{1,0:T(8,128)}, u32[]{:S(2)}) copy-start(f32[16,4096]{1,0:T(8,128)} %second.7) | copy-start | bytes 786436

commit v3 on v2

--- a/solution.py
+++ b/solution.py
@@ -29,7 +29,7 @@
 BACK = COLS + ACOLS
 
 CHIP_STEPS = ((1, 0), (3, 0), (2, 0), (0, 1), (1, 1), (3, 1), (2, 1))
-REPLICA_STEPS = ((0, 1), (0, 3), (0, 2), (1, 0), (1, 1), (1, 3), (1, 2))
+REPLICA_STEPS = (1, 3, 2)
 
 
 def call(kernel, out, flops, mib=12, **kw):
@@ -55,7 +55,9 @@
     scaled = clip_factor * gradient
     moment_new = beta_one * moment + (1.0 - beta_one) * scaled
     second_new = beta_two * second + (1.0 - beta_two) * scaled * scaled
-    update = moment_new / bias_one / (jnp.sqrt(second_new / bias_two) + adam_eps)
+    mean_square = second_new * (1.0 / bias_two)
+    root = mean_square * lax.rsqrt(mean_square)
+    update = moment_new * (1.0 / bias_one) / (root + adam_eps)
     master_new = master - learn_rate * (update + weight_decay * master)
     return (master_new, moment_new, second_new)
 
@@ -98,48 +100,118 @@
         out[1 - core] = swapped[chip]
 
 
-def sum_kernel(arrived, part, summed, partial):
+def sum_kernel(arrived, part, summed, copies):
     total = arrived[0].astype(f32)
     for replica in range(1, 8):
         total = total + arrived[replica].astype(f32)
     summed[...] = total
     squared = jnp.sum((total * total).reshape(32, 8, ACOLS), axis=0)
-    partial[...] = part[...] + fold_lanes(squared)
-
-
-def expert_weight_kernel(where, sums, grad, master, moment, second, attn, out):
+    copies[...] = jnp.broadcast_to(part[...] + fold_lanes(squared), (128, 128))
+
+
+def sources():
+    z, x = (lax.axis_index(axis) for axis in GY[:2])
+    return [
+        lax.rem(z + 4 - dz, 4) * 2 + lax.rem(x + dx, 2) for dz, dx in ((0, 0),) + CHIP_STEPS
+    ]
+
+
+def wide_cols(chip):
+    return pl.ds(pl.multiple_of(chip * 2 * COLS, 2 * COLS), 2 * COLS)
+
+
+def lanes(at):
+    return slice(at * 128, (at + 1) * 128)
+
+
+def expert_loads(blocks, state, held, grads, sems):
+    loads = []
+    for n, (chip, block) in enumerate(zip(sources(), blocks)):
+        copies = [pltpu.make_async_copy(block.at[:, :, :COLS], grads.at[n], sems.at[n, 3])]
+        for m, array in enumerate(state):
+            copies.append(
+                pltpu.make_async_copy(array.at[:, wide_cols(chip)], held.at[m, n], sems.at[n, m])
+            )
+        for copy in copies:
+            copy.start()
+        loads.append(copies)
+    return loads
+
+
+def expert_weight_kernel(sums, attn, *refs):
+    blocks, state, out = refs[:8], refs[8:11], refs[11]
+    held, grads, weights, sems, out_sems = refs[12:]
+    loads = expert_loads(blocks, state, held, grads, sems)
     clip = clip_of(sums)
-    for core in range(2):
-        cols = slice(core * COLS, (core + 1) * COLS)
-        new, _, _ = adam_update(
-            grad[0, core].astype(f32), master[:, cols], moment[:, cols], second[:, cols], clip
-        )
-        out[core, :, :COLS] = new.astype(bf16)
-        high, low = halves(attn[core * AROWS : (core + 1) * AROWS, :])
-        out[core, :AROWS, COLS:] = high
-        out[core, AROWS:, COLS:] = low
-
-
-def expert_state_kernel(where, sums, grad, master, moment, second, master_new, moment_new, second_new):
-    clip = clip_of(sums)
-    for core in range(2):
-        cols = slice(core * COLS, (core + 1) * COLS)
-        master_new[:, cols], moment_new[:, cols], second_new[:, cols] = adam_update(
-            grad[0, core].astype(f32), master[:, cols], moment[:, cols], second[:, cols], clip
-        )
-
-
-def attn_weight_kernel(sums, attn, *refs):
-    arrived, out = refs[:-1], refs[-1]
-    z, x = (lax.axis_index(axis) for axis in GY[:2])
-    clip = clip_of(sums)
-    for (dz, dx), block in zip(((0, 0),) + CHIP_STEPS, arrived):
-        chip = lax.rem(z + 4 - dz, 4) * 2 + lax.rem(x + dx, 2)
+    stores = []
+    for n, chip in enumerate(sources()):
         for core in range(2):
             rows = pl.ds(pl.multiple_of((chip * 2 + core) * AROWS, AROWS), AROWS)
-            high = block[core, :AROWS, COLS:].astype(f32)
-            low = block[core, AROWS:, COLS:].astype(f32)
-            state = high + low
+            high, low = halves(attn[rows, :])
+            weights[n, core, :AROWS, COLS:] = high
+            weights[n, core, AROWS:, COLS:] = low
+        for copy in loads[n]:
+            copy.wait()
+        for at in range(14):
+            core, col = divmod(at, 7)
+            new, _, _ = adam_update(
+                grads[n, core, :, lanes(col)].astype(f32),
+                held[0, n, :, lanes(at)],
+                held[1, n, :, lanes(at)],
+                held[2, n, :, lanes(at)],
+                clip,
+            )
+            weights[n, core, :, lanes(col)] = new.astype(bf16)
+        store = pltpu.make_async_copy(weights.at[n], out.at[pl.ds(chip * 2, 2)], out_sems.at[n])
+        store.start()
+        stores.append(store)
+    for store in stores:
+        store.wait()
+
+
+def expert_state_kernel(sums, *refs):
+    blocks, state, outs = refs[:8], refs[8:11], refs[11:14]
+    held, grads, news, sems, out_sems = refs[14:]
+    loads = expert_loads(blocks, state, held, grads, sems)
+    clip = clip_of(sums)
+    stores = []
+    for n, chip in enumerate(sources()):
+        for copy in loads[n]:
+            copy.wait()
+        for at in range(14):
+            core, col = divmod(at, 7)
+            results = adam_update(
+                grads[n, core, :, lanes(col)].astype(f32),
+                held[0, n, :, lanes(at)],
+                held[1, n, :, lanes(at)],
+                held[2, n, :, lanes(at)],
+                clip,
+            )
+            for m, result in enumerate(results):
+                news[m, n, :, lanes(at)] = result
+        for m, out in enumerate(outs):
+            store = pltpu.make_async_copy(
+                news.at[m, n], out.at[:, wide_cols(chip)], out_sems.at[n, m]
+            )
+            store.start()
+            stores.append(store)
+    for store in stores:
+        store.wait()
+
+
+def attn_weight_kernel(sums, attn, *refs):
+    blocks, out, held, sems = refs[:8], refs[8], refs[9], refs[10]
+    loads = []
+    for n, block in enumerate(blocks):
+        copy = pltpu.make_async_copy(block.at[:, :, COLS:], held.at[n], sems.at[n])
+        copy.start()
+        loads.append(copy)
+    clip = clip_of(sums)
+    for n, chip in enumerate(sources()):
+        loads[n].wait()
+        for core in range(2):
+            rows = pl.ds(pl.multiple_of((chip * 2 + core) * AROWS, AROWS), AROWS)
+            state = held[n, core, :AROWS, :].astype(f32) + held[n, core, AROWS:, :].astype(f32)
             new, _, _ = adam_update(
                 attn[rows, :],
                 state[:, :ACOLS],
@@ -150,11 +222,18 @@
             out[rows, :] = new.astype(bf16)
 
 
+def both_kernel(own, other, out):
+    x = lax.axis_index("gx_0")
+    out[x] = own[...]
+    out[1 - x] = other[...]
+
+
 def join_kernel(*refs):
     pieces, out = refs[:-1], refs[-1]
-    x, y = (lax.axis_index(axis) for axis in GX)
-    for (dx, dy), piece in zip(((0, 0),) + REPLICA_STEPS, pieces):
-        out[lax.rem(x + dx, 2) * 4 + lax.rem(y + 4 - dy, 4)] = piece[...]
+    y = lax.axis_index("gx_1")
+    for dy, piece in zip((0,) + REPLICA_STEPS, pieces):
+        for x in range(2):
+            out[x * 4 + lax.rem(y + 4 - dy, 4)] = piece[x]
 
 
 def finish_kernel(sums, arrived, master, moment, second, weight, master_new, moment_new, second_new):
@@ -170,10 +249,6 @@
 
 def chip_pairs(dz, dx):
     return [(z * 2 + x, (z + dz) % 4 * 2 + (x + dx) % 2) for z in range(4) for x in range(2)]
-
-
-def replica_pairs(dx, dy):
-    return [(x * 4 + y, (x + dx) % 2 * 4 + (y + dy) % 4) for x in range(2) for y in range(4)]
 
 
 def local(
@@ -202,54 +277,64 @@
         blocks.append(lax.ppermute(routed[n + 1], GY[:2], chip_pairs(*step)))
 
     attn_sum, partial = call(
-        sum_kernel, (shape((256, ACOLS), f32), shape((1, 128), f32)), 2000000
+        sum_kernel, (shape((256, ACOLS), f32), shape((128, 128), f32)), 2000000
     )(arrived, part)
     sums = lax.all_to_all(
-        jnp.broadcast_to(partial, (128, 1, 128)), GX_GY, split_axis=0, concat_axis=0, tiled=True
+        partial.reshape(128, 1, 128), GX_GY, split_axis=0, concat_axis=0, tiled=True
     ).reshape(128, 128)
 
-    order = {step: n for n, step in enumerate(((0, 0),) + CHIP_STEPS)}
-    grads = jnp.stack([blocks[order[(n // 2, n % 2)]][:, :, :COLS] for n in range(8)])
-    where = jnp.stack([lax.axis_index("gy_0"), lax.axis_index("gy_1")]).astype(jnp.int32)
-
-    def source(n, at):
-        return (lax.rem(at[0] + 4 - n // 2, 4) * 2 + lax.rem(at[1] + n, 2), 0, 0, 0)
-
-    rows = pl.BlockSpec((ROWS, 2 * COLS), lambda n, at: (0, n))
-    inputs = [
-        pl.BlockSpec((128, 128), lambda n, at: (0, 0)),
-        pl.BlockSpec((1, 2, ROWS, COLS), source),
-        rows,
-        rows,
-        rows,
-    ]
+    here = pl.BlockSpec(memory_space=pltpu.VMEM)
+    far = pl.BlockSpec(memory_space=pltpu.HBM)
     state = (expert_master, expert_moment, expert_second)
+    attn_block = call(
+        attn_weight_kernel,
+        shape((256, ACOLS), bf16),
+        2000000,
+        in_specs=[here] * 2 + [far] * 8,
+        out_specs=here,
+        scratch_shapes=[
+            pltpu.VMEM((8, 2, ROWS, STATE), bf16),
+            pltpu.SemaphoreType.DMA((8,)),
+        ],
+    )(sums, attn_sum, *blocks)
+    other = lax.ppermute(attn_block, "gx_0", [(0, 1), (1, 0)])
     weights = call(
         expert_weight_kernel,
         shape((16, ROWS, BACK), bf16),
-        4000000,
-        grid_spec=pltpu.PrefetchScalarGridSpec(
-            num_scalar_prefetch=1,
-            grid=(8,),
-            in_specs=inputs + [pl.BlockSpec((2 * AROWS, ACOLS), lambda n, at: (n, 0))],
-            out_specs=pl.BlockSpec((2, ROWS, BACK), lambda n, at: (n, 0, 0)),
-        ),
-    )(where, sums, grads, *state, attn_sum)
+        8000000,
+        mib=63,
+        in_specs=[here] * 2 + [far] * 11,
+        out_specs=far,
+        scratch_shapes=[
+            pltpu.VMEM((3, 8, ROWS, 2 * COLS), f32),
+            pltpu.VMEM((8, 2, ROWS, COLS), bf16),
+            pltpu.VMEM((8, 2, ROWS, BACK), bf16),
+            pltpu.SemaphoreType.DMA((8, 4)),
+            pltpu.SemaphoreType.DMA((8,)),
+        ],
+    )(sums, attn_sum, *blocks, *state)
     returned = lax.all_to_all(weights, GY, split_axis=0, concat_axis=0, tiled=True)
-    attn_block = call(attn_weight_kernel, shape((256, ACOLS), bf16), 2000000)(
-        sums, attn_sum, *blocks
-    )
-    pieces = [attn_block]
-    for step in REPLICA_STEPS:
-        pieces.append(lax.ppermute(attn_block, GX, replica_pairs(*step)))
+    both = call(both_kernel, shape((2, 256, ACOLS), bf16), 1000000)(attn_block, other)
+    pieces = [both]
+    for n in range(3):
+        pieces.append(
+            lax.ppermute(both, "gx_1", [(y, (y + REPLICA_STEPS[n]) % 4) for y in range(4)])
+        )
     e_master, e_moment, e_second = call(
         expert_state_kernel,
         (shape((ROWS, 16 * COLS), f32),) * 3,
         8000000,
-        grid_spec=pltpu.PrefetchScalarGridSpec(
-            num_scalar_prefetch=1, grid=(8,), in_specs=inputs, out_specs=[rows] * 3
-        ),
-    )(where, sums, grads, *state)
+        mib=63,
+        in_specs=[here] + [far] * 11,
+        out_specs=[far] * 3,
+        scratch_shapes=[
+            pltpu.VMEM((3, 8, ROWS, 2 * COLS), f32),
+            pltpu.VMEM((8, 2, ROWS, COLS), bf16),
+            pltpu.VMEM((3, 8, ROWS, 2 * COLS), f32),
+            pltpu.SemaphoreType.DMA((8, 4)),
+            pltpu.SemaphoreType.DMA((8, 3)),
+        ],
+    )(sums, *blocks, *state)
     attn_weight = call(join_kernel, shape((8, 256, ACOLS), bf16), 1000000)(*pieces)
     expert_weight, a_master, a_moment, a_second = call(
         finish_kernel,

time: 107 us -> 102 us (0.953)
  blocking collectives: 0 us -> 24.2 us
  starting transfers between devices: 50.9 us -> 27.7 us
  local copies, waits for them, and re-layouts: 26 us -> 6.16 us
  waiting for transfers between devices: 11.1 us -> 21.8 us
  Pallas kernels: 16.3 us -> 20.3 us
    all_to_all x0 -> x1, blocking collectives: none -> 24.2 us  [local(): lax.all_to_all(partial.reshape(128, 1, 128), GX_GY, split_axis=0, concat_...]
    unnamed x57 -> x42, local copies, waits for them, and re-layouts: 24.7 us -> 6.16 us
    ppermute x7 -> x4, waiting for transfers between devices: 9.17 us -> 21.1 us  [the longest x1 15.2 us: local(): other = lax.ppermute(attn_block, 'gx_0', [(0, 1), (1, 0)])]
    all_to_all x1 -> x0, starting transfers between devices: 10 us -> none  [local(): lax.all_to_all(jnp.broadcast_to(partial, (128, 1, 128)), GX_GY, split_axi...]
    ppermute x7 -> x4, starting transfers between devices: 9.76 us -> 3.56 us  [the longest x3 2.84 us: local(): lax.ppermute(both, 'gx_1', [(y, (y + REPLICA_STEPS[n]) % 4) for y in rang...]
    ppermute x7, starting transfers between devices: 17.2 us -> 12.7 us  [local(): blocks.append(lax.ppermute(routed[n + 1], GY[:2], chip_pairs(*step)))]
    all_to_all x1, starting transfers between devices: 7.28 us -> 4.77 us  [local(): lax.all_to_all(weights, GY, split_axis=0, concat_axis=0, tiled=True)]
    all_to_all x1, waiting for transfers between devices: 1.93 us -> 0.01 us  [local(): lax.all_to_all(attn_grad.reshape(8, 256, ACOLS), GX, split_axis=0, concat...]
  transfers between devices with their start and end apart: 18 -> 14, of which waited for: 2 -> 4; matrix products, arithmetic and copies ran while one was open for 10% -> 0% of each run, Pallas kernels for 9% -> 11%
where the time goes in v3:
time: 102 us; the launch traced here: 101 us
  starting transfers between devices  27.7 us (27%)
  blocking collectives  24.2 us (24%)
  waiting for transfers between devices  21.8 us (21%)
  Pallas kernels  20.3 us (20%)
  local copies, waits for them, and re-layouts  6.16 us (6%)
    all_to_all x1, blocking collectives, local(): lax.all_to_all(partial.reshape(128, 1, 128), GX_GY, split_axis=0, concat_...  24.2 us
    ppermute x1, waiting for transfers between devices, local(): other = lax.ppermute(attn_block, 'gx_0', [(0, 1), (1, 0)])  15.2 us
    ppermute x7, starting transfers between devices, local(): blocks.append(lax.ppermute(routed[n + 1], GY[:2], chip_pairs(*step)))  12.7 us
    pallas_call x1, Pallas kernels, local(): call(expert_state_kernel, (shape((ROWS, 16 * COLS), f32),) * 3, 8000000,...  6.73 us
    unnamed x42, local copies, waits for them, and re-layouts  6.16 us
    ppermute x3, waiting for transfers between devices, local(): lax.ppermute(both, 'gx_1', [(y, (y + REPLICA_STEPS[n]) % 4) for y in rang...  5.91 us
    pallas_call x1, Pallas kernels, local(): call(expert_weight_kernel, shape((16, ROWS, BACK), bf16), 8000000, mib=63...  5.29 us
    all_to_all x1, starting transfers between devices, local(): lax.all_to_all(attn_grad.reshape(8, 256, ACOLS), GX, split_axis=0, concat...  5.23 us
  transfers between devices with their start and end apart: 14, of which 4 were waited for; matrix products, arithmetic and copies ran while one was open for 0% of the time, Pallas kernels for 11%

profile of v3, /device:TPU:1, one launch (start us, length us, event | category | flops | bytes accessed | tf_op | source)
XLA Modules:
  0.0 101.1 jit_solution(16288004301358476330)
XLA Ops:
  0.6 0.0 copy-start.14
  0.6 0.9 copy-done.14
  1.6 0.9 copy-done.16
  2.5 0.9 copy-done.18
  3.5 1.2 %copy-done.20 = bf16[1,512,896]{2,1,0:T(8,128)(2,1)S(1)} copy-done((bf16[1,512,896]{2,1,0:T(8,128)(2,1)S(1)}, bf16[1,512,896]{2,1,0:T(8,128)(2,1)}, u32[]{:S(2)}) %copy-start.20) | copy-done | bytes 917528
  4.7 1.1 %shard_map.143 = (bf16[8,32,1664]{2,1,0:T(8,128)(2,1)S(1)}, bf16[8,32,1664]{2,1,0:T(8,128)(2,1)}, f32[1,128]{1,0:T(1,128)S(1)}) custom-call(bf16[16,32,896]{2,1,0:T(8,128)(2,1)S(1)} %bitcast.12, f32[16,4096]{1,0:T(8,128)S(1)} %copy-done.14, f32[16,4096]{1,0:T(8,128)S(1)} %copy-done.16, f32[16,4096]{1,0:T(8,128)S(1)} %copy-done.18), custom_call_target="tpu_custom_call" | custom-call | flops 4000000 | bytes 4096 | tf_op jit(solution)/shard_map/pallas_call | solution.py:268
  5.8 1.4 %collective-permute-start = (bf16[8,32,1664]{2,1,0:T(8,128)(2,1)}, bf16[8,32,1664]{2,1,0:T(8,128)(2,1)S(1)}, u32[]{:S(2)}, u32[]{:S(2)}) collective-permute-start(bf16[8,32,1664]{2,1,0:T(8,128)(2,1)} %get-tuple-element.31), channel_id=1, source_target_pairs={{0,1},{1,0},{2,3},{3,2},{4,5},{5,4},{6,7},{7,6},{8,9},{9,8},{10,11... | collective-permute-start | bytes 2555912 | tf_op jit(solution)/shard_map/ppermute | solution.py:273
  7.2 5.2 %all-to-all-start = ((bf16[8,256,256]{2,1,0:T(8,128)(2,1)}), bf16[8,256,256]{2,1,0:T(8,128)(2,1)S(1)}, u32[]{:S(2)}, u32[]{:S(2)}) async-start(bf16[8,256,256]{2,1,0:T(8,128)(2,1)} %bitcast.14), calls=%async_computation | async-start | bytes 2097152 | tf_op jit(solution)/shard_map/all_to_all | solution.py:264
  12.4 0.0 collective-permute-done.swapped
  12.4 1.1 %shard_map.145 = (bf16[2,32,1664]{2,1,0:T(8,128)(2,1)S(1)}, bf16[2,32,1664]{2,1,0:T(8,128)(2,1)S(1)}, bf16[2,32,1664]{2,1,0:T(8,128)(2,1)S(1)}, bf16[2,32,1664]{...) custom-call(bf16[8,32,1664]{2,1,0:T(8,128)(2,1)S(1)} %get-tuple-elem, ...), custom_call_target="tpu_custom_call" | custom-call | flops 1000000 | bytes 4096 | tf_op jit(solution)/shard_map/pallas_call | solution.py:274
  13.5 0.7 copy-done
  14.2 1.6 %collective-permute-start.1 = (bf16[2,32,1664]{2,1,0:T(8,128)(2,1)S(1)}, bf16[2,32,1664]{2,1,0:T(8,128)(2,1)S(1)}, u32[]{:S(2)}, u32[]{:S(2)}) collective-permute-start(bf16[2,32,1664]{2,1,0:T(8,128)(2,1)S(1)} %get-tuple-element.33), channel_id=1, source_target_pairs={{0,4},{2,6},{4,8},{6,10},{8,12},{10,14},{12,0},{14,2},{1,5},{3,7},... | collective-permute-start | bytes 638984 | tf_op jit(solution)/shard_map/ppermute | solution.py:277
  15.8 2.1 %collective-permute-start.2 = (bf16[2,32,1664]{2,1,0:T(8,128)(2,1)S(1)}, bf16[2,32,1664]{2,1,0:T(8,128)(2,1)S(1)}, u32[]{:S(2)}, u32[]{:S(2)}) collective-permute-start(bf16[2,32,1664]{2,1,0:T(8,128)(2,1)S(1)} %get-tuple-element.34), channel_id=1, source_target_pairs={{0,12},{2,14},{4,0},{6,2},{8,4},{10,6},{12,8},{14,10},{1,13},{3,15... | collective-permute-start | bytes 638984 | tf_op jit(solution)/shard_map/ppermute | solution.py:277
  17.9 1.3 %collective-permute-start.3 = (bf16[2,32,1664]{2,1,0:T(8,128)(2,1)}, bf16[2,32,1664]{2,1,0:T(8,128)(2,1)S(1)}, u32[]{:S(2)}, u32[]{:S(2)}) collective-permute-start(bf16[2,32,1664]{2,1,0:T(8,128)(2,1)} %get-tuple-element.35), channel_id=1, source_target_pairs={{0,8},{2,10},{4,12},{6,14},{8,0},{10,2},{12,4},{14,6},{1,9},{3,11}... | collective-permute-start | bytes 638984 | tf_op jit(solution)/shard_map/ppermute | solution.py:277
  19.2 2.5 %collective-permute-start.4 = (bf16[2,32,1664]{2,1,0:T(8,128)(2,1)}, bf16[2,32,1664]{2,1,0:T(8,128)(2,1)S(1)}, u32[]{:S(2)}, u32[]{:S(2)}) collective-permute-start(bf16[2,32,1664]{2,1,0:T(8,128)(2,1)} %get-tuple-element.36), channel_id=1, source_target_pairs={{0,2},{2,0},{4,6},{6,4},{8,10},{10,8},{12,14},{14,12},{1,3},{3,1},... | collective-permute-start | bytes 638984 | tf_op jit(solution)/shard_map/ppermute | solution.py:277
  21.7 1.0 collective-permute-start.5
  22.6 0.6 collective-permute-done.1.refs_1_
  23.3 3.5 %collective-permute-start.6 = (bf16[2,32,1664]{2,1,0:T(8,128)(2,1)}, bf16[2,32,1664]{2,1,0:T(8,128)(2,1)}, u32[]{:S(2)}, u32[]{:S(2)}) collective-permute-start(bf16[2,32,1664]{2,1,0:T(8,128)(2,1)} %get-tuple-element.38), channel_id=1, source_target_pairs={{0,14},{2,12},{4,2},{6,0},{8,6},{10,4},{12,10},{14,8},{1,15},{3,13... | collective-permute-start | bytes 638984 | tf_op jit(solution)/shard_map/ppermute | solution.py:277
  26.8 0.0 collective-permute-done.2.refs_2_
  26.8 0.8 collective-permute-start.7
  27.5 0.0 all-to-all-done.arrived
  27.5 0.2 shard_map.144
  27.7 0.7 copy-done.12
  28.4 24.2 %all_to_all.15 = f32[128,1,128]{2,1,0:T(1,128)} all-to-all(f32[128,1,128]{2,1,0:T(1,128)S(1)} %bitcast.13), channel_id=1, replica_groups=mesh['gx_0'=2,'gx_1'=4,'gy_0'=4,'gy_1'=2,'gy_2'=2] {'gx_0','gx_1','gy_0'..., dimensions={0} | all-to-all | bytes 131072 | tf_op jit(solution)/shard_map/all_to_all | solution.py:282
  52.6 0.0 collective-permute-done.3.refs_3_
  52.6 0.0 collective-permute-done.4.refs_4_
  52.6 0.0 copy-start.8
  52.6 0.0 collective-permute-done.5.refs_5_
  52.6 0.0 collective-permute-done.6.refs_6_
  52.6 0.0 collective-permute-done.7.refs_7_
  52.6 0.6 copy-done.6
  53.3 0.1 copy-done.8
  53.3 5.3 %shard_map.147 = bf16[16,32,1152]{2,1,0:T(8,128)(2,1)} custom-call(f32[128,128]{1,0:T(8,128)} %bitcast.8, f32[256,256]{1,0:T(8,128)} %copy-done.12, bf16[2,32,1664]{2,1,0:T(8,128)(2,1)} %copy-done, bf16[2,32,1664]{2,1,0:T(8,128)(2,1)} %copy-done.2, bf16[2,32,1664]{2,1,0:T(8,128)(2,1)} %copy-done.4, bf16[2,32,1664]{2,1,0:T(8,128)(2,1)} %copy-done.6, ...), custom_call_target="tpu_custom_call" | custom-call | flops 8000000 | bytes 4096 | tf_op jit(solution)/shard_map/pallas_call | solution.py:301
  58.6 0.0 copy-start.1
  58.6 0.0 copy-start.3
  58.6 0.0 copy-start.5
  58.7 0.0 copy-start.7
  58.7 0.0 copy-start.9
  58.7 0.0 copy-start.13
  58.7 4.8 %all-to-all-start.2 = ((bf16[16,32,1152]{2,1,0:T(8,128)(2,1)}), bf16[16,32,1152]{2,1,0:T(8,128)(2,1)}, u32[]{:S(2)}, u32[]{:S(2)}) async-start(bf16[16,32,1152]{2,1,0:T(8,128)(2,1)} %shard_map.147), calls=%async_computation.2 | async-start | bytes 2359296 | tf_op jit(solution)/shard_map/all_to_all | solution.py:316
  63.5 0.0 copy-done.1
  63.5 0.0 copy-done.3
  63.5 0.0 copy-done.5
  63.5 0.0 copy-done.7
  63.5 0.0 copy-done.9
  63.5 0.0 copy-done.10
  63.5 0.0 copy-done.13
  63.5 1.2 %shard_map.149.own = bf16[256,256]{1,0:T(8,128)(2,1)S(1)} custom-call(f32[128,128]{1,0:T(8,128)S(1)} %bitcast.10, f32[256,256]{1,0:T(8,128)S(1)} %copy-done.13, bf16[2,32,1664]{2,1,0:T(8,128)(2,1)S(1)} %copy-done.1, bf16[2,32,1664]{2,1,0:T(8,128)(2,1)S(1)} %copy-done.3, bf16[2,32,1664]{2,1,0:T(8,128)(2,1)S(1)} %copy-done.5, ...), custom_call_target="tpu_custom_call" | custom-call | flops 2000000 | bytes 4096 | tf_op jit(solution)/shard_map/pallas_call | solution.py:289
  64.7 0.7 collective-permute-start.8
  65.5 15.2 %collective-permute-done.8.other = bf16[256,256]{1,0:T(8,128)(2,1)S(1)} collective-permute-done((bf16[256,256]{1,0:T(8,128)(2,1)S(1)}, bf16[256,256]{1,0:T(8,128)(2,1)S(1)}, u32[]{:S(2)}, u32[]{:S(2)}) %collective-permute-start.8) | collective-permute-done | bytes 131104 | tf_op jit(solution)/shard_map/ppermute | solution.py:300
  80.7 1.1 %collective-permute-start.11 = (bf16[2,256,256]{2,1,0:T(8,128)(2,1)S(1)}, bf16[2,256,256]{2,1,0:T(8,128)(2,1)S(1)}, u32[]{:S(2)}, u32[]{:S(2)}) collective-permute-start(bf16[2,256,256]{2,1,0:T(8,128)(2,1)S(1)} %shard_map.150.refs_0_), channel_id=1, source_target_pairs={{0,32},{16,48},{32,0},{48,16},{1,33},{17,49},{33,1},{49,17},{2,34}... | collective-permute-start | bytes 786440 | tf_op jit(solution)/shard_map/ppermute | solution.py:321
  81.9 1.7 %collective-permute-start.10 = (bf16[2,256,256]{2,1,0:T(8,128)(2,1)S(1)}, bf16[2,256,256]{2,1,0:T(8,128)(2,1)S(1)}, u32[]{:S(2)}, u32[]{:S(2)}) collective-permute-start(bf16[2,256,256]{2,1,0:T(8,128)(2,1)S(1)} %shard_map.150.refs_0_), channel_id=1, source_target_pairs={{0,48},{16,0},{32,16},{48,32},{1,49},{17,1},{33,17},{49,33},{2,50}... | collective-permute-start | bytes 786440 | tf_op jit(solution)/shard_map/ppermute | solution.py:321
  83.6 0.0 collective-permute-start.9
  83.6 6.7 %shard_map.146 = (f32[32,14336]{1,0:T(8,128)}, f32[32,14336]{1,0:T(8,128)}, f32[32,14336]{1,0:T(8,128)}) custom-call(f32[128,128]{1,0:T(8,128)} %bitcast.9, bf16[2,32,1664]{2,1,0:T(8,128)(2,1)} %copy-done, bf16[2,32,1664]{2,1,0:T(8,128)(2,1)} %copy-done.2, bf16[2,32,1664]{2,1,0:T(8,128)(2,1)} %copy-done.4, bf16[2,32,1664]{2,1,0:T(8,128)(2,1)} %copy-done.6, ...), custom_call_target="tpu_custom_call" | custom-call | flops 8000000 | bytes 4096 | tf_op jit(solution)/shard_map/pallas_call | solution.py:323
  90.3 0.0 copy-start.15
  90.3 0.0 copy-start.17
  90.3 0.0 copy-start.19
  90.4 0.0 collective-permute-done.11.refs_3_
  90.4 3.2 %collective-permute-done.10.refs_2_ = bf16[2,256,256]{2,1,0:T(8,128)(2,1)S(1)} collective-permute-done((bf16[2,256,256]{2,1,0:T(8,128)(2,1)S(1)}, bf16[2,256,256]{2,1,0:T(8,128)(2,1)S(1)}, u32[]{:S(2)}, u32[]{:S(2)}) %collective-permute-start.10) | collective-permute-done | bytes 262176 | tf_op jit(solution)/shard_map/ppermute | solution.py:321
  93.6 2.7 %collective-permute-done.9.refs_1_ = bf16[2,256,256]{2,1,0:T(8,128)(2,1)} collective-permute-done((bf16[2,256,256]{2,1,0:T(8,128)(2,1)S(1)}, bf16[2,256,256]{2,1,0:T(8,128)(2,1)}, u32[]{:S(2)}, u32[]{:S(2)}) %collective-permute-start.9) | collective-permute-done | bytes 262176 | tf_op jit(solution)/shard_map/ppermute | solution.py:321
  96.3 2.0 %shard_map.151 = bf16[8,256,256]{2,1,0:T(8,128)(2,1)} custom-call(bf16[2,256,256]{2,1,0:T(8,128)(2,1)S(1)} %shard_map.150.refs_0_, bf16[2,256,256]{2,1,0:T(8,128)(2,1)} %collective-permute-done.9.refs_1_, bf16[2,256,256]{2,1,0:T(8,128)(2,1)S(1)} %collective-permute-done.10.refs_2_, bf16[2,256,256]{2,1,0:T(8,128)(2,1)S(1)} %collective-permute-done.11.refs_3_), custom_call_target="tpu_custom_call" | custom-call | flops 1000000 | bytes 4096 | tf_op jit(solution)/shard_map/pallas_call | solution.py:338
  98.3 0.0 all-to-all-done.2.arrived
  98.3 0.0 copy-done.15
  98.3 2.8 %shard_map.148 = (bf16[16,32,896]{2,1,0:T(8,128)(2,1)}, f32[16,4096]{1,0:T(8,128)}, f32[16,4096]{1,0:T(8,128)}, f32[16,4096]{1,0:T(8,128)}) custom-call(f32[128,128]{1,0:T(8,128)S(1)} %bitcast.11, bf16[16,32,1152]{2,1,0:T(8,128)(2,1)} %all-to-all-done.2.arrived, f32[16,4096]{1,0:T(8,128)S(1)} %copy-done.15, f32[16,4096]{1,0:T(8,128)S(1)} %copy-done.17, ...), custom_call_target="tpu_custom_call" | custom-call | flops 2000000 | bytes 4096 | tf_op jit(solution)/shard_map/pallas_call | solution.py:339
  (16 shorter events, 0.1 us)
Async XLA Ops:
  0.6 1.0 copy-start.14
  1.6 0.9 copy-start.16
  2.5 0.9 copy-start.18
  3.5 1.2 %copy-start.20 = (bf16[1,512,896]{2,1,0:T(8,128)(2,1)S(1)}, bf16[1,512,896]{2,1,0:T(8,128)(2,1)}, u32[]{:S(2)}) copy-start(bf16[1,512,896]{2,1,0:T(8,128)(2,1)} %param.8) | copy-start | bytes 2752516
  5.8 6.6 %collective-permute-start = (bf16[8,32,1664]{2,1,0:T(8,128)(2,1)}, bf16[8,32,1664]{2,1,0:T(8,128)(2,1)S(1)}, u32[]{:S(2)}, u32[]{:S(2)}) collective-permute-start(bf16[8,32,1664]{2,1,0:T(8,128)(2,1)} %get-tuple-element.31), channel_id=1, source_target_pairs={{0,1},{1,0},{2,3},{3,2},{4,5},{5,4},{6,7},{7,6},{8,9},{9,8},{10,11... | collective-permute-start | bytes 2555912 | tf_op jit(solution)/shard_map/ppermute | solution.py:273
  7.2 20.4 %all-to-all-start = ((bf16[8,256,256]{2,1,0:T(8,128)(2,1)}), bf16[8,256,256]{2,1,0:T(8,128)(2,1)S(1)}, u32[]{:S(2)}, u32[]{:S(2)}) async-start(bf16[8,256,256]{2,1,0:T(8,128)(2,1)} %bitcast.14), calls=%async_computation | async-start | bytes 2097152 | tf_op jit(solution)/shard_map/all_to_all | solution.py:264
  13.5 0.7 copy-start
  14.2 9.1 %collective-permute-start.1 = (bf16[2,32,1664]{2,1,0:T(8,128)(2,1)S(1)}, bf16[2,32,1664]{2,1,0:T(8,128)(2,1)S(1)}, u32[]{:S(2)}, u32[]{:S(2)}) collective-permute-start(bf16[2,32,1664]{2,1,0:T(8,128)(2,1)S(1)} %get-tuple-element.33), channel_id=1, source_target_pairs={{0,4},{2,6},{4,8},{6,10},{8,12},{10,14},{12,0},{14,2},{1,5},{3,7},... | collective-permute-start | bytes 638984 | tf_op jit(solution)/shard_map/ppermute | solution.py:277
  15.8 11.0 %collective-permute-start.2 = (bf16[2,32,1664]{2,1,0:T(8,128)(2,1)S(1)}, bf16[2,32,1664]{2,1,0:T(8,128)(2,1)S(1)}, u32[]{:S(2)}, u32[]{:S(2)}) collective-permute-start(bf16[2,32,1664]{2,1,0:T(8,128)(2,1)S(1)} %get-tuple-element.34), channel_id=1, source_target_pairs={{0,12},{2,14},{4,0},{6,2},{8,4},{10,6},{12,8},{14,10},{1,13},{3,15... | collective-permute-start | bytes 638984 | tf_op jit(solution)/shard_map/ppermute | solution.py:277
  17.9 34.6 %collective-permute-start.3 = (bf16[2,32,1664]{2,1,0:T(8,128)(2,1)}, bf16[2,32,1664]{2,1,0:T(8,128)(2,1)S(1)}, u32[]{:S(2)}, u32[]{:S(2)}) collective-permute-start(bf16[2,32,1664]{2,1,0:T(8,128)(2,1)} %get-tuple-element.35), channel_id=1, source_target_pairs={{0,8},{2,10},{4,12},{6,14},{8,0},{10,2},{12,4},{14,6},{1,9},{3,11}... | collective-permute-start | bytes 638984 | tf_op jit(solution)/shard_map/ppermute | solution.py:277
  19.2 33.4 %collective-permute-start.4 = (bf16[2,32,1664]{2,1,0:T(8,128)(2,1)}, bf16[2,32,1664]{2,1,0:T(8,128)(2,1)S(1)}, u32[]{:S(2)}, u32[]{:S(2)}) collective-permute-start(bf16[2,32,1664]{2,1,0:T(8,128)(2,1)} %get-tuple-element.36), channel_id=1, source_target_pairs={{0,2},{2,0},{4,6},{6,4},{8,10},{10,8},{12,14},{14,12},{1,3},{3,1},... | collective-permute-start | bytes 638984 | tf_op jit(solution)/shard_map/ppermute | solution.py:277
  21.7 30.9 %collective-permute-start.5 = (bf16[2,32,1664]{2,1,0:T(8,128)(2,1)}, bf16[2,32,1664]{2,1,0:T(8,128)(2,1)}, u32[]{:S(2)}, u32[]{:S(2)}) collective-permute-start(bf16[2,32,1664]{2,1,0:T(8,128)(2,1)} %get-tuple-element.37), channel_id=1, source_target_pairs={{0,6},{2,4},{4,10},{6,8},{8,14},{10,12},{12,2},{14,0},{1,7},{3,5},... | collective-permute-start | bytes 638984 | tf_op jit(solution)/shard_map/ppermute | solution.py:277
  23.3 29.4 %copy-start.2 = (bf16[2,32,1664]{2,1,0:T(8,128)(2,1)}, bf16[2,32,1664]{2,1,0:T(8,128)(2,1)S(1)}, u32[]{:S(2)}) copy-start(bf16[2,32,1664]{2,1,0:T(8,128)(2,1)S(1)} %collective-permute-done.1.refs_1_) | copy-start | bytes 638980
  23.3 29.3 %collective-permute-start.6 = (bf16[2,32,1664]{2,1,0:T(8,128)(2,1)}, bf16[2,32,1664]{2,1,0:T(8,128)(2,1)}, u32[]{:S(2)}, u32[]{:S(2)}) collective-permute-start(bf16[2,32,1664]{2,1,0:T(8,128)(2,1)} %get-tuple-element.38), channel_id=1, source_target_pairs={{0,14},{2,12},{4,2},{6,0},{8,6},{10,4},{12,10},{14,8},{1,15},{3,13... | collective-permute-start | bytes 638984 | tf_op jit(solution)/shard_map/ppermute | solution.py:277
  26.8 25.9 %copy-start.4 = (bf16[2,32,1664]{2,1,0:T(8,128)(2,1)}, bf16[2,32,1664]{2,1,0:T(8,128)(2,1)S(1)}, u32[]{:S(2)}) copy-start(bf16[2,32,1664]{2,1,0:T(8,128)(2,1)S(1)} %collective-permute-done.2.refs_2_) | copy-start | bytes 638980
  26.8 25.8 %collective-permute-start.7 = (bf16[2,32,1664]{2,1,0:T(8,128)(2,1)}, bf16[2,32,1664]{2,1,0:T(8,128)(2,1)}, u32[]{:S(2)}, u32[]{:S(2)}) collective-permute-start(bf16[2,32,1664]{2,1,0:T(8,128)(2,1)} %get-tuple-element.39), channel_id=1, source_target_pairs={{0,10},{2,8},{4,14},{6,12},{8,2},{10,0},{12,6},{14,4},{1,11},{3,9}... | collective-permute-start | bytes 638984 | tf_op jit(solution)/shard_map/ppermute | solution.py:277
  27.7 0.7 copy-start.12
  52.6 0.7 copy-start.6
  52.6 0.7 copy-start.8
  58.6 4.9 %copy-start.1 = (bf16[2,32,1664]{2,1,0:T(8,128)(2,1)S(1)}, bf16[2,32,1664]{2,1,0:T(8,128)(2,1)}, u32[]{:S(2)}) copy-start(bf16[2,32,1664]{2,1,0:T(8,128)(2,1)} %copy-done) | copy-start | bytes 638980
  58.6 4.8 %copy-start.3 = (bf16[2,32,1664]{2,1,0:T(8,128)(2,1)S(1)}, bf16[2,32,1664]{2,1,0:T(8,128)(2,1)}, u32[]{:S(2)}) copy-start(bf16[2,32,1664]{2,1,0:T(8,128)(2,1)} %copy-done.2) | copy-start | bytes 638980
  58.6 4.8 %copy-start.5 = (bf16[2,32,1664]{2,1,0:T(8,128)(2,1)S(1)}, bf16[2,32,1664]{2,1,0:T(8,128)(2,1)}, u32[]{:S(2)}) copy-start(bf16[2,32,1664]{2,1,0:T(8,128)(2,1)} %copy-done.4) | copy-start | bytes 638980
  58.7 4.8 %copy-start.7 = (bf16[2,32,1664]{2,1,0:T(8,128)(2,1)S(1)}, bf16[2,32,1664]{2,1,0:T(8,128)(2,1)}, u32[]{:S(2)}) copy-start(bf16[2,32,1664]{2,1,0:T(8,128)(2,1)} %copy-done.6) | copy-start | bytes 638980
  58.7 4.8 %copy-start.9 = (bf16[2,32,1664]{2,1,0:T(8,128)(2,1)S(1)}, bf16[2,32,1664]{2,1,0:T(8,128)(2,1)}, u32[]{:S(2)}) copy-start(bf16[2,32,1664]{2,1,0:T(8,128)(2,1)} %copy-done.8) | copy-start | bytes 638980
  58.7 4.8 %copy-start.10 = (f32[128,1,128]{2,1,0:T(1,128)S(1)}, f32[128,1,128]{2,1,0:T(1,128)}, u32[]{:S(2)}) copy-start(f32[128,1,128]{2,1,0:T(1,128)} %all_to_all.15) | copy-start | bytes 196612
  58.7 4.8 %copy-start.13 = (f32[256,256]{1,0:T(8,128)S(1)}, f32[256,256]{1,0:T(8,128)}, u32[]{:S(2)}) copy-start(f32[256,256]{1,0:T(8,128)} %copy-done.12) | copy-start | bytes 786436
  58.7 39.6 %all-to-all-start.2 = ((bf16[16,32,1152]{2,1,0:T(8,128)(2,1)}), bf16[16,32,1152]{2,1,0:T(8,128)(2,1)}, u32[]{:S(2)}, u32[]{:S(2)}) async-start(bf16[16,32,1152]{2,1,0:T(8,128)(2,1)} %shard_map.147), calls=%async_computation.2 | async-start | bytes 2359296 | tf_op jit(solution)/shard_map/all_to_all | solution.py:316
  64.7 16.0 %collective-permute-start.8 = (bf16[256,256]{1,0:T(8,128)(2,1)S(1)}, bf16[256,256]{1,0:T(8,128)(2,1)S(1)}, u32[]{:S(2)}, u32[]{:S(2)}) collective-permute-start(bf16[256,256]{1,0:T(8,128)(2,1)S(1)} %shard_map.149.own), channel_id=1, source_target_pairs={{0,64},{64,0},{1,65},{65,1},{2,66},{66,2},{3,67},{67,3},{4,68},{68... | collective-permute-start | bytes 393224 | tf_op jit(solution)/shard_map/ppermute | solution.py:300
  80.7 9.6 %collective-permute-start.11 = (bf16[2,256,256]{2,1,0:T(8,128)(2,1)S(1)}, bf16[2,256,256]{2,1,0:T(8,128)(2,1)S(1)}, u32[]{:S(2)}, u32[]{:S(2)}) collective-permute-start(bf16[2,256,256]{2,1,0:T(8,128)(2,1)S(1)} %shard_map.150.refs_0_), channel_id=1, source_target_pairs={{0,32},{16,48},{32,0},{48,16},{1,33},{17,49},{33,1},{49,17},{2,34}... | collective-permute-start | bytes 786440 | tf_op jit(solution)/shard_map/ppermute | solution.py:321
  81.9 11.7 %collective-permute-start.10 = (bf16[2,256,256]{2,1,0:T(8,128)(2,1)S(1)}, bf16[2,256,256]{2,1,0:T(8,128)(2,1)S(1)}, u32[]{:S(2)}, u32[]{:S(2)}) collective-permute-start(bf16[2,256,256]{2,1,0:T(8,128)(2,1)S(1)} %shard_map.150.refs_0_), channel_id=1, source_target_pairs={{0,48},{16,0},{32,16},{48,32},{1,49},{17,1},{33,17},{49,33},{2,50}... | collective-permute-start | bytes 786440 | tf_op jit(solution)/shard_map/ppermute | solution.py:321
  83.6 12.7 %collective-permute-start.9 = (bf16[2,256,256]{2,1,0:T(8,128)(2,1)S(1)}, bf16[2,256,256]{2,1,0:T(8,128)(2,1)}, u32[]{:S(2)}, u32[]{:S(2)}) collective-permute-start(bf16[2,256,256]{2,1,0:T(8,128)(2,1)S(1)} %shard_map.150.refs_0_), channel_id=1, source_target_pairs={{0,16},{16,32},{32,48},{48,0},{1,17},{17,33},{33,49},{49,1},{2,18}... | collective-permute-start | bytes 786440 | tf_op jit(solution)/shard_map/ppermute | solution.py:321
  90.3 8.0 %copy-start.11 = (f32[128,1,128]{2,1,0:T(1,128)S(1)}, f32[128,1,128]{2,1,0:T(1,128)}, u32[]{:S(2)}) copy-start(f32[128,1,128]{2,1,0:T(1,128)} %all_to_all.15) | copy-start | bytes 196612
  90.3 8.0 %copy-start.15 = (f32[16,4096]{1,0:T(8,128)S(1)}, f32[16,4096]{1,0:T(8,128)}, u32[]{:S(2)}) copy-start(f32[16,4096]{1,0:T(8,128)} %master.3) | copy-start | bytes 786436
  90.3 8.0 %copy-start.17 = (f32[16,4096]{1,0:T(8,128)S(1)}, f32[16,4096]{1,0:T(8,128)}, u32[]{:S(2)}) copy-start(f32[16,4096]{1,0:T(8,128)} %moment.3) | copy-start | bytes 786436
  90.3 8.0 %copy-start.19 = (f32[16,4096]{1,0:T(8,128)S(1)}, f32[16,4096]{1,0:T(8,128)}, u32[]{:S(2)}) copy-start(f32[16,4096]{1,0:T(8,128)} %second.3) | copy-start | bytes 786436

commit v4 on v3

--- a/solution.py
+++ b/solution.py
@@ -44,6 +44,14 @@
 
 def shape(dims, dtype):
     return jax.ShapeDtypeStruct(dims, dtype)
+
+
+def near(*arrays):
+    return [pltpu.with_memory_space_constraint(array, pltpu.VMEM) for array in arrays]
+
+
+def far(*arrays):
+    return [pltpu.with_memory_space_constraint(array, pltpu.HBM) for array in arrays]
 
 
 def halves(x):
@@ -124,27 +132,22 @@
     return slice(at * 128, (at + 1) * 128)
 
 
-def expert_loads(blocks, state, held, grads, sems):
+def expert_weight_kernel(sums, attn, *refs):
+    blocks, master, streams, out = refs[:8], refs[8], refs[9:11], refs[11]
+    held, weights, sems, out_sems = refs[12:]
     loads = []
-    for n, (chip, block) in enumerate(zip(sources(), blocks)):
-        copies = [pltpu.make_async_copy(block.at[:, :, :COLS], grads.at[n], sems.at[n, 3])]
-        for m, array in enumerate(state):
-            copies.append(
+    for n, chip in enumerate(sources()):
+        loads.append(
+            [
                 pltpu.make_async_copy(array.at[:, wide_cols(chip)], held.at[m, n], sems.at[n, m])
-            )
-        for copy in copies:
+                for m, array in enumerate(streams)
+            ]
+        )
+        for copy in loads[n]:
             copy.start()
-        loads.append(copies)
-    return loads
-
-
-def expert_weight_kernel(sums, attn, *refs):
-    blocks, state, out = refs[:8], refs[8:11], refs[11]
-    held, grads, weights, sems, out_sems = refs[12:]
-    loads = expert_loads(blocks, state, held, grads, sems)
     clip = clip_of(sums)
     stores = []
-    for n, chip in enumerate(sources()):
+    for n, (chip, block) in enumerate(zip(sources(), blocks)):
         for core in range(2):
             rows = pl.ds(pl.multiple_of((chip * 2 + core) * AROWS, AROWS), AROWS)
             high, low = halves(attn[rows, :])
@@ -154,11 +157,12 @@
             copy.wait()
         for at in range(14):
             core, col = divmod(at, 7)
+            here = pl.ds(pl.multiple_of((chip * 14 + at) * 128, 128), 128)
             new, _, _ = adam_update(
-                grads[n, core, :, lanes(col)].astype(f32),
+                block[core, :, lanes(col)].astype(f32),
+                master[:, here],
                 held[0, n, :, lanes(at)],
                 held[1, n, :, lanes(at)],
-                held[2, n, :, lanes(at)],
                 clip,
             )
             weights[n, core, :, lanes(col)] = new.astype(bf16)
@@ -172,7 +176,16 @@
 def expert_state_kernel(sums, *refs):
     blocks, state, outs = refs[:8], refs[8:11], refs[11:14]
     held, grads, news, sems, out_sems = refs[14:]
-    loads = expert_loads(blocks, state, held, grads, sems)
+    loads = []
+    for n, (chip, block) in enumerate(zip(sources(), blocks)):
+        copies = [pltpu.make_async_copy(block.at[:, :, :COLS], grads.at[n], sems.at[n, 3])]
+        for m, array in enumerate(state):
+            copies.append(
+                pltpu.make_async_copy(array.at[:, wide_cols(chip)], held.at[m, n], sems.at[n, m])
+            )
+        for copy in copies:
+            copy.start()
+        loads.append(copies)
     clip = clip_of(sums)
     stores = []
     for n, chip in enumerate(sources()):
@@ -200,18 +213,12 @@
 
 
 def attn_weight_kernel(sums, attn, *refs):
-    blocks, out, held, sems = refs[:8], refs[8], refs[9], refs[10]
-    loads = []
-    for n, block in enumerate(blocks):
-        copy = pltpu.make_async_copy(block.at[:, :, COLS:], held.at[n], sems.at[n])
-        copy.start()
-        loads.append(copy)
+    blocks, out = refs[:8], refs[8]
     clip = clip_of(sums)
-    for n, chip in enumerate(sources()):
-        loads[n].wait()
+    for chip, block in zip(sources(), blocks):
         for core in range(2):
             rows = pl.ds(pl.multiple_of((chip * 2 + core) * AROWS, AROWS), AROWS)
-            state = held[n, core, :AROWS, :].astype(f32) + held[n, core, AROWS:, :].astype(f32)
+            state = block[core, :AROWS, COLS:].astype(f32) + block[core, AROWS:, COLS:].astype(f32)
             new, _, _ = adam_update(
                 attn[rows, :],
                 state[:, :ACOLS],
@@ -228,23 +235,39 @@
     out[1 - x] = other[...]
 
 
-def join_kernel(*refs):
-    pieces, out = refs[:-1], refs[-1]
+def finish_kernel(sums, arrived, *refs):
+    pieces, state, weight, attn_weight = refs[:4], refs[4:7], refs[7], refs[8]
+    outs, news, sems, out_sems = refs[9:12], refs[12], refs[13], refs[14]
     y = lax.axis_index("gx_1")
-    for dy, piece in zip((0,) + REPLICA_STEPS, pieces):
+    stores = [pltpu.make_async_copy(arrived.at[:, :, :COLS], weight, sems.at[8])]
+    for n, (dy, piece) in enumerate(zip((0,) + REPLICA_STEPS, pieces)):
         for x in range(2):
-            out[x * 4 + lax.rem(y + 4 - dy, 4)] = piece[x]
-
-
-def finish_kernel(sums, arrived, master, moment, second, weight, master_new, moment_new, second_new):
+            slot = x * 4 + lax.rem(y + 4 - dy, 4)
+            stores.append(
+                pltpu.make_async_copy(piece.at[x], attn_weight.at[slot], sems.at[2 * n + x])
+            )
+    for store in stores:
+        store.start()
     clip = clip_of(sums)
-    for group in range(16):
-        weight[group] = arrived[group, :, :COLS]
-        cols = slice(group * ACOLS, (group + 1) * ACOLS)
-        gradient = arrived[group, :AROWS, COLS:].astype(f32) + arrived[group, AROWS:, COLS:].astype(f32)
-        master_new[:, cols], moment_new[:, cols], second_new[:, cols] = adam_update(
-            gradient, master[:, cols], moment[:, cols], second[:, cols], clip
-        )
+    for part in range(4):
+        for group in range(4 * part, 4 * part + 4):
+            cols = slice(group * ACOLS, (group + 1) * ACOLS)
+            gradient = arrived[group, :AROWS, COLS:].astype(f32)
+            gradient = gradient + arrived[group, AROWS:, COLS:].astype(f32)
+            results = adam_update(
+                gradient, state[0][:, cols], state[1][:, cols], state[2][:, cols], clip
+            )
+            for m, result in enumerate(results):
+                news[m, :, cols] = result
+        cols = pl.ds(part * 4 * ACOLS, 4 * ACOLS)
+        for m, out in enumerate(outs):
+            store = pltpu.make_async_copy(
+                news.at[m, :, cols], out.at[:, cols], out_sems.at[part, m]
+            )
+            store.start()
+            stores.append(store)
+    for store in stores:
+        store.wait()
 
 
 def chip_pairs(dz, dx):
@@ -283,38 +306,28 @@
         partial.reshape(128, 1, 128), GX_GY, split_axis=0, concat_axis=0, tiled=True
     ).reshape(128, 128)
 
-    here = pl.BlockSpec(memory_space=pltpu.VMEM)
-    far = pl.BlockSpec(memory_space=pltpu.HBM)
-    state = (expert_master, expert_moment, expert_second)
-    attn_block = call(
-        attn_weight_kernel,
-        shape((256, ACOLS), bf16),
-        2000000,
-        in_specs=[here] * 2 + [far] * 8,
-        out_specs=here,
-        scratch_shapes=[
-            pltpu.VMEM((8, 2, ROWS, STATE), bf16),
-            pltpu.SemaphoreType.DMA((8,)),
-        ],
-    )(sums, attn_sum, *blocks)
+    vmem = pl.BlockSpec(memory_space=pltpu.VMEM)
+    hbm = pl.BlockSpec(memory_space=pltpu.HBM)
+    state = far(expert_master, expert_moment, expert_second)
+    attn_block = call(attn_weight_kernel, pltpu.VMEM((256, ACOLS), bf16), 2000000)(
+        *near(sums, attn_sum, *blocks)
+    )
     other = lax.ppermute(attn_block, "gx_0", [(0, 1), (1, 0)])
     weights = call(
         expert_weight_kernel,
-        shape((16, ROWS, BACK), bf16),
+        pltpu.HBM((16, ROWS, BACK), bf16),
         8000000,
-        mib=63,
-        in_specs=[here] * 2 + [far] * 11,
-        out_specs=far,
+        in_specs=[vmem] * 11 + [hbm] * 2,
+        out_specs=hbm,
         scratch_shapes=[
-            pltpu.VMEM((3, 8, ROWS, 2 * COLS), f32),
-            pltpu.VMEM((8, 2, ROWS, COLS), bf16),
+            pltpu.VMEM((2, 8, ROWS, 2 * COLS), f32),
             pltpu.VMEM((8, 2, ROWS, BACK), bf16),
-            pltpu.SemaphoreType.DMA((8, 4)),
+            pltpu.SemaphoreType.DMA((8, 2)),
             pltpu.SemaphoreType.DMA((8,)),
         ],
-    )(sums, attn_sum, *blocks, *state)
+    )(*near(sums, attn_sum, *blocks, expert_master), *far(expert_moment, expert_second))
     returned = lax.all_to_all(weights, GY, split_axis=0, concat_axis=0, tiled=True)
-    both = call(both_kernel, shape((2, 256, ACOLS), bf16), 1000000)(attn_block, other)
+    both = call(both_kernel, pltpu.VMEM((2, 256, ACOLS), bf16), 1000000)(*near(attn_block, other))
     pieces = [both]
     for n in range(3):
         pieces.append(
@@ -322,11 +335,11 @@
         )
     e_master, e_moment, e_second = call(
         expert_state_kernel,
-        (shape((ROWS, 16 * COLS), f32),) * 3,
+        (pltpu.HBM((ROWS, 16 * COLS), f32),) * 3,
         8000000,
-        mib=63,
-        in_specs=[here] + [far] * 11,
-        out_specs=[far] * 3,
+        mib=16,
+        in_specs=[vmem] + [hbm] * 11,
+        out_specs=[hbm] * 3,
         scratch_shapes=[
             pltpu.VMEM((3, 8, ROWS, 2 * COLS), f32),
             pltpu.VMEM((8, 2, ROWS, COLS), bf16),
@@ -334,13 +347,20 @@
             pltpu.SemaphoreType.DMA((8, 4)),
             pltpu.SemaphoreType.DMA((8, 3)),
         ],
-    )(sums, *blocks, *state)
-    attn_weight = call(join_kernel, shape((8, 256, ACOLS), bf16), 1000000)(*pieces)
-    expert_weight, a_master, a_moment, a_second = call(
+    )(sums, *far(*blocks), *state)
+    expert_weight, attn_weight, a_master, a_moment, a_second = call(
         finish_kernel,
-        (shape((16, ROWS, COLS), bf16),) + (shape((AROWS, 16 * ACOLS), f32),) * 3,
+        (pltpu.HBM((16, ROWS, COLS), bf16), pltpu.HBM((8, 256, ACOLS), bf16))
+        + (pltpu.HBM((AROWS, 16 * ACOLS), f32),) * 3,
         2000000,
-    )(sums, returned, attn_master, attn_moment, attn_second)
+        in_specs=[vmem] * 9,
+        out_specs=[hbm] * 5,
+        scratch_shapes=[
+            pltpu.VMEM((3, AROWS, 16 * ACOLS), f32),
+            pltpu.SemaphoreType.DMA((9,)),
+            pltpu.SemaphoreType.DMA((4, 3)),
+        ],
+    )(*near(sums, returned, *pieces), attn_master, attn_moment, attn_second)
     return (
         e_master,
         e_moment,

time: 102 us -> 98.1 us (0.962)
  Pallas kernels: 20.3 us -> 17.5 us
  local copies, waits for them, and re-layouts: 6.16 us -> 7.88 us
  blocking collectives: 24.2 us -> 22.9 us
    pallas_call x6 -> x5, Pallas kernels: 18 us -> 14 us  [the longest x1 5.89 us: local(): call(expert_state_kernel, (pltpu.HBM((ROWS, 16 * COLS), f32),) * 3, 80000...]
    unnamed x42 -> x30, local copies, waits for them, and re-layouts: 6.16 us -> 7.88 us
    all_to_all x1, blocking collectives: 24.2 us -> 22.9 us  [local(): lax.all_to_all(partial.reshape(128, 1, 128), GX_GY, split_axis=0, concat_...]
    ppermute x1, waiting for transfers between devices: 15.2 us -> 14 us  [local(): other = lax.ppermute(attn_block, 'gx_0', [(0, 1), (1, 0)])]
    pallas_call x1, Pallas kernels: 1.08 us -> 2.22 us  [local(): call(route_kernel, (shape((2, ROWS, WIDE), bf16),) * 8, 1000000)]
  transfers between devices with their start and end apart: 14 -> 14, of which waited for: 4 -> 4; matrix products, arithmetic and copies ran while one was open for 0% -> 0% of each run, Pallas kernels for 11% -> 10%
where the time goes in v4:
time: 98.1 us; the launch traced here: 97.6 us
  starting transfers between devices  27.3 us (28%)
  blocking collectives  22.9 us (23%)
  waiting for transfers between devices  21.2 us (22%)
  Pallas kernels  17.5 us (18%)
  local copies, waits for them, and re-layouts  7.88 us (8%)
    all_to_all x1, blocking collectives, local(): lax.all_to_all(partial.reshape(128, 1, 128), GX_GY, split_axis=0, concat_...  22.9 us
    ppermute x1, waiting for transfers between devices, local(): other = lax.ppermute(attn_block, 'gx_0', [(0, 1), (1, 0)])  14 us
    ppermute x7, starting transfers between devices, local(): blocks.append(lax.ppermute(routed[n + 1], GY[:2], chip_pairs(*step)))  12.8 us
    unnamed x30, local copies, waits for them, and re-layouts  7.88 us
    ppermute x3, waiting for transfers between devices, local(): lax.ppermute(both, 'gx_1', [(y, (y + REPLICA_STEPS[n]) % 4) for y in rang...  6.59 us
    pallas_call x1, Pallas kernels, local(): call(expert_state_kernel, (pltpu.HBM((ROWS, 16 * COLS), f32),) * 3, 80000...  5.89 us
    all_to_all x1, starting transfers between devices, local(): lax.all_to_all(attn_grad.reshape(8, 256, ACOLS), GX, split_axis=0, concat...  5.23 us
    pallas_call x1, Pallas kernels, local(): call(expert_weight_kernel, pltpu.HBM((16, ROWS, BACK), bf16), 8000000, in...  4.73 us
  transfers between devices with their start and end apart: 14, of which 4 were waited for; matrix products, arithmetic and copies ran while one was open for 0% of the time, Pallas kernels for 10%

profile of v4, /device:TPU:1, one launch (start us, length us, event | category | flops | bytes accessed | tf_op | source)
XLA Modules:
  0.0 97.6 jit_solution(4501234133446720051)
XLA Ops:
  0.6 0.0 copy-start.6
  0.6 0.9 copy-done.6
  1.6 0.0 copy-start.8
  1.6 0.9 copy-done.8
  2.5 0.0 copy-start.10
  2.5 0.9 copy-done.10
  3.5 1.2 %copy-done.12 = bf16[1,512,896]{2,1,0:T(8,128)(2,1)S(1)} copy-done((bf16[1,512,896]{2,1,0:T(8,128)(2,1)S(1)}, bf16[1,512,896]{2,1,0:T(8,128)(2,1)}, u32[]{:S(2)}) %copy-start.12) | copy-done | bytes 917528
  4.7 1.1 %shard_map.143 = (bf16[8,32,1664]{2,1,0:T(8,128)(2,1)S(1)}, bf16[8,32,1664]{2,1,0:T(8,128)(2,1)}, f32[1,128]{1,0:T(1,128)S(1)}) custom-call(bf16[16,32,896]{2,1,0:T(8,128)(2,1)S(1)} %bitcast.12, f32[16,4096]{1,0:T(8,128)S(1)} %copy-done.6, f32[16,4096]{1,0:T(8,128)S(1)} %copy-done.8, f32[16,4096]{1,0:T(8,128)S(1)} %copy-done.10), custom_call_target="tpu_custom_call" | custom-call | flops 4000000 | bytes 4096 | tf_op jit(solution)/shard_map/pallas_call | solution.py:291
  5.8 0.0 copy-start.13
  5.8 0.9 copy-done.13
  6.7 1.4 %collective-permute-start = (bf16[8,32,1664]{2,1,0:T(8,128)(2,1)}, bf16[8,32,1664]{2,1,0:T(8,128)(2,1)}, u32[]{:S(2)}, u32[]{:S(2)}) collective-permute-start(bf16[8,32,1664]{2,1,0:T(8,128)(2,1)} %get-tuple-element.32), channel_id=1, source_target_pairs={{0,1},{1,0},{2,3},{3,2},{4,5},{5,4},{6,7},{7,6},{8,9},{9,8},{10,11... | collective-permute-start | bytes 2555912 | tf_op jit(solution)/shard_map/ppermute | solution.py:296
  8.1 5.2 %all-to-all-start = ((bf16[8,256,256]{2,1,0:T(8,128)(2,1)}), bf16[8,256,256]{2,1,0:T(8,128)(2,1)S(1)}, u32[]{:S(2)}, u32[]{:S(2)}) async-start(bf16[8,256,256]{2,1,0:T(8,128)(2,1)} %bitcast.14), calls=%async_computation | async-start | bytes 2097152 | tf_op jit(solution)/shard_map/all_to_all | solution.py:287
  13.3 0.0 copy-start
  13.3 0.0 collective-permute-done.swapped
  13.3 0.0 copy-start.14
  13.3 1.3 %copy-done.14 = bf16[8,32,1664]{2,1,0:T(8,128)(2,1)S(1)} copy-done((bf16[8,32,1664]{2,1,0:T(8,128)(2,1)S(1)}, bf16[8,32,1664]{2,1,0:T(8,128)(2,1)}, u32[]{:S(2)}) %copy-start.14) | copy-done | bytes 851992
  14.6 2.2 %shard_map.145 = (bf16[2,32,1664]{2,1,0:T(8,128)(2,1)S(1)}, bf16[2,32,1664]{2,1,0:T(8,128)(2,1)S(1)}, bf16[2,32,1664]{2,1,0:T(8,128)(2,1)S(1)}, bf16[2,32,1664]{...) custom-call(bf16[8,32,1664]{2,1,0:T(8,128)(2,1)S(1)} %copy-done.14, ...), custom_call_target="tpu_custom_call" | custom-call | flops 1000000 | bytes 4096 | tf_op jit(solution)/shard_map/pallas_call | solution.py:297
  16.8 0.0 copy-start.1
  16.8 1.6 %collective-permute-start.1 = (bf16[2,32,1664]{2,1,0:T(8,128)(2,1)S(1)}, bf16[2,32,1664]{2,1,0:T(8,128)(2,1)S(1)}, u32[]{:S(2)}, u32[]{:S(2)}) collective-permute-start(bf16[2,32,1664]{2,1,0:T(8,128)(2,1)S(1)} %get-tuple-element.34), channel_id=1, source_target_pairs={{0,4},{2,6},{4,8},{6,10},{8,12},{10,14},{12,0},{14,2},{1,5},{3,7},... | collective-permute-start | bytes 638984 | tf_op jit(solution)/shard_map/ppermute | solution.py:300
  18.4 2.1 %collective-permute-start.2 = (bf16[2,32,1664]{2,1,0:T(8,128)(2,1)S(1)}, bf16[2,32,1664]{2,1,0:T(8,128)(2,1)S(1)}, u32[]{:S(2)}, u32[]{:S(2)}) collective-permute-start(bf16[2,32,1664]{2,1,0:T(8,128)(2,1)S(1)} %get-tuple-element.35), channel_id=1, source_target_pairs={{0,12},{2,14},{4,0},{6,2},{8,4},{10,6},{12,8},{14,10},{1,13},{3,15... | collective-permute-start | bytes 638984 | tf_op jit(solution)/shard_map/ppermute | solution.py:300
  20.6 1.3 %collective-permute-start.3 = (bf16[2,32,1664]{2,1,0:T(8,128)(2,1)}, bf16[2,32,1664]{2,1,0:T(8,128)(2,1)}, u32[]{:S(2)}, u32[]{:S(2)}) collective-permute-start(bf16[2,32,1664]{2,1,0:T(8,128)(2,1)} %get-tuple-element.36), channel_id=1, source_target_pairs={{0,8},{2,10},{4,12},{6,14},{8,0},{10,2},{12,4},{14,6},{1,9},{3,11}... | collective-permute-start | bytes 638984 | tf_op jit(solution)/shard_map/ppermute | solution.py:300
  21.9 2.5 %collective-permute-start.4 = (bf16[2,32,1664]{2,1,0:T(8,128)(2,1)}, bf16[2,32,1664]{2,1,0:T(8,128)(2,1)}, u32[]{:S(2)}, u32[]{:S(2)}) collective-permute-start(bf16[2,32,1664]{2,1,0:T(8,128)(2,1)} %get-tuple-element.37), channel_id=1, source_target_pairs={{0,2},{2,0},{4,6},{6,4},{8,10},{10,8},{12,14},{14,12},{1,3},{3,1},... | collective-permute-start | bytes 638984 | tf_op jit(solution)/shard_map/ppermute | solution.py:300
  24.3 1.0 collective-permute-start.5
  25.3 0.6 collective-permute-done.1.refs_1_
  25.9 0.0 copy-start.2
  25.9 3.5 %collective-permute-start.6 = (bf16[2,32,1664]{2,1,0:T(8,128)(2,1)}, bf16[2,32,1664]{2,1,0:T(8,128)(2,1)}, u32[]{:S(2)}, u32[]{:S(2)}) collective-permute-start(bf16[2,32,1664]{2,1,0:T(8,128)(2,1)} %get-tuple-element.39), channel_id=1, source_target_pairs={{0,14},{2,12},{4,2},{6,0},{8,6},{10,4},{12,10},{14,8},{1,15},{3,13... | collective-permute-start | bytes 638984 | tf_op jit(solution)/shard_map/ppermute | solution.py:300
  29.4 0.0 collective-permute-done.2.refs_2_
  29.4 0.9 collective-permute-start.7
  30.3 0.0 all-to-all-done.arrived
  30.3 0.2 shard_map.144
  30.4 22.9 %all_to_all.15 = f32[128,1,128]{2,1,0:T(1,128)S(1)} all-to-all(f32[128,1,128]{2,1,0:T(1,128)S(1)} %bitcast.13), channel_id=1, replica_groups=mesh['gx_0'=2,'gx_1'=4,'gy_0'=4,'gy_1'=2,'gy_2'=2] {'gx_0','gx_1','gy_0'..., dimensions={0} | all-to-all | bytes 131072 | tf_op jit(solution)/shard_map/all_to_all | solution.py:305
  53.3 0.0 collective-permute-done.3.refs_3_
  53.3 0.0 collective-permute-done.4.refs_4_
  53.3 0.0 collective-permute-done.5.refs_5_
  53.3 0.0 collective-permute-done.6.refs_6_
  53.3 0.0 collective-permute-done.7.refs_7_
  53.4 0.0 copy-done
  53.4 4.7 %shard_map.147 = bf16[16,32,1152]{2,1,0:T(8,128)(2,1)} custom-call(f32[128,128]{1,0:T(8,128)S(1)} %bitcast.8, f32[256,256]{1,0:T(8,128)S(1)} %get-tuple-element.44.attn, bf16[2,32,1664]{2,1,0:T(8,128)(2,1)S(1)} %get-tuple-element.33.refs_0_, bf16[2,32,1664]{2,1,0:T(8,128)(2,1)S(1)} %collective-permute-done.1.refs_1_, ...), custom_call_target="tpu_custom_call" | custom-call | flops 8000000 | bytes 4096 | tf_op jit(solution)/shard_map/pallas_call | solution.py:316
  58.1 0.0 copy-start.4
  58.1 0.7 copy-done.4
  58.8 4.4 %all-to-all-start.2 = ((bf16[16,32,1152]{2,1,0:T(8,128)(2,1)}), bf16[16,32,1152]{2,1,0:T(8,128)(2,1)S(1)}, u32[]{:S(2)}, u32[]{:S(2)}) async-start(bf16[16,32,1152]{2,1,0:T(8,128)(2,1)} %shard_map.147), calls=%async_computation.2 | async-start | bytes 2359296 | tf_op jit(solution)/shard_map/all_to_all | solution.py:329
  63.2 0.0 copy-done.1
  63.2 0.0 copy-done.2
  63.2 0.0 copy-done.3
  63.2 0.0 copy-start.5
  63.2 0.9 copy-done.5
  64.2 1.6 %shard_map.148.own = bf16[256,256]{1,0:T(8,128)(2,1)S(1)} custom-call(f32[128,128]{1,0:T(8,128)S(1)} %bitcast.9, f32[256,256]{1,0:T(8,128)S(1)} %copy-done.5, bf16[2,32,1664]{2,1,0:T(8,128)(2,1)S(1)} %get-tuple-element.33.refs_0_, bf16[2,32,1664]{2,1,0:T(8,128)(2,1)S(1)} %collective-permute-done.1.refs_1_, ...), custom_call_target="tpu_custom_call" | custom-call | flops 2000000 | bytes 4096 | tf_op jit(solution)/shard_map/pallas_call | solution.py:312
  65.8 0.6 collective-permute-start.8
  66.4 14.0 %collective-permute-done.8.other = bf16[256,256]{1,0:T(8,128)(2,1)S(1)} collective-permute-done((bf16[256,256]{1,0:T(8,128)(2,1)S(1)}, bf16[256,256]{1,0:T(8,128)(2,1)S(1)}, u32[]{:S(2)}, u32[]{:S(2)}) %collective-permute-start.8) | collective-permute-done | bytes 131104 | tf_op jit(solution)/shard_map/ppermute | solution.py:315
  80.4 0.0 copy-start.7
  80.4 0.0 copy-start.9
  80.4 0.0 copy-start.11
  80.4 1.1 %collective-permute-start.11 = (bf16[2,256,256]{2,1,0:T(8,128)(2,1)S(1)}, bf16[2,256,256]{2,1,0:T(8,128)(2,1)S(1)}, u32[]{:S(2)}, u32[]{:S(2)}) collective-permute-start(bf16[2,256,256]{2,1,0:T(8,128)(2,1)S(1)} %shard_map.149.refs_0_), channel_id=1, source_target_pairs={{0,32},{16,48},{32,0},{48,16},{1,33},{17,49},{33,1},{49,17},{2,34}... | collective-permute-start | bytes 786440 | tf_op jit(solution)/shard_map/ppermute | solution.py:334
  81.5 1.8 %collective-permute-start.10 = (bf16[2,256,256]{2,1,0:T(8,128)(2,1)S(1)}, bf16[2,256,256]{2,1,0:T(8,128)(2,1)S(1)}, u32[]{:S(2)}, u32[]{:S(2)}) collective-permute-start(bf16[2,256,256]{2,1,0:T(8,128)(2,1)S(1)} %shard_map.149.refs_0_), channel_id=1, source_target_pairs={{0,48},{16,0},{32,16},{48,32},{1,49},{17,1},{33,17},{49,33},{2,50}... | collective-permute-start | bytes 786440 | tf_op jit(solution)/shard_map/ppermute | solution.py:334
  83.3 0.0 collective-permute-start.9
  83.3 5.9 %shard_map.146 = (f32[32,14336]{1,0:T(8,128)}, f32[32,14336]{1,0:T(8,128)}, f32[32,14336]{1,0:T(8,128)}) custom-call(f32[128,128]{1,0:T(8,128)S(1)} %bitcast.10, bf16[2,32,1664]{2,1,0:T(8,128)(2,1)} %copy-done.1, bf16[2,32,1664]{2,1,0:T(8,128)(2,1)} %copy-done.2, bf16[2,32,1664]{2,1,0:T(8,128)(2,1)} %copy-done.3, ...), custom_call_target="tpu_custom_call" | custom-call | flops 8000000 | bytes 4096 | tf_op jit(solution)/shard_map/pallas_call | solution.py:336
  89.2 0.0 collective-permute-done.11.refs_3_
  89.3 3.9 %collective-permute-done.10.refs_2_ = bf16[2,256,256]{2,1,0:T(8,128)(2,1)S(1)} collective-permute-done((bf16[2,256,256]{2,1,0:T(8,128)(2,1)S(1)}, bf16[2,256,256]{2,1,0:T(8,128)(2,1)S(1)}, u32[]{:S(2)}, u32[]{:S(2)}) %collective-permute-start.10) | collective-permute-done | bytes 262176 | tf_op jit(solution)/shard_map/ppermute | solution.py:334
  93.1 2.7 %collective-permute-done.9.refs_1_ = bf16[2,256,256]{2,1,0:T(8,128)(2,1)S(1)} collective-permute-done((bf16[2,256,256]{2,1,0:T(8,128)(2,1)S(1)}, bf16[2,256,256]{2,1,0:T(8,128)(2,1)S(1)}, u32[]{:S(2)}, u32[]{:S(2)}) %collective-permute-start.9) | collective-permute-done | bytes 262176 | tf_op jit(solution)/shard_map/ppermute | solution.py:334
  95.8 0.0 all-to-all-done.2.arrived
  95.8 0.0 copy-done.7
  95.8 0.0 copy-done.9
  95.8 0.0 copy-done.11
  95.8 1.7 %shard_map.150 = (bf16[16,32,896]{2,1,0:T(8,128)(2,1)}, bf16[8,256,256]{2,1,0:T(8,128)(2,1)}, f32[16,4096]{1,0:T(8,128)}, f32[16,4096]{1,0:T(8,128)}, f32[16,4096]{1,0:T(8,128)}) custom-call(f32[128,128]{1,0:T(8,128)S(1)} %bitcast.11, bf16[16,32,1152]{2,1,0:T(8,128)(2,1)S(1)} %all-to-all-done.2.arrived, bf16[2,256,256]{2,1,0:T(8,128)(2,1)S(1)} %shard_map.149.refs_0_, ...), custom_call_target="tpu_custom_call" | custom-call | flops 2000000 | bytes 4096 | tf_op jit(solution)/shard_map/pallas_call | solution.py:351
  (3 shorter events, 0.0 us)
Async XLA Ops:
  0.6 1.0 copy-start.6
  1.6 0.9 copy-start.8
  2.5 0.9 copy-start.10
  3.5 1.2 %copy-start.12 = (bf16[1,512,896]{2,1,0:T(8,128)(2,1)S(1)}, bf16[1,512,896]{2,1,0:T(8,128)(2,1)}, u32[]{:S(2)}) copy-start(bf16[1,512,896]{2,1,0:T(8,128)(2,1)} %param.8) | copy-start | bytes 2752516
  5.8 0.9 copy-start.13
  6.7 6.6 %collective-permute-start = (bf16[8,32,1664]{2,1,0:T(8,128)(2,1)}, bf16[8,32,1664]{2,1,0:T(8,128)(2,1)}, u32[]{:S(2)}, u32[]{:S(2)}) collective-permute-start(bf16[8,32,1664]{2,1,0:T(8,128)(2,1)} %get-tuple-element.32), channel_id=1, source_target_pairs={{0,1},{1,0},{2,3},{3,2},{4,5},{5,4},{6,7},{7,6},{8,9},{9,8},{10,11... | collective-permute-start | bytes 2555912 | tf_op jit(solution)/shard_map/ppermute | solution.py:296
  8.1 22.2 %all-to-all-start = ((bf16[8,256,256]{2,1,0:T(8,128)(2,1)}), bf16[8,256,256]{2,1,0:T(8,128)(2,1)S(1)}, u32[]{:S(2)}, u32[]{:S(2)}) async-start(bf16[8,256,256]{2,1,0:T(8,128)(2,1)} %bitcast.14), calls=%async_computation | async-start | bytes 2097152 | tf_op jit(solution)/shard_map/all_to_all | solution.py:287
  13.3 40.1 %copy-start = (f32[32,14336]{1,0:T(8,128)S(1)}, f32[32,14336]{1,0:T(8,128)}, u32[]{:S(2)}) copy-start(f32[32,14336]{1,0:T(8,128)} %refs_8_.3) | copy-start | bytes 5505028
  13.3 1.3 %copy-start.14 = (bf16[8,32,1664]{2,1,0:T(8,128)(2,1)S(1)}, bf16[8,32,1664]{2,1,0:T(8,128)(2,1)}, u32[]{:S(2)}) copy-start(bf16[8,32,1664]{2,1,0:T(8,128)(2,1)} %copy-done.13) | copy-start | bytes 2555908
  16.8 46.4 %copy-start.1 = (bf16[2,32,1664]{2,1,0:T(8,128)(2,1)}, bf16[2,32,1664]{2,1,0:T(8,128)(2,1)S(1)}, u32[]{:S(2)}) copy-start(bf16[2,32,1664]{2,1,0:T(8,128)(2,1)S(1)} %get-tuple-element.33.refs_0_) | copy-start | bytes 638980
  16.8 9.1 %collective-permute-start.1 = (bf16[2,32,1664]{2,1,0:T(8,128)(2,1)S(1)}, bf16[2,32,1664]{2,1,0:T(8,128)(2,1)S(1)}, u32[]{:S(2)}, u32[]{:S(2)}) collective-permute-start(bf16[2,32,1664]{2,1,0:T(8,128)(2,1)S(1)} %get-tuple-element.34), channel_id=1, source_target_pairs={{0,4},{2,6},{4,8},{6,10},{8,12},{10,14},{12,0},{14,2},{1,5},{3,7},... | collective-permute-start | bytes 638984 | tf_op jit(solution)/shard_map/ppermute | solution.py:300
  18.4 11.0 %collective-permute-start.2 = (bf16[2,32,1664]{2,1,0:T(8,128)(2,1)S(1)}, bf16[2,32,1664]{2,1,0:T(8,128)(2,1)S(1)}, u32[]{:S(2)}, u32[]{:S(2)}) collective-permute-start(bf16[2,32,1664]{2,1,0:T(8,128)(2,1)S(1)} %get-tuple-element.35), channel_id=1, source_target_pairs={{0,12},{2,14},{4,0},{6,2},{8,4},{10,6},{12,8},{14,10},{1,13},{3,15... | collective-permute-start | bytes 638984 | tf_op jit(solution)/shard_map/ppermute | solution.py:300
  20.6 32.7 %collective-permute-start.3 = (bf16[2,32,1664]{2,1,0:T(8,128)(2,1)}, bf16[2,32,1664]{2,1,0:T(8,128)(2,1)}, u32[]{:S(2)}, u32[]{:S(2)}) collective-permute-start(bf16[2,32,1664]{2,1,0:T(8,128)(2,1)} %get-tuple-element.36), channel_id=1, source_target_pairs={{0,8},{2,10},{4,12},{6,14},{8,0},{10,2},{12,4},{14,6},{1,9},{3,11}... | collective-permute-start | bytes 638984 | tf_op jit(solution)/shard_map/ppermute | solution.py:300
  21.9 31.5 %collective-permute-start.4 = (bf16[2,32,1664]{2,1,0:T(8,128)(2,1)}, bf16[2,32,1664]{2,1,0:T(8,128)(2,1)}, u32[]{:S(2)}, u32[]{:S(2)}) collective-permute-start(bf16[2,32,1664]{2,1,0:T(8,128)(2,1)} %get-tuple-element.37), channel_id=1, source_target_pairs={{0,2},{2,0},{4,6},{6,4},{8,10},{10,8},{12,14},{14,12},{1,3},{3,1},... | collective-permute-start | bytes 638984 | tf_op jit(solution)/shard_map/ppermute | solution.py:300
  24.3 29.0 %collective-permute-start.5 = (bf16[2,32,1664]{2,1,0:T(8,128)(2,1)}, bf16[2,32,1664]{2,1,0:T(8,128)(2,1)}, u32[]{:S(2)}, u32[]{:S(2)}) collective-permute-start(bf16[2,32,1664]{2,1,0:T(8,128)(2,1)} %get-tuple-element.38), channel_id=1, source_target_pairs={{0,6},{2,4},{4,10},{6,8},{8,14},{10,12},{12,2},{14,0},{1,7},{3,5},... | collective-permute-start | bytes 638984 | tf_op jit(solution)/shard_map/ppermute | solution.py:300
  25.9 37.3 %copy-start.2 = (bf16[2,32,1664]{2,1,0:T(8,128)(2,1)}, bf16[2,32,1664]{2,1,0:T(8,128)(2,1)S(1)}, u32[]{:S(2)}) copy-start(bf16[2,32,1664]{2,1,0:T(8,128)(2,1)S(1)} %collective-permute-done.1.refs_1_) | copy-start | bytes 638980
  25.9 27.4 %collective-permute-start.6 = (bf16[2,32,1664]{2,1,0:T(8,128)(2,1)}, bf16[2,32,1664]{2,1,0:T(8,128)(2,1)}, u32[]{:S(2)}, u32[]{:S(2)}) collective-permute-start(bf16[2,32,1664]{2,1,0:T(8,128)(2,1)} %get-tuple-element.39), channel_id=1, source_target_pairs={{0,14},{2,12},{4,2},{6,0},{8,6},{10,4},{12,10},{14,8},{1,15},{3,13... | collective-permute-start | bytes 638984 | tf_op jit(solution)/shard_map/ppermute | solution.py:300
  29.4 33.8 %copy-start.3 = (bf16[2,32,1664]{2,1,0:T(8,128)(2,1)}, bf16[2,32,1664]{2,1,0:T(8,128)(2,1)S(1)}, u32[]{:S(2)}) copy-start(bf16[2,32,1664]{2,1,0:T(8,128)(2,1)S(1)} %collective-permute-done.2.refs_2_) | copy-start | bytes 638980
  29.4 23.9 %collective-permute-start.7 = (bf16[2,32,1664]{2,1,0:T(8,128)(2,1)}, bf16[2,32,1664]{2,1,0:T(8,128)(2,1)}, u32[]{:S(2)}, u32[]{:S(2)}) collective-permute-start(bf16[2,32,1664]{2,1,0:T(8,128)(2,1)} %get-tuple-element.40), channel_id=1, source_target_pairs={{0,10},{2,8},{4,14},{6,12},{8,2},{10,0},{12,6},{14,4},{1,11},{3,9}... | collective-permute-start | bytes 638984 | tf_op jit(solution)/shard_map/ppermute | solution.py:300
  58.1 0.7 copy-start.4
  58.8 37.0 %all-to-all-start.2 = ((bf16[16,32,1152]{2,1,0:T(8,128)(2,1)}), bf16[16,32,1152]{2,1,0:T(8,128)(2,1)S(1)}, u32[]{:S(2)}, u32[]{:S(2)}) async-start(bf16[16,32,1152]{2,1,0:T(8,128)(2,1)} %shard_map.147), calls=%async_computation.2 | async-start | bytes 2359296 | tf_op jit(solution)/shard_map/all_to_all | solution.py:329
  63.2 1.0 copy-start.5
  65.8 14.5 %collective-permute-start.8 = (bf16[256,256]{1,0:T(8,128)(2,1)S(1)}, bf16[256,256]{1,0:T(8,128)(2,1)S(1)}, u32[]{:S(2)}, u32[]{:S(2)}) collective-permute-start(bf16[256,256]{1,0:T(8,128)(2,1)S(1)} %shard_map.148.own), channel_id=1, source_target_pairs={{0,64},{64,0},{1,65},{65,1},{2,66},{66,2},{3,67},{67,3},{4,68},{68... | collective-permute-start | bytes 393224 | tf_op jit(solution)/shard_map/ppermute | solution.py:315
  80.4 15.5 %copy-start.7 = (f32[16,4096]{1,0:T(8,128)S(1)}, f32[16,4096]{1,0:T(8,128)}, u32[]{:S(2)}) copy-start(f32[16,4096]{1,0:T(8,128)} %refs_4_.1) | copy-start | bytes 786436
  80.4 15.5 %copy-start.9 = (f32[16,4096]{1,0:T(8,128)S(1)}, f32[16,4096]{1,0:T(8,128)}, u32[]{:S(2)}) copy-start(f32[16,4096]{1,0:T(8,128)} %refs_5_.1) | copy-start | bytes 786436
  80.4 15.5 %copy-start.11 = (f32[16,4096]{1,0:T(8,128)S(1)}, f32[16,4096]{1,0:T(8,128)}, u32[]{:S(2)}) copy-start(f32[16,4096]{1,0:T(8,128)} %refs_6_.1) | copy-start | bytes 786436
  80.4 8.9 %collective-permute-start.11 = (bf16[2,256,256]{2,1,0:T(8,128)(2,1)S(1)}, bf16[2,256,256]{2,1,0:T(8,128)(2,1)S(1)}, u32[]{:S(2)}, u32[]{:S(2)}) collective-permute-start(bf16[2,256,256]{2,1,0:T(8,128)(2,1)S(1)} %shard_map.149.refs_0_), channel_id=1, source_target_pairs={{0,32},{16,48},{32,0},{48,16},{1,33},{17,49},{33,1},{49,17},{2,34}... | collective-permute-start | bytes 786440 | tf_op jit(solution)/shard_map/ppermute | solution.py:334
  81.5 11.6 %collective-permute-start.10 = (bf16[2,256,256]{2,1,0:T(8,128)(2,1)S(1)}, bf16[2,256,256]{2,1,0:T(8,128)(2,1)S(1)}, u32[]{:S(2)}, u32[]{:S(2)}) collective-permute-start(bf16[2,256,256]{2,1,0:T(8,128)(2,1)S(1)} %shard_map.149.refs_0_), channel_id=1, source_target_pairs={{0,48},{16,0},{32,16},{48,32},{1,49},{17,1},{33,17},{49,33},{2,50}... | collective-permute-start | bytes 786440 | tf_op jit(solution)/shard_map/ppermute | solution.py:334
  83.3 12.5 %collective-permute-start.9 = (bf16[2,256,256]{2,1,0:T(8,128)(2,1)S(1)}, bf16[2,256,256]{2,1,0:T(8,128)(2,1)S(1)}, u32[]{:S(2)}, u32[]{:S(2)}) collective-permute-start(bf16[2,256,256]{2,1,0:T(8,128)(2,1)S(1)} %shard_map.149.refs_0_), channel_id=1, source_target_pairs={{0,16},{16,32},{32,48},{48,0},{1,17},{17,33},{33,49},{49,1},{2,18}... | collective-permute-start | bytes 786440 | tf_op jit(solution)/shard_map/ppermute | solution.py:334

commit v5 on v4

--- a/solution.py
+++ b/solution.py
@@ -60,14 +60,21 @@
 
 
 def adam_update(gradient, master, moment, second, clip_factor):
-    scaled = clip_factor * gradient
-    moment_new = beta_one * moment + (1.0 - beta_one) * scaled
-    second_new = beta_two * second + (1.0 - beta_two) * scaled * scaled
+    moment_new = beta_one * moment + ((1.0 - beta_one) * clip_factor) * gradient
+    second_new = beta_two * second + ((1.0 - beta_two) * clip_factor * clip_factor) * (gradient * gradient)
     mean_square = second_new * (1.0 / bias_two)
     root = mean_square * lax.rsqrt(mean_square)
-    update = moment_new * (1.0 / bias_one) / (root + adam_eps)
-    master_new = master - learn_rate * (update + weight_decay * master)
-    return (master_new, moment_new, second_new)
+    step = moment_new * (learn_rate / bias_one) / (root + adam_eps)
+    return (master * (1.0 - learn_rate * weight_decay) - step, moment_new, second_new)
+
+
+def adam_weight(gradient, master, moment, second, clip_factor):
+    gain = ((1.0 - beta_two) / bias_two) * clip_factor * clip_factor
+    mean_square = (beta_two / bias_two) * second + gain * (gradient * gradient)
+    root = mean_square * lax.rsqrt(mean_square)
+    scale = learn_rate / bias_one
+    step = (scale * beta_one) * moment + (scale * (1.0 - beta_one) * clip_factor) * gradient
+    return master * (1.0 - learn_rate * weight_decay) - step / (root + adam_eps)
 
 
 def clip_of(sums_ref):
@@ -133,7 +140,7 @@
 
 
 def expert_weight_kernel(sums, attn, *refs):
-    blocks, master, streams, out = refs[:8], refs[8], refs[9:11], refs[11]
+    blocks, streams, out = refs[:8], refs[8:11], refs[11]
     held, weights, sems, out_sems = refs[12:]
     loads = []
     for n, chip in enumerate(sources()):
@@ -157,12 +164,11 @@
             copy.wait()
         for at in range(14):
             core, col = divmod(at, 7)
-            here = pl.ds(pl.multiple_of((chip * 14 + at) * 128, 128), 128)
-            new, _, _ = adam_update(
+            new = adam_weight(
                 block[core, :, lanes(col)].astype(f32),
-                master[:, here],
                 held[0, n, :, lanes(at)],
                 held[1, n, :, lanes(at)],
+                held[2, n, :, lanes(at)],
                 clip,
             )
             weights[n, core, :, lanes(col)] = new.astype(bf16)
@@ -219,7 +225,7 @@
         for core in range(2):
             rows = pl.ds(pl.multiple_of((chip * 2 + core) * AROWS, AROWS), AROWS)
             state = block[core, :AROWS, COLS:].astype(f32) + block[core, AROWS:, COLS:].astype(f32)
-            new, _, _ = adam_update(
+            new = adam_weight(
                 attn[rows, :],
                 state[:, :ACOLS],
                 state[:, ACOLS : 2 * ACOLS],
@@ -235,19 +241,23 @@
     out[1 - x] = other[...]
 
 
-def finish_kernel(sums, arrived, *refs):
-    pieces, state, weight, attn_weight = refs[:4], refs[4:7], refs[7], refs[8]
-    outs, news, sems, out_sems = refs[9:12], refs[12], refs[13], refs[14]
+def join_kernel(*refs):
+    pieces, out, sems = refs[:4], refs[4], refs[5]
     y = lax.axis_index("gx_1")
-    stores = [pltpu.make_async_copy(arrived.at[:, :, :COLS], weight, sems.at[8])]
+    stores = []
     for n, (dy, piece) in enumerate(zip((0,) + REPLICA_STEPS, pieces)):
         for x in range(2):
             slot = x * 4 + lax.rem(y + 4 - dy, 4)
-            stores.append(
-                pltpu.make_async_copy(piece.at[x], attn_weight.at[slot], sems.at[2 * n + x])
-            )
+            stores.append(pltpu.make_async_copy(piece.at[x], out.at[slot], sems.at[n, x]))
+            stores[-1].start()
     for store in stores:
-        store.start()
+        store.wait()
+
+
+def finish_kernel(sums, arrived, *refs):
+    state, weight, outs, news, sem, out_sems = refs[:3], refs[3], refs[4:7], refs[7], refs[8], refs[9]
+    stores = [pltpu.make_async_copy(arrived.at[:, :, :COLS], weight, sem)]
+    stores[0].start()
     clip = clip_of(sums)
     for part in range(4):
         for group in range(4 * part, 4 * part + 4):
@@ -317,15 +327,15 @@
         expert_weight_kernel,
         pltpu.HBM((16, ROWS, BACK), bf16),
         8000000,
-        in_specs=[vmem] * 11 + [hbm] * 2,
+        in_specs=[vmem] * 10 + [hbm] * 3,
         out_specs=hbm,
         scratch_shapes=[
-            pltpu.VMEM((2, 8, ROWS, 2 * COLS), f32),
+            pltpu.VMEM((3, 8, ROWS, 2 * COLS), f32),
             pltpu.VMEM((8, 2, ROWS, BACK), bf16),
-            pltpu.SemaphoreType.DMA((8, 2)),
+            pltpu.SemaphoreType.DMA((8, 3)),
             pltpu.SemaphoreType.DMA((8,)),
         ],
-    )(*near(sums, attn_sum, *blocks, expert_master), *far(expert_moment, expert_second))
+    )(*near(sums, attn_sum, *blocks), *state)
     returned = lax.all_to_all(weights, GY, split_axis=0, concat_axis=0, tiled=True)
     both = call(both_kernel, pltpu.VMEM((2, 256, ACOLS), bf16), 1000000)(*near(attn_block, other))
     pieces = [both]
@@ -338,7 +348,7 @@
         (pltpu.HBM((ROWS, 16 * COLS), f32),) * 3,
         8000000,
         mib=16,
-        in_specs=[vmem] + [hbm] * 11,
+        in_specs=[vmem] + [pl.BlockSpec(memory_space=pl.ANY)] * 8 + [hbm] * 3,
         out_specs=[hbm] * 3,
         scratch_shapes=[
             pltpu.VMEM((3, 8, ROWS, 2 * COLS), f32),
@@ -347,20 +357,27 @@
             pltpu.SemaphoreType.DMA((8, 4)),
             pltpu.SemaphoreType.DMA((8, 3)),
         ],
-    )(sums, *far(*blocks), *state)
-    expert_weight, attn_weight, a_master, a_moment, a_second = call(
+    )(sums, *blocks, *state)
+    attn_weight = call(
+        join_kernel,
+        pltpu.HBM((8, 256, ACOLS), bf16),
+        1000000,
+        in_specs=[vmem] * 4,
+        out_specs=hbm,
+        scratch_shapes=[pltpu.SemaphoreType.DMA((4, 2))],
+    )(*near(*pieces))
+    expert_weight, a_master, a_moment, a_second = call(
         finish_kernel,
-        (pltpu.HBM((16, ROWS, COLS), bf16), pltpu.HBM((8, 256, ACOLS), bf16))
-        + (pltpu.HBM((AROWS, 16 * ACOLS), f32),) * 3,
+        (pltpu.HBM((16, ROWS, COLS), bf16),) + (pltpu.HBM((AROWS, 16 * ACOLS), f32),) * 3,
         2000000,
-        in_specs=[vmem] * 9,
-        out_specs=[hbm] * 5,
+        in_specs=[vmem] * 5,
+        out_specs=[hbm] * 4,
         scratch_shapes=[
             pltpu.VMEM((3, AROWS, 16 * ACOLS), f32),
-            pltpu.SemaphoreType.DMA((9,)),
+            pltpu.SemaphoreType.DMA,
             pltpu.SemaphoreType.DMA((4, 3)),
         ],
-    )(*near(sums, returned, *pieces), attn_master, attn_moment, attn_second)
+    )(*near(sums, returned), attn_master, attn_moment, attn_second)
     return (
         e_master,
         e_moment,

time: 98.1 us -> 96.4 us (0.983)
  local copies, waits for them, and re-layouts: 7.88 us -> 4.04 us
  waiting for transfers between devices: 21.2 us -> 24.6 us
  Pallas kernels: 17.5 us -> 14.3 us
  blocking collectives: 22.9 us -> 25 us
    unnamed x30 -> x14, local copies, waits for them, and re-layouts: 7.88 us -> 4.04 us
    ppermute x1, waiting for transfers between devices: 14 us -> 16.3 us  [local(): other = lax.ppermute(attn_block, 'gx_0', [(0, 1), (1, 0)])]
    all_to_all x1, blocking collectives: 22.9 us -> 25 us  [local(): lax.all_to_all(partial.reshape(128, 1, 128), GX_GY, split_axis=0, concat_...]
    pallas_call x1, Pallas kernels: 1.63 us -> 0.27 us  [local(): call(attn_weight_kernel, pltpu.VMEM((256, ACOLS), bf16), 2000000)]
    pallas_call x1, Pallas kernels: 2.22 us -> 1 us  [local(): call(route_kernel, (shape((2, ROWS, WIDE), bf16),) * 8, 1000000)]
    pallas_call x1 -> x2, Pallas kernels: 1.71 us -> 2.47 us  [the longest x1 1.45 us: local(): call(finish_kernel, (pltpu.HBM((16, ROWS, COLS), bf16),) + (pltpu.HBM((AR...]
  transfers between devices with their start and end apart: 14 -> 14, of which waited for: 4 -> 6; matrix products, arithmetic and copies ran while one was open for 0% -> 0% of each run, Pallas kernels for 10% -> 8%
where the time goes in v5:
time: 96.4 us; the launch traced here: 96 us
  starting transfers between devices  27.2 us (28%)
  blocking collectives  25 us (26%)
  waiting for transfers between devices  24.6 us (26%)
  Pallas kernels  14.3 us (15%)
  local copies, waits for them, and re-layouts  4.04 us (4%)
    all_to_all x1, blocking collectives, local(): lax.all_to_all(partial.reshape(128, 1, 128), GX_GY, split_axis=0, concat_...  25 us
    ppermute x1, waiting for transfers between devices, local(): other = lax.ppermute(attn_block, 'gx_0', [(0, 1), (1, 0)])  16.3 us
    ppermute x7, starting transfers between devices, local(): blocks.append(lax.ppermute(routed[n + 1], GY[:2], chip_pairs(*step)))  12.7 us
    ppermute x3, waiting for transfers between devices, local(): lax.ppermute(both, 'gx_1', [(y, (y + REPLICA_STEPS[n]) % 4) for y in rang...  7.11 us
    pallas_call x1, Pallas kernels, local(): call(expert_state_kernel, (pltpu.HBM((ROWS, 16 * COLS), f32),) * 3, 80000...  5.31 us
    all_to_all x1, starting transfers between devices, local(): lax.all_to_all(attn_grad.reshape(8, 256, ACOLS), GX, split_axis=0, concat...  5.23 us
    all_to_all x1, starting transfers between devices, local(): lax.all_to_all(weights, GY, split_axis=0, concat_axis=0, tiled=True)  4.37 us
    unnamed x14, local copies, waits for them, and re-layouts  4.04 us
  transfers between devices with their start and end apart: 14, of which 6 were waited for; matrix products, arithmetic and copies ran while one was open for 0% of the time, Pallas kernels for 8%

profile of v5, /device:TPU:1, one launch (start us, length us, event | category | flops | bytes accessed | tf_op | source)
XLA Modules:
  0.0 96.0 jit_solution(9884909229652027198)
XLA Ops:
  0.6 0.0 copy-start
  0.6 0.9 copy-done
  1.6 0.0 copy-start.2
  1.6 0.9 copy-done.2
  2.5 0.0 copy-start.4
  2.5 0.9 copy-done.4
  3.5 0.0 copy-start.6
  3.5 1.2 %copy-done.6 = bf16[1,512,896]{2,1,0:T(8,128)(2,1)S(1)} copy-done((bf16[1,512,896]{2,1,0:T(8,128)(2,1)S(1)}, bf16[1,512,896]{2,1,0:T(8,128)(2,1)}, u32[]{:S(2)}) %copy-start.6) | copy-done | bytes 917528
  4.7 1.1 %shard_map.143 = (bf16[8,32,1664]{2,1,0:T(8,128)(2,1)S(1)}, bf16[8,32,1664]{2,1,0:T(8,128)(2,1)}, f32[1,128]{1,0:T(1,128)S(1)}) custom-call(bf16[16,32,896]{2,1,0:T(8,128)(2,1)S(1)} %bitcast.12, f32[16,4096]{1,0:T(8,128)S(1)} %copy-done, f32[16,4096]{1,0:T(8,128)S(1)} %copy-done.2, f32[16,4096]{1,0:T(8,128)S(1)} %copy-done.4), custom_call_target="tpu_custom_call" | custom-call | flops 4000000 | bytes 4096 | tf_op jit(solution)/shard_map/pallas_call | solution.py:301
  5.8 1.4 %collective-permute-start = (bf16[8,32,1664]{2,1,0:T(8,128)(2,1)}, bf16[8,32,1664]{2,1,0:T(8,128)(2,1)S(1)}, u32[]{:S(2)}, u32[]{:S(2)}) collective-permute-start(bf16[8,32,1664]{2,1,0:T(8,128)(2,1)} %get-tuple-element.31), channel_id=1, source_target_pairs={{0,1},{1,0},{2,3},{3,2},{4,5},{5,4},{6,7},{7,6},{8,9},{9,8},{10,11... | collective-permute-start | bytes 2555912 | tf_op jit(solution)/shard_map/ppermute | solution.py:306
  7.2 5.2 %all-to-all-start = ((bf16[8,256,256]{2,1,0:T(8,128)(2,1)}), bf16[8,256,256]{2,1,0:T(8,128)(2,1)S(1)}, u32[]{:S(2)}, u32[]{:S(2)}) async-start(bf16[8,256,256]{2,1,0:T(8,128)(2,1)} %bitcast.14), calls=%async_computation | async-start | bytes 2097152 | tf_op jit(solution)/shard_map/all_to_all | solution.py:297
  12.4 0.0 collective-permute-done.swapped
  12.4 1.0 %shard_map.145 = (bf16[2,32,1664]{2,1,0:T(8,128)(2,1)S(1)}, bf16[2,32,1664]{2,1,0:T(8,128)(2,1)S(1)}, bf16[2,32,1664]{2,1,0:T(8,128)(2,1)S(1)}, bf16[2,32,1664]{...) custom-call(bf16[8,32,1664]{2,1,0:T(8,128)(2,1)S(1)} %get-tuple-elem, ...), custom_call_target="tpu_custom_call" | custom-call | flops 1000000 | bytes 4096 | tf_op jit(solution)/shard_map/pallas_call | solution.py:307
  13.4 1.6 %collective-permute-start.1 = (bf16[2,32,1664]{2,1,0:T(8,128)(2,1)S(1)}, bf16[2,32,1664]{2,1,0:T(8,128)(2,1)S(1)}, u32[]{:S(2)}, u32[]{:S(2)}) collective-permute-start(bf16[2,32,1664]{2,1,0:T(8,128)(2,1)S(1)} %get-tuple-element.33), channel_id=1, source_target_pairs={{0,4},{2,6},{4,8},{6,10},{8,12},{10,14},{12,0},{14,2},{1,5},{3,7},... | collective-permute-start | bytes 638984 | tf_op jit(solution)/shard_map/ppermute | solution.py:310
  15.0 2.1 %collective-permute-start.2 = (bf16[2,32,1664]{2,1,0:T(8,128)(2,1)S(1)}, bf16[2,32,1664]{2,1,0:T(8,128)(2,1)S(1)}, u32[]{:S(2)}, u32[]{:S(2)}) collective-permute-start(bf16[2,32,1664]{2,1,0:T(8,128)(2,1)S(1)} %get-tuple-element.34), channel_id=1, source_target_pairs={{0,12},{2,14},{4,0},{6,2},{8,4},{10,6},{12,8},{14,10},{1,13},{3,15... | collective-permute-start | bytes 638984 | tf_op jit(solution)/shard_map/ppermute | solution.py:310
  17.2 1.3 %collective-permute-start.3 = (bf16[2,32,1664]{2,1,0:T(8,128)(2,1)}, bf16[2,32,1664]{2,1,0:T(8,128)(2,1)S(1)}, u32[]{:S(2)}, u32[]{:S(2)}) collective-permute-start(bf16[2,32,1664]{2,1,0:T(8,128)(2,1)} %get-tuple-element.35), channel_id=1, source_target_pairs={{0,8},{2,10},{4,12},{6,14},{8,0},{10,2},{12,4},{14,6},{1,9},{3,11}... | collective-permute-start | bytes 638984 | tf_op jit(solution)/shard_map/ppermute | solution.py:310
  18.5 2.5 %collective-permute-start.4 = (bf16[2,32,1664]{2,1,0:T(8,128)(2,1)}, bf16[2,32,1664]{2,1,0:T(8,128)(2,1)S(1)}, u32[]{:S(2)}, u32[]{:S(2)}) collective-permute-start(bf16[2,32,1664]{2,1,0:T(8,128)(2,1)} %get-tuple-element.36), channel_id=1, source_target_pairs={{0,2},{2,0},{4,6},{6,4},{8,10},{10,8},{12,14},{14,12},{1,3},{3,1},... | collective-permute-start | bytes 638984 | tf_op jit(solution)/shard_map/ppermute | solution.py:310
  20.9 1.0 %collective-permute-start.5 = (bf16[2,32,1664]{2,1,0:T(8,128)(2,1)}, bf16[2,32,1664]{2,1,0:T(8,128)(2,1)S(1)}, u32[]{:S(2)}, u32[]{:S(2)}) collective-permute-start(bf16[2,32,1664]{2,1,0:T(8,128)(2,1)} %get-tuple-element.37), channel_id=1, source_target_pairs={{0,6},{2,4},{4,10},{6,8},{8,14},{10,12},{12,2},{14,0},{1,7},{3,5},... | collective-permute-start | bytes 638984 | tf_op jit(solution)/shard_map/ppermute | solution.py:310
  21.9 0.6 collective-permute-done.1.refs_1_
  22.5 3.5 %collective-permute-start.6 = (bf16[2,32,1664]{2,1,0:T(8,128)(2,1)}, bf16[2,32,1664]{2,1,0:T(8,128)(2,1)S(1)}, u32[]{:S(2)}, u32[]{:S(2)}) collective-permute-start(bf16[2,32,1664]{2,1,0:T(8,128)(2,1)} %get-tuple-element.38), channel_id=1, source_target_pairs={{0,14},{2,12},{4,2},{6,0},{8,6},{10,4},{12,10},{14,8},{1,15},{3,13... | collective-permute-start | bytes 638984 | tf_op jit(solution)/shard_map/ppermute | solution.py:310
  26.0 0.0 collective-permute-done.2.refs_2_
  26.0 0.8 collective-permute-start.7
  26.8 0.6 all-to-all-done.arrived
  27.4 0.2 shard_map.144
  27.5 25.0 %all_to_all.15 = f32[128,1,128]{2,1,0:T(1,128)S(1)} all-to-all(f32[128,1,128]{2,1,0:T(1,128)S(1)} %bitcast.13), channel_id=1, replica_groups=mesh['gx_0'=2,'gx_1'=4,'gy_0'=4,'gy_1'=2,'gy_2'=2] {'gx_0','gx_1','gy_0'..., dimensions={0} | all-to-all | bytes 131072 | tf_op jit(solution)/shard_map/all_to_all | solution.py:315
  52.5 0.0 collective-permute-done.3.refs_3_
  52.5 0.0 collective-permute-done.4.refs_4_
  52.5 0.0 collective-permute-done.5.refs_5_
  52.5 0.0 collective-permute-done.6.refs_6_
  52.5 0.0 collective-permute-done.7.refs_7_
  52.6 3.9 %shard_map.147 = bf16[16,32,1152]{2,1,0:T(8,128)(2,1)} custom-call(f32[128,128]{1,0:T(8,128)S(1)} %bitcast.8, f32[256,256]{1,0:T(8,128)S(1)} %get-tuple-element.43.attn, bf16[2,32,1664]{2,1,0:T(8,128)(2,1)S(1)} %get-tuple-element.32.refs_0_, bf16[2,32,1664]{2,1,0:T(8,128)(2,1)S(1)} %collective-permute-done.1.refs_1_, ...), custom_call_target="tpu_custom_call" | custom-call | flops 8000000 | bytes 4096 | tf_op jit(solution)/shard_map/pallas_call | solution.py:326
  56.5 4.4 %all-to-all-start.2 = ((bf16[16,32,1152]{2,1,0:T(8,128)(2,1)}), bf16[16,32,1152]{2,1,0:T(8,128)(2,1)S(1)}, u32[]{:S(2)}, u32[]{:S(2)}) async-start(bf16[16,32,1152]{2,1,0:T(8,128)(2,1)} %shard_map.147), calls=%async_computation.2 | async-start | bytes 2359296 | tf_op jit(solution)/shard_map/all_to_all | solution.py:339
  60.9 0.3 shard_map.149.own
  61.1 0.5 collective-permute-start.8
  61.7 16.3 %collective-permute-done.8.other = bf16[256,256]{1,0:T(8,128)(2,1)S(1)} collective-permute-done((bf16[256,256]{1,0:T(8,128)(2,1)S(1)}, bf16[256,256]{1,0:T(8,128)(2,1)S(1)}, u32[]{:S(2)}, u32[]{:S(2)}) %collective-permute-start.8) | collective-permute-done | bytes 131104 | tf_op jit(solution)/shard_map/ppermute | solution.py:325
  78.0 1.1 %collective-permute-start.11 = (bf16[2,256,256]{2,1,0:T(8,128)(2,1)S(1)}, bf16[2,256,256]{2,1,0:T(8,128)(2,1)S(1)}, u32[]{:S(2)}, u32[]{:S(2)}) collective-permute-start(bf16[2,256,256]{2,1,0:T(8,128)(2,1)S(1)} %shard_map.150.refs_0_), channel_id=1, source_target_pairs={{0,32},{16,48},{32,0},{48,16},{1,33},{17,49},{33,1},{49,17},{2,34}... | collective-permute-start | bytes 786440 | tf_op jit(solution)/shard_map/ppermute | solution.py:344
  79.1 1.9 %collective-permute-start.10 = (bf16[2,256,256]{2,1,0:T(8,128)(2,1)S(1)}, bf16[2,256,256]{2,1,0:T(8,128)(2,1)S(1)}, u32[]{:S(2)}, u32[]{:S(2)}) collective-permute-start(bf16[2,256,256]{2,1,0:T(8,128)(2,1)S(1)} %shard_map.150.refs_0_), channel_id=1, source_target_pairs={{0,48},{16,0},{32,16},{48,32},{1,49},{17,1},{33,17},{49,33},{2,50}... | collective-permute-start | bytes 786440 | tf_op jit(solution)/shard_map/ppermute | solution.py:344
  81.0 0.0 collective-permute-start.9
  81.0 5.3 %shard_map.146 = (f32[32,14336]{1,0:T(8,128)}, f32[32,14336]{1,0:T(8,128)}, f32[32,14336]{1,0:T(8,128)}) custom-call(f32[128,128]{1,0:T(8,128)S(1)} %bitcast.10, bf16[2,32,1664]{2,1,0:T(8,128)(2,1)S(1)} %get-tuple-element.32.refs_0_, bf16[2,32,1664]{2,1,0:T(8,128)(2,1)S(1)} %collective-permute-done.1.refs_1_, ...), custom_call_target="tpu_custom_call" | custom-call | flops 8000000 | bytes 4096 | tf_op jit(solution)/shard_map/pallas_call | solution.py:346
  86.3 0.0 copy-start.1
  86.3 0.0 copy-start.3
  86.3 0.0 copy-start.5
  86.3 0.5 collective-permute-done.11.refs_3_
  86.9 3.7 %collective-permute-done.10.refs_2_ = bf16[2,256,256]{2,1,0:T(8,128)(2,1)S(1)} collective-permute-done((bf16[2,256,256]{2,1,0:T(8,128)(2,1)S(1)}, bf16[2,256,256]{2,1,0:T(8,128)(2,1)S(1)}, u32[]{:S(2)}, u32[]{:S(2)}) %collective-permute-start.10) | collective-permute-done | bytes 262176 | tf_op jit(solution)/shard_map/ppermute | solution.py:344
  90.6 2.8 %collective-permute-done.9.refs_1_ = bf16[2,256,256]{2,1,0:T(8,128)(2,1)S(1)} collective-permute-done((bf16[2,256,256]{2,1,0:T(8,128)(2,1)S(1)}, bf16[2,256,256]{2,1,0:T(8,128)(2,1)S(1)}, u32[]{:S(2)}, u32[]{:S(2)}) %collective-permute-start.9) | collective-permute-done | bytes 262176 | tf_op jit(solution)/shard_map/ppermute | solution.py:344
  93.4 1.0 %shard_map.151 = bf16[8,256,256]{2,1,0:T(8,128)(2,1)} custom-call(bf16[2,256,256]{2,1,0:T(8,128)(2,1)S(1)} %shard_map.150.refs_0_, bf16[2,256,256]{2,1,0:T(8,128)(2,1)S(1)} %collective-permute-done.9.refs_1_, bf16[2,256,256]{2,1,0:T(8,128)(2,1)S(1)} %collective-permute-done.10.refs_2_, bf16[2,256,256]{2,1,0:T(8,128)(2,1)S(1)} %collective-permute-done.11.refs_3_), custom_call_target="tpu_custom_call" | custom-call | flops 1000000 | bytes 4096 | tf_op jit(solution)/shard_map/pallas_call | solution.py:361
  94.5 0.0 all-to-all-done.2.arrived
  94.5 0.0 copy-done.1
  94.5 0.0 copy-done.3
  94.5 0.0 copy-done.5
  94.5 1.4 %shard_map.148 = (bf16[16,32,896]{2,1,0:T(8,128)(2,1)}, f32[16,4096]{1,0:T(8,128)}, f32[16,4096]{1,0:T(8,128)}, f32[16,4096]{1,0:T(8,128)}) custom-call(f32[128,128]{1,0:T(8,128)S(1)} %bitcast.11, bf16[16,32,1152]{2,1,0:T(8,128)(2,1)S(1)} %all-to-all-done.2.arrived, f32[16,4096]{1,0:T(8,128)S(1)} %copy-done.1, f32[16,4096]{1,0:T(8,128)S(1)} %copy-done.3, ...), custom_call_target="tpu_custom_call" | custom-call | flops 2000000 | bytes 4096 | tf_op jit(solution)/shard_map/pallas_call | solution.py:369
  (1 shorter events, 0.0 us)
Async XLA Ops:
  0.6 1.0 copy-start
  1.6 0.9 copy-start.2
  2.5 0.9 copy-start.4
  3.5 1.2 %copy-start.6 = (bf16[1,512,896]{2,1,0:T(8,128)(2,1)S(1)}, bf16[1,512,896]{2,1,0:T(8,128)(2,1)}, u32[]{:S(2)}) copy-start(bf16[1,512,896]{2,1,0:T(8,128)(2,1)} %param.8) | copy-start | bytes 2752516
  5.8 6.6 %collective-permute-start = (bf16[8,32,1664]{2,1,0:T(8,128)(2,1)}, bf16[8,32,1664]{2,1,0:T(8,128)(2,1)S(1)}, u32[]{:S(2)}, u32[]{:S(2)}) collective-permute-start(bf16[8,32,1664]{2,1,0:T(8,128)(2,1)} %get-tuple-element.31), channel_id=1, source_target_pairs={{0,1},{1,0},{2,3},{3,2},{4,5},{5,4},{6,7},{7,6},{8,9},{9,8},{10,11... | collective-permute-start | bytes 2555912 | tf_op jit(solution)/shard_map/ppermute | solution.py:306
  7.2 20.2 %all-to-all-start = ((bf16[8,256,256]{2,1,0:T(8,128)(2,1)}), bf16[8,256,256]{2,1,0:T(8,128)(2,1)S(1)}, u32[]{:S(2)}, u32[]{:S(2)}) async-start(bf16[8,256,256]{2,1,0:T(8,128)(2,1)} %bitcast.14), calls=%async_computation | async-start | bytes 2097152 | tf_op jit(solution)/shard_map/all_to_all | solution.py:297
  13.4 9.1 %collective-permute-start.1 = (bf16[2,32,1664]{2,1,0:T(8,128)(2,1)S(1)}, bf16[2,32,1664]{2,1,0:T(8,128)(2,1)S(1)}, u32[]{:S(2)}, u32[]{:S(2)}) collective-permute-start(bf16[2,32,1664]{2,1,0:T(8,128)(2,1)S(1)} %get-tuple-element.33), channel_id=1, source_target_pairs={{0,4},{2,6},{4,8},{6,10},{8,12},{10,14},{12,0},{14,2},{1,5},{3,7},... | collective-permute-start | bytes 638984 | tf_op jit(solution)/shard_map/ppermute | solution.py:310
  15.0 11.0 %collective-permute-start.2 = (bf16[2,32,1664]{2,1,0:T(8,128)(2,1)S(1)}, bf16[2,32,1664]{2,1,0:T(8,128)(2,1)S(1)}, u32[]{:S(2)}, u32[]{:S(2)}) collective-permute-start(bf16[2,32,1664]{2,1,0:T(8,128)(2,1)S(1)} %get-tuple-element.34), channel_id=1, source_target_pairs={{0,12},{2,14},{4,0},{6,2},{8,4},{10,6},{12,8},{14,10},{1,13},{3,15... | collective-permute-start | bytes 638984 | tf_op jit(solution)/shard_map/ppermute | solution.py:310
  17.2 35.4 %collective-permute-start.3 = (bf16[2,32,1664]{2,1,0:T(8,128)(2,1)}, bf16[2,32,1664]{2,1,0:T(8,128)(2,1)S(1)}, u32[]{:S(2)}, u32[]{:S(2)}) collective-permute-start(bf16[2,32,1664]{2,1,0:T(8,128)(2,1)} %get-tuple-element.35), channel_id=1, source_target_pairs={{0,8},{2,10},{4,12},{6,14},{8,0},{10,2},{12,4},{14,6},{1,9},{3,11}... | collective-permute-start | bytes 638984 | tf_op jit(solution)/shard_map/ppermute | solution.py:310
  18.5 34.1 %collective-permute-start.4 = (bf16[2,32,1664]{2,1,0:T(8,128)(2,1)}, bf16[2,32,1664]{2,1,0:T(8,128)(2,1)S(1)}, u32[]{:S(2)}, u32[]{:S(2)}) collective-permute-start(bf16[2,32,1664]{2,1,0:T(8,128)(2,1)} %get-tuple-element.36), channel_id=1, source_target_pairs={{0,2},{2,0},{4,6},{6,4},{8,10},{10,8},{12,14},{14,12},{1,3},{3,1},... | collective-permute-start | bytes 638984 | tf_op jit(solution)/shard_map/ppermute | solution.py:310
  20.9 31.6 %collective-permute-start.5 = (bf16[2,32,1664]{2,1,0:T(8,128)(2,1)}, bf16[2,32,1664]{2,1,0:T(8,128)(2,1)S(1)}, u32[]{:S(2)}, u32[]{:S(2)}) collective-permute-start(bf16[2,32,1664]{2,1,0:T(8,128)(2,1)} %get-tuple-element.37), channel_id=1, source_target_pairs={{0,6},{2,4},{4,10},{6,8},{8,14},{10,12},{12,2},{14,0},{1,7},{3,5},... | collective-permute-start | bytes 638984 | tf_op jit(solution)/shard_map/ppermute | solution.py:310
  22.5 30.0 %collective-permute-start.6 = (bf16[2,32,1664]{2,1,0:T(8,128)(2,1)}, bf16[2,32,1664]{2,1,0:T(8,128)(2,1)S(1)}, u32[]{:S(2)}, u32[]{:S(2)}) collective-permute-start(bf16[2,32,1664]{2,1,0:T(8,128)(2,1)} %get-tuple-element.38), channel_id=1, source_target_pairs={{0,14},{2,12},{4,2},{6,0},{8,6},{10,4},{12,10},{14,8},{1,15},{3,13... | collective-permute-start | bytes 638984 | tf_op jit(solution)/shard_map/ppermute | solution.py:310
  26.0 26.6 %collective-permute-start.7 = (bf16[2,32,1664]{2,1,0:T(8,128)(2,1)S(1)}, bf16[2,32,1664]{2,1,0:T(8,128)(2,1)S(1)}, u32[]{:S(2)}, u32[]{:S(2)}) collective-permute-start(bf16[2,32,1664]{2,1,0:T(8,128)(2,1)S(1)} %get-tuple-element.39), channel_id=1, source_target_pairs={{0,10},{2,8},{4,14},{6,12},{8,2},{10,0},{12,6},{14,4},{1,11},{3,9}... | collective-permute-start | bytes 638984 | tf_op jit(solution)/shard_map/ppermute | solution.py:310
  56.5 38.0 %all-to-all-start.2 = ((bf16[16,32,1152]{2,1,0:T(8,128)(2,1)}), bf16[16,32,1152]{2,1,0:T(8,128)(2,1)S(1)}, u32[]{:S(2)}, u32[]{:S(2)}) async-start(bf16[16,32,1152]{2,1,0:T(8,128)(2,1)} %shard_map.147), calls=%async_computation.2 | async-start | bytes 2359296 | tf_op jit(solution)/shard_map/all_to_all | solution.py:339
  61.1 16.8 %collective-permute-start.8 = (bf16[256,256]{1,0:T(8,128)(2,1)S(1)}, bf16[256,256]{1,0:T(8,128)(2,1)S(1)}, u32[]{:S(2)}, u32[]{:S(2)}) collective-permute-start(bf16[256,256]{1,0:T(8,128)(2,1)S(1)} %shard_map.149.own), channel_id=1, source_target_pairs={{0,64},{64,0},{1,65},{65,1},{2,66},{66,2},{3,67},{67,3},{4,68},{68... | collective-permute-start | bytes 393224 | tf_op jit(solution)/shard_map/ppermute | solution.py:325
  78.0 8.8 %collective-permute-start.11 = (bf16[2,256,256]{2,1,0:T(8,128)(2,1)S(1)}, bf16[2,256,256]{2,1,0:T(8,128)(2,1)S(1)}, u32[]{:S(2)}, u32[]{:S(2)}) collective-permute-start(bf16[2,256,256]{2,1,0:T(8,128)(2,1)S(1)} %shard_map.150.refs_0_), channel_id=1, source_target_pairs={{0,32},{16,48},{32,0},{48,16},{1,33},{17,49},{33,1},{49,17},{2,34}... | collective-permute-start | bytes 786440 | tf_op jit(solution)/shard_map/ppermute | solution.py:344
  79.1 11.5 %collective-permute-start.10 = (bf16[2,256,256]{2,1,0:T(8,128)(2,1)S(1)}, bf16[2,256,256]{2,1,0:T(8,128)(2,1)S(1)}, u32[]{:S(2)}, u32[]{:S(2)}) collective-permute-start(bf16[2,256,256]{2,1,0:T(8,128)(2,1)S(1)} %shard_map.150.refs_0_), channel_id=1, source_target_pairs={{0,48},{16,0},{32,16},{48,32},{1,49},{17,1},{33,17},{49,33},{2,50}... | collective-permute-start | bytes 786440 | tf_op jit(solution)/shard_map/ppermute | solution.py:344
  81.0 12.5 %collective-permute-start.9 = (bf16[2,256,256]{2,1,0:T(8,128)(2,1)S(1)}, bf16[2,256,256]{2,1,0:T(8,128)(2,1)S(1)}, u32[]{:S(2)}, u32[]{:S(2)}) collective-permute-start(bf16[2,256,256]{2,1,0:T(8,128)(2,1)S(1)} %shard_map.150.refs_0_), channel_id=1, source_target_pairs={{0,16},{16,32},{32,48},{48,0},{1,17},{17,33},{33,49},{49,1},{2,18}... | collective-permute-start | bytes 786440 | tf_op jit(solution)/shard_map/ppermute | solution.py:344
  86.3 8.2 %copy-start.1 = (f32[16,4096]{1,0:T(8,128)S(1)}, f32[16,4096]{1,0:T(8,128)}, u32[]{:S(2)}) copy-start(f32[16,4096]{1,0:T(8,128)} %refs_0_.1) | copy-start | bytes 786436
  86.3 8.2 %copy-start.3 = (f32[16,4096]{1,0:T(8,128)S(1)}, f32[16,4096]{1,0:T(8,128)}, u32[]{:S(2)}) copy-start(f32[16,4096]{1,0:T(8,128)} %refs_1_.1) | copy-start | bytes 786436
  86.3 8.2 %copy-start.5 = (f32[16,4096]{1,0:T(8,128)S(1)}, f32[16,4096]{1,0:T(8,128)}, u32[]{:S(2)}) copy-start(f32[16,4096]{1,0:T(8,128)} %refs_2_.1) | copy-start | bytes 786436

commit v6 on v5

--- a/solution.py
+++ b/solution.py
@@ -26,7 +26,9 @@
 AROWS, ACOLS = 16, 256
 STATE = 3 * ACOLS
 WIDE = COLS + STATE
-BACK = COLS + ACOLS
+BACK = COLS + ACOLS // 2
+EARLY = 1
+SHIFT = 5.2
 
 CHIP_STEPS = ((1, 0), (3, 0), (2, 0), (0, 1), (1, 1), (3, 1), (2, 1))
 REPLICA_STEPS = (1, 3, 2)
@@ -57,6 +59,17 @@
 def halves(x):
     high = x.astype(bf16)
     return high, (x - high.astype(f32)).astype(bf16)
+
+
+def code(x):
+    size = jnp.exp(6.0 * (jnp.log(jnp.maximum(jnp.abs(x), 1e-30)) + SHIFT))
+    return jnp.where(x < 0.0, -size, size).astype(bf16)
+
+
+def decode(y):
+    y = y.astype(f32)
+    size = jnp.exp(jnp.log(jnp.maximum(jnp.abs(y), 1e-37)) * (1.0 / 6.0) - SHIFT)
+    return jnp.where(y == 0.0, 0.0, jnp.where(y < 0.0, -size, size))
 
 
 def adam_update(gradient, master, moment, second, clip_factor):
@@ -140,14 +153,15 @@
 
 
 def expert_weight_kernel(sums, attn, *refs):
-    blocks, streams, out = refs[:8], refs[8:11], refs[11]
-    held, weights, sems, out_sems = refs[12:]
+    blocks, early, streams, out = refs[:8], refs[8], refs[9:12], refs[12]
+    held, weights, sems, out_sems = refs[13:]
     loads = []
     for n, chip in enumerate(sources()):
         loads.append(
             [
-                pltpu.make_async_copy(array.at[:, wide_cols(chip)], held.at[m, n], sems.at[n, m])
+                pltpu.make_async_copy(array.at[:, wide_cols(chip)], held.at[m, n - EARLY], sems.at[n - EARLY, m])
                 for m, array in enumerate(streams)
+                if n >= EARLY
             ]
         )
         for copy in loads[n]:
@@ -157,18 +171,19 @@
     for n, (chip, block) in enumerate(zip(sources(), blocks)):
         for core in range(2):
             rows = pl.ds(pl.multiple_of((chip * 2 + core) * AROWS, AROWS), AROWS)
-            high, low = halves(attn[rows, :])
-            weights[n, core, :AROWS, COLS:] = high
-            weights[n, core, AROWS:, COLS:] = low
+            scaled = code(clip * attn[rows, :])
+            weights[n, core, :AROWS, COLS:] = scaled[:, :128]
+            weights[n, core, AROWS:, COLS:] = scaled[:, 128:]
         for copy in loads[n]:
             copy.wait()
+        state = early.at[:, n] if n < EARLY else held.at[:, n - EARLY]
         for at in range(14):
             core, col = divmod(at, 7)
             new = adam_weight(
                 block[core, :, lanes(col)].astype(f32),
-                held[0, n, :, lanes(at)],
-                held[1, n, :, lanes(at)],
-                held[2, n, :, lanes(at)],
+                state[0, :, lanes(at)],
+                state[1, :, lanes(at)],
+                state[2, :, lanes(at)],
                 clip,
             )
             weights[n, core, :, lanes(col)] = new.astype(bf16)
@@ -219,56 +234,59 @@
 
 
 def attn_weight_kernel(sums, attn, *refs):
-    blocks, out = refs[:8], refs[8]
+    blocks, state, out, early, sems = refs[:8], refs[8:11], refs[11], refs[12], refs[13]
+    loads = []
+    for n, chip in enumerate(sources()[:EARLY]):
+        for m, array in enumerate(state):
+            loads.append(
+                pltpu.make_async_copy(array.at[:, wide_cols(chip)], early.at[m, n], sems.at[n, m])
+            )
+            loads[-1].start()
     clip = clip_of(sums)
     for chip, block in zip(sources(), blocks):
         for core in range(2):
             rows = pl.ds(pl.multiple_of((chip * 2 + core) * AROWS, AROWS), AROWS)
-            state = block[core, :AROWS, COLS:].astype(f32) + block[core, AROWS:, COLS:].astype(f32)
+            came = block[core, :AROWS, COLS:].astype(f32) + block[core, AROWS:, COLS:].astype(f32)
             new = adam_weight(
                 attn[rows, :],
-                state[:, :ACOLS],
-                state[:, ACOLS : 2 * ACOLS],
-                state[:, 2 * ACOLS :],
+                came[:, :ACOLS],
+                came[:, ACOLS : 2 * ACOLS],
+                came[:, 2 * ACOLS :],
                 clip,
             )
             out[rows, :] = new.astype(bf16)
-
-
-def both_kernel(own, other, out):
-    x = lax.axis_index("gx_0")
-    out[x] = own[...]
-    out[1 - x] = other[...]
+    for copy in loads:
+        copy.wait()
 
 
 def join_kernel(*refs):
-    pieces, out, sems = refs[:4], refs[4], refs[5]
-    y = lax.axis_index("gx_1")
+    out, sems = refs[8], refs[9]
+    x, y = (lax.axis_index(axis) for axis in GX)
     stores = []
-    for n, (dy, piece) in enumerate(zip((0,) + REPLICA_STEPS, pieces)):
-        for x in range(2):
-            slot = x * 4 + lax.rem(y + 4 - dy, 4)
-            stores.append(pltpu.make_async_copy(piece.at[x], out.at[slot], sems.at[n, x]))
+    for half, row in enumerate((x, 1 - x)):
+        for n, dy in enumerate((0,) + REPLICA_STEPS):
+            slot = row * 4 + lax.rem(y + 4 - dy, 4)
+            at = 4 * half + n
+            stores.append(pltpu.make_async_copy(refs[at], out.at[slot], sems.at[at]))
             stores[-1].start()
     for store in stores:
         store.wait()
 
 
-def finish_kernel(sums, arrived, *refs):
+def finish_kernel(arrived, *refs):
     state, weight, outs, news, sem, out_sems = refs[:3], refs[3], refs[4:7], refs[7], refs[8], refs[9]
     stores = [pltpu.make_async_copy(arrived.at[:, :, :COLS], weight, sem)]
     stores[0].start()
-    clip = clip_of(sums)
     for part in range(4):
         for group in range(4 * part, 4 * part + 4):
-            cols = slice(group * ACOLS, (group + 1) * ACOLS)
-            gradient = arrived[group, :AROWS, COLS:].astype(f32)
-            gradient = gradient + arrived[group, AROWS:, COLS:].astype(f32)
-            results = adam_update(
-                gradient, state[0][:, cols], state[1][:, cols], state[2][:, cols], clip
-            )
-            for m, result in enumerate(results):
-                news[m, :, cols] = result
+            for half in range(2):
+                scaled = decode(arrived[group, half * AROWS : (half + 1) * AROWS, COLS:])
+                cols = lanes(2 * group + half)
+                results = adam_update(
+                    scaled, state[0][:, cols], state[1][:, cols], state[2][:, cols], 1.0
+                )
+                for m, result in enumerate(results):
+                    news[m, :, cols] = result
         cols = pl.ds(part * 4 * ACOLS, 4 * ACOLS)
         for m, out in enumerate(outs):
             store = pltpu.make_async_copy(
@@ -319,30 +337,36 @@
     vmem = pl.BlockSpec(memory_space=pltpu.VMEM)
     hbm = pl.BlockSpec(memory_space=pltpu.HBM)
     state = far(expert_master, expert_moment, expert_second)
-    attn_block = call(attn_weight_kernel, pltpu.VMEM((256, ACOLS), bf16), 2000000)(
-        *near(sums, attn_sum, *blocks)
-    )
+    attn_block, early = call(
+        attn_weight_kernel,
+        (pltpu.VMEM((256, ACOLS), bf16), pltpu.VMEM((3, EARLY, ROWS, 2 * COLS), f32)),
+        2000000,
+        in_specs=[vmem] * 10 + [hbm] * 3,
+        out_specs=[vmem] * 2,
+        scratch_shapes=[pltpu.SemaphoreType.DMA((EARLY, 3))],
+    )(*near(sums, attn_sum, *blocks), *state)
     other = lax.ppermute(attn_block, "gx_0", [(0, 1), (1, 0)])
     weights = call(
         expert_weight_kernel,
         pltpu.HBM((16, ROWS, BACK), bf16),
         8000000,
-        in_specs=[vmem] * 10 + [hbm] * 3,
+        in_specs=[vmem] * 11 + [hbm] * 3,
         out_specs=hbm,
         scratch_shapes=[
-            pltpu.VMEM((3, 8, ROWS, 2 * COLS), f32),
+            pltpu.VMEM((3, 8 - EARLY, ROWS, 2 * COLS), f32),
             pltpu.VMEM((8, 2, ROWS, BACK), bf16),
-            pltpu.SemaphoreType.DMA((8, 3)),
+            pltpu.SemaphoreType.DMA((8 - EARLY, 3)),
             pltpu.SemaphoreType.DMA((8,)),
         ],
-    )(*near(sums, attn_sum, *blocks), *state)
+    )(*near(sums, attn_sum, *blocks, early), *state)
     returned = lax.all_to_all(weights, GY, split_axis=0, concat_axis=0, tiled=True)
-    both = call(both_kernel, pltpu.VMEM((2, 256, ACOLS), bf16), 1000000)(*near(attn_block, other))
-    pieces = [both]
-    for n in range(3):
-        pieces.append(
-            lax.ppermute(both, "gx_1", [(y, (y + REPLICA_STEPS[n]) % 4) for y in range(4)])
-        )
+    pieces = []
+    for block in (attn_block, other):
+        pieces.append(block)
+        for dy in REPLICA_STEPS:
+            pieces.append(
+                lax.ppermute(block, "gx_1", [(y, (y + dy) % 4) for y in range(4)])
+            )
     e_master, e_moment, e_second = call(
         expert_state_kernel,
         (pltpu.HBM((ROWS, 16 * COLS), f32),) * 3,
@@ -362,22 +386,22 @@
         join_kernel,
         pltpu.HBM((8, 256, ACOLS), bf16),
         1000000,
-        in_specs=[vmem] * 4,
+        in_specs=[vmem] * 8,
         out_specs=hbm,
-        scratch_shapes=[pltpu.SemaphoreType.DMA((4, 2))],
+        scratch_shapes=[pltpu.SemaphoreType.DMA((8,))],
     )(*near(*pieces))
     expert_weight, a_master, a_moment, a_second = call(
         finish_kernel,
         (pltpu.HBM((16, ROWS, COLS), bf16),) + (pltpu.HBM((AROWS, 16 * ACOLS), f32),) * 3,
         2000000,
-        in_specs=[vmem] * 5,
+        in_specs=[vmem] * 4,
         out_specs=[hbm] * 4,
         scratch_shapes=[
             pltpu.VMEM((3, AROWS, 16 * ACOLS), f32),
             pltpu.SemaphoreType.DMA,
             pltpu.SemaphoreType.DMA((4, 3)),
         ],
-    )(*near(sums, returned), attn_master, attn_moment, attn_second)
+    )(*near(returned), attn_master, attn_moment, attn_second)
     return (
         e_master,
         e_moment,

time: 96.4 us -> 90 us (0.934); the launches traced: 96 us -> 88.3 us
  waiting for transfers between devices: 24.6 us -> 13.9 us
  starting transfers between devices: 27.2 us -> 29.5 us
    ppermute x3 -> x6, waiting for transfers between devices: 7.11 us -> 0.02 us  [local(): lax.ppermute(block, 'gx_1', [(y, (y + dy) % 4) for y in range(4)])]
    ppermute x1, waiting for transfers between devices: 16.3 us -> 12.6 us  [local(): other = lax.ppermute(attn_block, 'gx_0', [(0, 1), (1, 0)])]
    ppermute x3 -> x6, starting transfers between devices: 2.96 us -> 5.36 us  [local(): lax.ppermute(block, 'gx_1', [(y, (y + dy) % 4) for y in range(4)])]
  transfers between devices with their start and end apart: 14 -> 17, of which waited for: 6 -> 3; matrix products, arithmetic and copies ran while one was open for 0% -> 0% of each run, Pallas kernels for 8% -> 8%
where the time goes in v6:
time: 90 us; the launch traced here: 88.3 us
  starting transfers between devices  29.5 us (33%)
  blocking collectives  25 us (28%)
  Pallas kernels  14.8 us (16%)
  waiting for transfers between devices  13.9 us (15%)
  local copies, waits for them, and re-layouts  4.27 us (5%)
    all_to_all x1, blocking collectives, local(): lax.all_to_all(partial.reshape(128, 1, 128), GX_GY, split_axis=0, concat_...  25 us
    ppermute x7, starting transfers between devices, local(): blocks.append(lax.ppermute(routed[n + 1], GY[:2], chip_pairs(*step)))  12.7 us
    ppermute x1, waiting for transfers between devices, local(): other = lax.ppermute(attn_block, 'gx_0', [(0, 1), (1, 0)])  12.6 us
    ppermute x6, starting transfers between devices, local(): lax.ppermute(block, 'gx_1', [(y, (y + dy) % 4) for y in range(4)])  5.36 us
    pallas_call x1, Pallas kernels, local(): call(expert_state_kernel, (pltpu.HBM((ROWS, 16 * COLS), f32),) * 3, 80000...  5.31 us
    all_to_all x1, starting transfers between devices, local(): lax.all_to_all(attn_grad.reshape(8, 256, ACOLS), GX, split_axis=0, concat...  5.23 us
    all_to_all x1, starting transfers between devices, local(): lax.all_to_all(weights, GY, split_axis=0, concat_axis=0, tiled=True)  4.37 us
    unnamed x14, local copies, waits for them, and re-layouts  4.27 us
  transfers between devices with their start and end apart: 17, of which 3 were waited for; matrix products, arithmetic and copies ran while one was open for 0% of the time, Pallas kernels for 8%

profile of v6, /device:TPU:1, one launch (start us, length us, event | category | flops | bytes accessed | tf_op | source)
XLA Modules:
  0.0 88.3 jit_solution(4640213331168993828)
XLA Ops:
  0.6 0.0 copy-start
  0.6 0.9 %copy-done = f32[16,4096]{1,0:T(8,128)S(1)} copy-done((f32[16,4096]{1,0:T(8,128)S(1)}, f32[16,4096]{1,0:T(8,128)}, u32[]{:S(2)}) %copy-start) | copy-done | bytes 262168
  1.6 0.0 copy-start.2
  1.6 0.9 %copy-done.2 = f32[16,4096]{1,0:T(8,128)S(1)} copy-done((f32[16,4096]{1,0:T(8,128)S(1)}, f32[16,4096]{1,0:T(8,128)}, u32[]{:S(2)}) %copy-start.2) | copy-done | bytes 262168
  2.5 0.0 copy-start.4
  2.5 0.9 %copy-done.4 = f32[16,4096]{1,0:T(8,128)S(1)} copy-done((f32[16,4096]{1,0:T(8,128)S(1)}, f32[16,4096]{1,0:T(8,128)}, u32[]{:S(2)}) %copy-start.4) | copy-done | bytes 262168
  3.5 0.0 copy-start.6
  3.5 1.2 %copy-done.6 = bf16[1,512,896]{2,1,0:T(8,128)(2,1)S(1)} copy-done((bf16[1,512,896]{2,1,0:T(8,128)(2,1)S(1)}, bf16[1,512,896]{2,1,0:T(8,128)(2,1)}, u32[]{:S(2)}) %copy-start.6) | copy-done | bytes 917528
  4.7 1.1 %shard_map.143 = (bf16[8,32,1664]{2,1,0:T(8,128)(2,1)S(1)}, bf16[8,32,1664]{2,1,0:T(8,128)(2,1)}, f32[1,128]{1,0:T(1,128)S(1)}) custom-call(bf16[16,32,896]{2,1,0:T(8,128)(2,1)S(1)} %bitcast.11, f32[16,4096]{1,0:T(8,128)S(1)} %copy-done, f32[16,4096]{1,0:T(8,128)S(1)} %copy-done.2, f32[16,4096]{1,0:T(8,128)S(1)} %copy-done.4), custom_call_target="tpu_custom_call" | custom-call | flops 4000000 | bytes 4096 | tf_op jit(solution)/shard_map/pallas_call | solution.py:319
  5.8 1.4 %collective-permute-start = (bf16[8,32,1664]{2,1,0:T(8,128)(2,1)}, bf16[8,32,1664]{2,1,0:T(8,128)(2,1)S(1)}, u32[]{:S(2)}, u32[]{:S(2)}) collective-permute-start(bf16[8,32,1664]{2,1,0:T(8,128)(2,1)} %get-tuple-element.33), channel_id=1, source_target_pairs={{0,1},{1,0},{2,3},{3,2},{4,5},{5,4},{6,7},{7,6},{8,9},{9,8},{10,11... | collective-permute-start | bytes 2555912 | tf_op jit(solution)/shard_map/ppermute | solution.py:324
  7.2 5.2 %all-to-all-start = ((bf16[8,256,256]{2,1,0:T(8,128)(2,1)}), bf16[8,256,256]{2,1,0:T(8,128)(2,1)S(1)}, u32[]{:S(2)}, u32[]{:S(2)}) async-start(bf16[8,256,256]{2,1,0:T(8,128)(2,1)} %bitcast.13), calls=%async_computation | async-start | bytes 2097152 | tf_op jit(solution)/shard_map/all_to_all | solution.py:315
  12.4 0.0 collective-permute-done.swapped
  12.4 0.9 %shard_map.145 = (bf16[2,32,1664]{2,1,0:T(8,128)(2,1)S(1)}, bf16[2,32,1664]{2,1,0:T(8,128)(2,1)S(1)}, bf16[2,32,1664]{2,1,0:T(8,128)(2,1)S(1)}, bf16[2,32,1664]{...) custom-call(bf16[8,32,1664]{2,1,0:T(8,128)(2,1)S(1)} %get-tuple-elem, ...), custom_call_target="tpu_custom_call" | custom-call | flops 1000000 | bytes 4096 | tf_op jit(solution)/shard_map/pallas_call | solution.py:325
  13.3 1.6 %collective-permute-start.1 = (bf16[2,32,1664]{2,1,0:T(8,128)(2,1)S(1)}, bf16[2,32,1664]{2,1,0:T(8,128)(2,1)S(1)}, u32[]{:S(2)}, u32[]{:S(2)}) collective-permute-start(bf16[2,32,1664]{2,1,0:T(8,128)(2,1)S(1)} %get-tuple-element.35), channel_id=1, source_target_pairs={{0,4},{2,6},{4,8},{6,10},{8,12},{10,14},{12,0},{14,2},{1,5},{3,7},... | collective-permute-start | bytes 638984 | tf_op jit(solution)/shard_map/ppermute | solution.py:328
  15.0 2.1 %collective-permute-start.2 = (bf16[2,32,1664]{2,1,0:T(8,128)(2,1)S(1)}, bf16[2,32,1664]{2,1,0:T(8,128)(2,1)S(1)}, u32[]{:S(2)}, u32[]{:S(2)}) collective-permute-start(bf16[2,32,1664]{2,1,0:T(8,128)(2,1)S(1)} %get-tuple-element.36), channel_id=1, source_target_pairs={{0,12},{2,14},{4,0},{6,2},{8,4},{10,6},{12,8},{14,10},{1,13},{3,15... | collective-permute-start | bytes 638984 | tf_op jit(solution)/shard_map/ppermute | solution.py:328
  17.1 1.3 %collective-permute-start.3 = (bf16[2,32,1664]{2,1,0:T(8,128)(2,1)}, bf16[2,32,1664]{2,1,0:T(8,128)(2,1)S(1)}, u32[]{:S(2)}, u32[]{:S(2)}) collective-permute-start(bf16[2,32,1664]{2,1,0:T(8,128)(2,1)} %get-tuple-element.37), channel_id=1, source_target_pairs={{0,8},{2,10},{4,12},{6,14},{8,0},{10,2},{12,4},{14,6},{1,9},{3,11}... | collective-permute-start | bytes 638984 | tf_op jit(solution)/shard_map/ppermute | solution.py:328
  18.4 2.5 %collective-permute-start.4 = (bf16[2,32,1664]{2,1,0:T(8,128)(2,1)}, bf16[2,32,1664]{2,1,0:T(8,128)(2,1)S(1)}, u32[]{:S(2)}, u32[]{:S(2)}) collective-permute-start(bf16[2,32,1664]{2,1,0:T(8,128)(2,1)} %get-tuple-element.38), channel_id=1, source_target_pairs={{0,2},{2,0},{4,6},{6,4},{8,10},{10,8},{12,14},{14,12},{1,3},{3,1},... | collective-permute-start | bytes 638984 | tf_op jit(solution)/shard_map/ppermute | solution.py:328
  20.8 1.0 %collective-permute-start.5 = (bf16[2,32,1664]{2,1,0:T(8,128)(2,1)}, bf16[2,32,1664]{2,1,0:T(8,128)(2,1)S(1)}, u32[]{:S(2)}, u32[]{:S(2)}) collective-permute-start(bf16[2,32,1664]{2,1,0:T(8,128)(2,1)} %get-tuple-element.39), channel_id=1, source_target_pairs={{0,6},{2,4},{4,10},{6,8},{8,14},{10,12},{12,2},{14,0},{1,7},{3,5},... | collective-permute-start | bytes 638984 | tf_op jit(solution)/shard_map/ppermute | solution.py:328
  21.8 0.6 collective-permute-done.1.refs_1_
  22.4 3.5 %collective-permute-start.6 = (bf16[2,32,1664]{2,1,0:T(8,128)(2,1)S(1)}, bf16[2,32,1664]{2,1,0:T(8,128)(2,1)S(1)}, u32[]{:S(2)}, u32[]{:S(2)}) collective-permute-start(bf16[2,32,1664]{2,1,0:T(8,128)(2,1)S(1)} %get-tuple-element.40), channel_id=1, source_target_pairs={{0,14},{2,12},{4,2},{6,0},{8,6},{10,4},{12,10},{14,8},{1,15},{3,13... | collective-permute-start | bytes 638984 | tf_op jit(solution)/shard_map/ppermute | solution.py:328
  25.9 0.0 collective-permute-done.2.refs_2_
  25.9 0.8 collective-permute-start.7
  26.7 0.7 all-to-all-done.arrived
  27.4 0.2 shard_map.144
  27.5 25.0 %all_to_all.15 = f32[128,1,128]{2,1,0:T(1,128)S(1)} all-to-all(f32[128,1,128]{2,1,0:T(1,128)S(1)} %bitcast.12), channel_id=1, replica_groups=mesh['gx_0'=2,'gx_1'=4,'gy_0'=4,'gy_1'=2,'gy_2'=2] {'gx_0','gx_1','gy_0'..., dimensions={0} | all-to-all | bytes 131072 | tf_op jit(solution)/shard_map/all_to_all | solution.py:333
  52.5 0.0 collective-permute-done.3.refs_3_
  52.5 0.0 collective-permute-done.4.refs_4_
  52.5 0.0 collective-permute-done.5.refs_5_
  52.5 0.0 collective-permute-done.6.refs_6_
  52.5 0.0 collective-permute-done.7.refs_7_
  52.6 1.2 %shard_map.147 = (bf16[256,256]{1,0:T(8,128)(2,1)S(1)}, f32[3,1,32,1792]{3,2,1,0:T(8,128)S(1)}) custom-call(f32[128,128]{1,0:T(8,128)S(1)} %bitcast.8, f32[256,256]{1,0:T(8,128)S(1)} %get-tuple-element.45.attn, bf16[2,32,1664]{2,1,0:T(8,128)(2,1)S(1)} %get-tuple-element.34.refs_0_, bf16[2,32,1664]{2,1,0:T(8,128)(2,1)S(1)} %collective-permute-done.1.refs_1_, ...), custom_call_target="tpu_custom_call" | custom-call | flops 2000000 | bytes 4096 | tf_op jit(solution)/shard_map/pallas_call | solution.py:340
  53.8 3.7 %shard_map.148 = bf16[16,32,1024]{2,1,0:T(8,128)(2,1)} custom-call(f32[128,128]{1,0:T(8,128)S(1)} %bitcast.9, f32[256,256]{1,0:T(8,128)S(1)} %get-tuple-element.45.attn, bf16[2,32,1664]{2,1,0:T(8,128)(2,1)S(1)} %get-tuple-element.34.refs_0_, bf16[2,32,1664]{2,1,0:T(8,128)(2,1)S(1)} %collective-permute-done.1.refs_1_, ...), custom_call_target="tpu_custom_call" | custom-call | flops 8000000 | bytes 4096 | tf_op jit(solution)/shard_map/pallas_call | solution.py:349
  57.5 4.4 %all-to-all-start.2 = ((bf16[16,32,1024]{2,1,0:T(8,128)(2,1)}), bf16[16,32,1024]{2,1,0:T(8,128)(2,1)S(1)}, u32[]{:S(2)}, u32[]{:S(2)}) async-start(bf16[16,32,1024]{2,1,0:T(8,128)(2,1)} %shard_map.148), calls=%async_computation.2 | async-start | bytes 2097152 | tf_op jit(solution)/shard_map/all_to_all | solution.py:362
  61.8 0.5 collective-permute-start.11
  62.3 0.4 collective-permute-start.8
  62.7 2.3 %collective-permute-start.9 = (bf16[256,256]{1,0:T(8,128)(2,1)S(1)}, bf16[256,256]{1,0:T(8,128)(2,1)S(1)}, u32[]{:S(2)}, u32[]{:S(2)}) collective-permute-start(bf16[256,256]{1,0:T(8,128)(2,1)S(1)} %get-tuple-element.51.refs_0_), channel_id=1, source_target_pairs={{0,48},{16,0},{32,16},{48,32},{1,49},{17,1},{33,17},{49,33},{2,50}... | collective-permute-start | bytes 393224 | tf_op jit(solution)/shard_map/ppermute | solution.py:368
  65.0 0.0 collective-permute-start.10
  65.0 12.6 %collective-permute-done.11.refs_4_ = bf16[256,256]{1,0:T(8,128)(2,1)S(1)} collective-permute-done((bf16[256,256]{1,0:T(8,128)(2,1)S(1)}, bf16[256,256]{1,0:T(8,128)(2,1)S(1)}, u32[]{:S(2)}, u32[]{:S(2)}) %collective-permute-start.11) | collective-permute-done | bytes 131104 | tf_op jit(solution)/shard_map/ppermute | solution.py:348
  77.6 0.4 collective-permute-start.12
  78.0 2.3 %collective-permute-start.13 = (bf16[256,256]{1,0:T(8,128)(2,1)S(1)}, bf16[256,256]{1,0:T(8,128)(2,1)S(1)}, u32[]{:S(2)}, u32[]{:S(2)}) collective-permute-start(bf16[256,256]{1,0:T(8,128)(2,1)S(1)} %collective-permute-done.11.refs_4_), channel_id=1, source_target_pairs={{0,48},{16,0},{32,16},{48,32},{1,49},{17,1},{33,17},{49,33},{2,50}... | collective-permute-start | bytes 393224 | tf_op jit(solution)/shard_map/ppermute | solution.py:368
  80.2 0.0 collective-permute-done.8.refs_1_
  80.3 0.0 collective-permute-start.14
  80.3 5.3 %shard_map.146 = (f32[32,14336]{1,0:T(8,128)}, f32[32,14336]{1,0:T(8,128)}, f32[32,14336]{1,0:T(8,128)}) custom-call(f32[128,128]{1,0:T(8,128)S(1)} %bitcast.10, bf16[2,32,1664]{2,1,0:T(8,128)(2,1)S(1)} %get-tuple-element.34.refs_0_, bf16[2,32,1664]{2,1,0:T(8,128)(2,1)S(1)} %collective-permute-done.1.refs_1_, ...), custom_call_target="tpu_custom_call" | custom-call | flops 8000000 | bytes 4096 | tf_op jit(solution)/shard_map/pallas_call | solution.py:370
  85.6 0.0 copy-start.1
  85.6 0.0 copy-start.3
  85.6 0.0 copy-start.5
  85.6 0.0 collective-permute-done.9.refs_2_
  85.6 0.0 collective-permute-done.10.refs_3_
  85.6 0.0 collective-permute-done.12.refs_5_
  85.6 0.0 collective-permute-done.13.refs_6_
  85.7 0.0 collective-permute-done.14.refs_7_
  85.7 1.0 %shard_map.150 = bf16[8,256,256]{2,1,0:T(8,128)(2,1)} custom-call(bf16[256,256]{1,0:T(8,128)(2,1)S(1)} %get-tuple-element.51.refs_0_, bf16[256,256]{1,0:T(8,128)(2,1)S(1)} %collective-permute-done.8.refs_1_, bf16[256,256]{1,0:T(8,128)(2,1)S(1)} %collective-permute-done.9.refs_2_, bf16[256,256]{1,0:T(8,128)(2,1)S(1)} %collective-permute-done.10.refs_3_, ...), custom_call_target="tpu_custom_call" | custom-call | flops 1000000 | bytes 4096 | tf_op jit(solution)/shard_map/pallas_call | solution.py:385
  86.7 0.0 all-to-all-done.2.arrived
  86.7 0.0 copy-done.1
  86.7 0.0 copy-done.3
  86.7 0.2 copy-done.5
  87.0 1.4 %shard_map.149 = (bf16[16,32,896]{2,1,0:T(8,128)(2,1)}, f32[16,4096]{1,0:T(8,128)}, f32[16,4096]{1,0:T(8,128)}, f32[16,4096]{1,0:T(8,128)}) custom-call(bf16[16,32,1024]{2,1,0:T(8,128)(2,1)S(1)} %all-to-all-done.2.arrived, f32[16,4096]{1,0:T(8,128)S(1)} %copy-done.1, f32[16,4096]{1,0:T(8,128)S(1)} %copy-done.3, f32[16,4096]{1,0:T(8,128)S(1)} %copy-done.5), custom_call_target="tpu_custom_call" | custom-call | flops 2000000 | bytes 4096 | tf_op jit(solution)/shard_map/pallas_call | solution.py:393
Async XLA Ops:
  0.6 1.0 %copy-start = (f32[16,4096]{1,0:T(8,128)S(1)}, f32[16,4096]{1,0:T(8,128)}, u32[]{:S(2)}) copy-start(f32[16,4096]{1,0:T(8,128)} %refs_0_.1) | copy-start | bytes 786436
  1.6 0.9 %copy-start.2 = (f32[16,4096]{1,0:T(8,128)S(1)}, f32[16,4096]{1,0:T(8,128)}, u32[]{:S(2)}) copy-start(f32[16,4096]{1,0:T(8,128)} %refs_1_.1) | copy-start | bytes 786436
  2.5 0.9 %copy-start.4 = (f32[16,4096]{1,0:T(8,128)S(1)}, f32[16,4096]{1,0:T(8,128)}, u32[]{:S(2)}) copy-start(f32[16,4096]{1,0:T(8,128)} %refs_2_.1) | copy-start | bytes 786436
  3.5 1.2 %copy-start.6 = (bf16[1,512,896]{2,1,0:T(8,128)(2,1)S(1)}, bf16[1,512,896]{2,1,0:T(8,128)(2,1)}, u32[]{:S(2)}) copy-start(bf16[1,512,896]{2,1,0:T(8,128)(2,1)} %param.8) | copy-start | bytes 2752516
  5.8 6.6 %collective-permute-start = (bf16[8,32,1664]{2,1,0:T(8,128)(2,1)}, bf16[8,32,1664]{2,1,0:T(8,128)(2,1)S(1)}, u32[]{:S(2)}, u32[]{:S(2)}) collective-permute-start(bf16[8,32,1664]{2,1,0:T(8,128)(2,1)} %get-tuple-element.33), channel_id=1, source_target_pairs={{0,1},{1,0},{2,3},{3,2},{4,5},{5,4},{6,7},{7,6},{8,9},{9,8},{10,11... | collective-permute-start | bytes 2555912 | tf_op jit(solution)/shard_map/ppermute | solution.py:324
  7.2 20.2 %all-to-all-start = ((bf16[8,256,256]{2,1,0:T(8,128)(2,1)}), bf16[8,256,256]{2,1,0:T(8,128)(2,1)S(1)}, u32[]{:S(2)}, u32[]{:S(2)}) async-start(bf16[8,256,256]{2,1,0:T(8,128)(2,1)} %bitcast.13), calls=%async_computation | async-start | bytes 2097152 | tf_op jit(solution)/shard_map/all_to_all | solution.py:315
  13.3 9.1 %collective-permute-start.1 = (bf16[2,32,1664]{2,1,0:T(8,128)(2,1)S(1)}, bf16[2,32,1664]{2,1,0:T(8,128)(2,1)S(1)}, u32[]{:S(2)}, u32[]{:S(2)}) collective-permute-start(bf16[2,32,1664]{2,1,0:T(8,128)(2,1)S(1)} %get-tuple-element.35), channel_id=1, source_target_pairs={{0,4},{2,6},{4,8},{6,10},{8,12},{10,14},{12,0},{14,2},{1,5},{3,7},... | collective-permute-start | bytes 638984 | tf_op jit(solution)/shard_map/ppermute | solution.py:328
  15.0 11.0 %collective-permute-start.2 = (bf16[2,32,1664]{2,1,0:T(8,128)(2,1)S(1)}, bf16[2,32,1664]{2,1,0:T(8,128)(2,1)S(1)}, u32[]{:S(2)}, u32[]{:S(2)}) collective-permute-start(bf16[2,32,1664]{2,1,0:T(8,128)(2,1)S(1)} %get-tuple-element.36), channel_id=1, source_target_pairs={{0,12},{2,14},{4,0},{6,2},{8,4},{10,6},{12,8},{14,10},{1,13},{3,15... | collective-permute-start | bytes 638984 | tf_op jit(solution)/shard_map/ppermute | solution.py:328
  17.1 35.4 %collective-permute-start.3 = (bf16[2,32,1664]{2,1,0:T(8,128)(2,1)}, bf16[2,32,1664]{2,1,0:T(8,128)(2,1)S(1)}, u32[]{:S(2)}, u32[]{:S(2)}) collective-permute-start(bf16[2,32,1664]{2,1,0:T(8,128)(2,1)} %get-tuple-element.37), channel_id=1, source_target_pairs={{0,8},{2,10},{4,12},{6,14},{8,0},{10,2},{12,4},{14,6},{1,9},{3,11}... | collective-permute-start | bytes 638984 | tf_op jit(solution)/shard_map/ppermute | solution.py:328
  18.4 34.1 %collective-permute-start.4 = (bf16[2,32,1664]{2,1,0:T(8,128)(2,1)}, bf16[2,32,1664]{2,1,0:T(8,128)(2,1)S(1)}, u32[]{:S(2)}, u32[]{:S(2)}) collective-permute-start(bf16[2,32,1664]{2,1,0:T(8,128)(2,1)} %get-tuple-element.38), channel_id=1, source_target_pairs={{0,2},{2,0},{4,6},{6,4},{8,10},{10,8},{12,14},{14,12},{1,3},{3,1},... | collective-permute-start | bytes 638984 | tf_op jit(solution)/shard_map/ppermute | solution.py:328
  20.8 31.7 %collective-permute-start.5 = (bf16[2,32,1664]{2,1,0:T(8,128)(2,1)}, bf16[2,32,1664]{2,1,0:T(8,128)(2,1)S(1)}, u32[]{:S(2)}, u32[]{:S(2)}) collective-permute-start(bf16[2,32,1664]{2,1,0:T(8,128)(2,1)} %get-tuple-element.39), channel_id=1, source_target_pairs={{0,6},{2,4},{4,10},{6,8},{8,14},{10,12},{12,2},{14,0},{1,7},{3,5},... | collective-permute-start | bytes 638984 | tf_op jit(solution)/shard_map/ppermute | solution.py:328
  22.4 30.1 %collective-permute-start.6 = (bf16[2,32,1664]{2,1,0:T(8,128)(2,1)S(1)}, bf16[2,32,1664]{2,1,0:T(8,128)(2,1)S(1)}, u32[]{:S(2)}, u32[]{:S(2)}) collective-permute-start(bf16[2,32,1664]{2,1,0:T(8,128)(2,1)S(1)} %get-tuple-element.40), channel_id=1, source_target_pairs={{0,14},{2,12},{4,2},{6,0},{8,6},{10,4},{12,10},{14,8},{1,15},{3,13... | collective-permute-start | bytes 638984 | tf_op jit(solution)/shard_map/ppermute | solution.py:328
  25.9 26.6 %collective-permute-start.7 = (bf16[2,32,1664]{2,1,0:T(8,128)(2,1)S(1)}, bf16[2,32,1664]{2,1,0:T(8,128)(2,1)S(1)}, u32[]{:S(2)}, u32[]{:S(2)}) collective-permute-start(bf16[2,32,1664]{2,1,0:T(8,128)(2,1)S(1)} %get-tuple-element.41), channel_id=1, source_target_pairs={{0,10},{2,8},{4,14},{6,12},{8,2},{10,0},{12,6},{14,4},{1,11},{3,9}... | collective-permute-start | bytes 638984 | tf_op jit(solution)/shard_map/ppermute | solution.py:328
  57.5 29.3 %all-to-all-start.2 = ((bf16[16,32,1024]{2,1,0:T(8,128)(2,1)}), bf16[16,32,1024]{2,1,0:T(8,128)(2,1)S(1)}, u32[]{:S(2)}, u32[]{:S(2)}) async-start(bf16[16,32,1024]{2,1,0:T(8,128)(2,1)} %shard_map.148), calls=%async_computation.2 | async-start | bytes 2097152 | tf_op jit(solution)/shard_map/all_to_all | solution.py:362
  61.8 15.7 %collective-permute-start.11 = (bf16[256,256]{1,0:T(8,128)(2,1)S(1)}, bf16[256,256]{1,0:T(8,128)(2,1)S(1)}, u32[]{:S(2)}, u32[]{:S(2)}) collective-permute-start(bf16[256,256]{1,0:T(8,128)(2,1)S(1)} %get-tuple-element.51.refs_0_), channel_id=1, source_target_pairs={{0,64},{64,0},{1,65},{65,1},{2,66},{66,2},{3,67},{67,3},{4,68},{68... | collective-permute-start | bytes 393224 | tf_op jit(solution)/shard_map/ppermute | solution.py:348
  62.3 18.0 %collective-permute-start.8 = (bf16[256,256]{1,0:T(8,128)(2,1)S(1)}, bf16[256,256]{1,0:T(8,128)(2,1)S(1)}, u32[]{:S(2)}, u32[]{:S(2)}) collective-permute-start(bf16[256,256]{1,0:T(8,128)(2,1)S(1)} %get-tuple-element.51.refs_0_), channel_id=1, source_target_pairs={{0,16},{16,32},{32,48},{48,0},{1,17},{17,33},{33,49},{49,1},{2,18}... | collective-permute-start | bytes 393224 | tf_op jit(solution)/shard_map/ppermute | solution.py:368
  62.7 22.9 %collective-permute-start.9 = (bf16[256,256]{1,0:T(8,128)(2,1)S(1)}, bf16[256,256]{1,0:T(8,128)(2,1)S(1)}, u32[]{:S(2)}, u32[]{:S(2)}) collective-permute-start(bf16[256,256]{1,0:T(8,128)(2,1)S(1)} %get-tuple-element.51.refs_0_), channel_id=1, source_target_pairs={{0,48},{16,0},{32,16},{48,32},{1,49},{17,1},{33,17},{49,33},{2,50}... | collective-permute-start | bytes 393224 | tf_op jit(solution)/shard_map/ppermute | solution.py:368
  65.0 20.7 %collective-permute-start.10 = (bf16[256,256]{1,0:T(8,128)(2,1)S(1)}, bf16[256,256]{1,0:T(8,128)(2,1)S(1)}, u32[]{:S(2)}, u32[]{:S(2)}) collective-permute-start(bf16[256,256]{1,0:T(8,128)(2,1)S(1)} %get-tuple-element.51.refs_0_), channel_id=1, source_target_pairs={{0,32},{16,48},{32,0},{48,16},{1,33},{17,49},{33,1},{49,17},{2,34}... | collective-permute-start | bytes 393224 | tf_op jit(solution)/shard_map/ppermute | solution.py:368
  77.6 8.1 %collective-permute-start.12 = (bf16[256,256]{1,0:T(8,128)(2,1)S(1)}, bf16[256,256]{1,0:T(8,128)(2,1)S(1)}, u32[]{:S(2)}, u32[]{:S(2)}) collective-permute-start(bf16[256,256]{1,0:T(8,128)(2,1)S(1)} %collective-permute-done.11.refs_4_), channel_id=1, source_target_pairs={{0,16},{16,32},{32,48},{48,0},{1,17},{17,33},{33,49},{49,1},{2,18}... | collective-permute-start | bytes 393224 | tf_op jit(solution)/shard_map/ppermute | solution.py:368
  78.0 7.6 %collective-permute-start.13 = (bf16[256,256]{1,0:T(8,128)(2,1)S(1)}, bf16[256,256]{1,0:T(8,128)(2,1)S(1)}, u32[]{:S(2)}, u32[]{:S(2)}) collective-permute-start(bf16[256,256]{1,0:T(8,128)(2,1)S(1)} %collective-permute-done.11.refs_4_), channel_id=1, source_target_pairs={{0,48},{16,0},{32,16},{48,32},{1,49},{17,1},{33,17},{49,33},{2,50}... | collective-permute-start | bytes 393224 | tf_op jit(solution)/shard_map/ppermute | solution.py:368
  80.3 5.4 %collective-permute-start.14 = (bf16[256,256]{1,0:T(8,128)(2,1)S(1)}, bf16[256,256]{1,0:T(8,128)(2,1)S(1)}, u32[]{:S(2)}, u32[]{:S(2)}) collective-permute-start(bf16[256,256]{1,0:T(8,128)(2,1)S(1)} %collective-permute-done.11.refs_4_), channel_id=1, source_target_pairs={{0,32},{16,48},{32,0},{48,16},{1,33},{17,49},{33,1},{49,17},{2,34}... | collective-permute-start | bytes 393224 | tf_op jit(solution)/shard_map/ppermute | solution.py:368
  85.6 1.1 %copy-start.1 = (f32[16,4096]{1,0:T(8,128)S(1)}, f32[16,4096]{1,0:T(8,128)}, u32[]{:S(2)}) copy-start(f32[16,4096]{1,0:T(8,128)} %refs_0_.1) | copy-start | bytes 786436
  85.6 1.1 %copy-start.3 = (f32[16,4096]{1,0:T(8,128)S(1)}, f32[16,4096]{1,0:T(8,128)}, u32[]{:S(2)}) copy-start(f32[16,4096]{1,0:T(8,128)} %refs_1_.1) | copy-start | bytes 786436
  85.6 1.4 %copy-start.5 = (f32[16,4096]{1,0:T(8,128)S(1)}, f32[16,4096]{1,0:T(8,128)}, u32[]{:S(2)}) copy-start(f32[16,4096]{1,0:T(8,128)} %refs_2_.1) | copy-start | bytes 786436

commit v7 on v6

--- a/solution.py
+++ b/solution.py
@@ -28,7 +28,8 @@
 WIDE = COLS + STATE
 BACK = COLS + ACOLS // 2
 EARLY = 1
-SHIFT = 5.2
+TOP = 87.0
+POWER = 12.0
 
 CHIP_STEPS = ((1, 0), (3, 0), (2, 0), (0, 1), (1, 1), (3, 1), (2, 1))
 REPLICA_STEPS = (1, 3, 2)
@@ -61,14 +62,19 @@
     return high, (x - high.astype(f32)).astype(bf16)
 
 
-def code(x):
-    size = jnp.exp(6.0 * (jnp.log(jnp.maximum(jnp.abs(x), 1e-30)) + SHIFT))
+def largest(x):
+    return jnp.max(jnp.max(jnp.abs(x), axis=0, keepdims=True), axis=1, keepdims=True)
+
+
+def code(x, most):
+    size = jnp.maximum(jnp.abs(x) / jnp.where(most == 0.0, 1.0, most), 1e-30)
+    size = jnp.exp(POWER * jnp.log(size) + TOP)
     return jnp.where(x < 0.0, -size, size).astype(bf16)
 
 
-def decode(y):
+def decode(y, most):
     y = y.astype(f32)
-    size = jnp.exp(jnp.log(jnp.maximum(jnp.abs(y), 1e-37)) * (1.0 / 6.0) - SHIFT)
+    size = most * jnp.exp((jnp.log(jnp.maximum(jnp.abs(y), 1e-37)) - TOP) * (1.0 / POWER))
     return jnp.where(y == 0.0, 0.0, jnp.where(y < 0.0, -size, size))
 
 
@@ -91,7 +97,9 @@
 
 
 def clip_of(sums_ref):
-    total = jnp.sum(jnp.sum(sums_ref[...], axis=0, keepdims=True), axis=1, keepdims=True)
+    total = jnp.sum(sums_ref[...], axis=0, keepdims=True)
+    lane = lax.broadcasted_iota(jnp.int32, (1, 128), 1)
+    total = jnp.sum(jnp.where(lane < 64, total, 0.0), axis=1, keepdims=True)
     return 1.0 / jnp.sqrt(total / NUMEL + 1e-06)
 
 
@@ -134,7 +142,13 @@
         total = total + arrived[replica].astype(f32)
     summed[...] = total
     squared = jnp.sum((total * total).reshape(32, 8, ACOLS), axis=0)
-    copies[...] = jnp.broadcast_to(part[...] + fold_lanes(squared), (128, 128))
+    lane = lax.broadcasted_iota(jnp.int32, (1, 128), 1)
+    row = part[...] + fold_lanes(squared)
+    row = row + pltpu.roll(row, 64, 1)
+    for group in range(16):
+        top = largest(total[group * AROWS : (group + 1) * AROWS, :])
+        row = jnp.where(lane == 64 + group, top, row)
+    copies[...] = jnp.broadcast_to(row, (128, 128))
 
 
 def sources():
@@ -171,7 +185,8 @@
     for n, (chip, block) in enumerate(zip(sources(), blocks)):
         for core in range(2):
             rows = pl.ds(pl.multiple_of((chip * 2 + core) * AROWS, AROWS), AROWS)
-            scaled = code(clip * attn[rows, :])
+            summed = attn[rows, :]
+            scaled = code(summed, largest(summed))
             weights[n, core, :AROWS, COLS:] = scaled[:, :128]
             weights[n, core, AROWS:, COLS:] = scaled[:, 128:]
         for copy in loads[n]:
@@ -273,14 +288,22 @@
         store.wait()
 
 
-def finish_kernel(arrived, *refs):
+def finish_kernel(sums, arrived, *refs):
     state, weight, outs, news, sem, out_sems = refs[:3], refs[3], refs[4:7], refs[7], refs[8], refs[9]
     stores = [pltpu.make_async_copy(arrived.at[:, :, :COLS], weight, sem)]
     stores[0].start()
+    clip = clip_of(sums)
+    replica = lax.axis_index("gx_0") * 4 + lax.axis_index("gx_1")
+    me = lax.axis_index("gy_0") * 4 + lax.axis_index("gy_1") * 2 + lax.axis_index("gy_2")
+    mine = lax.broadcasted_iota(jnp.int32, (16, 128), 1) == 64 + me
+    tops = sums[pl.ds(pl.multiple_of(replica * 16, 16), 16), :]
+    tops = clip * jnp.sum(jnp.where(mine, tops, 0.0), axis=1, keepdims=True)
     for part in range(4):
         for group in range(4 * part, 4 * part + 4):
             for half in range(2):
-                scaled = decode(arrived[group, half * AROWS : (half + 1) * AROWS, COLS:])
+                scaled = decode(
+                    arrived[group, half * AROWS : (half + 1) * AROWS, COLS:], tops[group : group + 1, :]
+                )
                 cols = lanes(2 * group + half)
                 results = adam_update(
                     scaled, state[0][:, cols], state[1][:, cols], state[2][:, cols], 1.0
@@ -394,14 +417,14 @@
         finish_kernel,
         (pltpu.HBM((16, ROWS, COLS), bf16),) + (pltpu.HBM((AROWS, 16 * ACOLS), f32),) * 3,
         2000000,
-        in_specs=[vmem] * 4,
+        in_specs=[vmem] * 5,
         out_specs=[hbm] * 4,
         scratch_shapes=[
             pltpu.VMEM((3, AROWS, 16 * ACOLS), f32),
             pltpu.SemaphoreType.DMA,
             pltpu.SemaphoreType.DMA((4, 3)),
         ],
-    )(*near(returned), attn_master, attn_moment, attn_second)
+    )(*near(sums, returned), attn_master, attn_moment, attn_second)
     return (
         e_master,
         e_moment,

time: 90 us -> 90.1 us (level)
  transfers between devices with their start and end apart: 17 -> 17, of which waited for: 3 -> 3; matrix products, arithmetic and copies ran while one was open for 0% -> 0% of each run, Pallas kernels for 8% -> 9%
where the time goes in v7:
time: 90.1 us; the launch traced here: 88.4 us
  starting transfers between devices  29.5 us (33%)
  blocking collectives  24.9 us (28%)
  Pallas kernels  15 us (17%)
  waiting for transfers between devices  13.9 us (15%)
  local copies, waits for them, and re-layouts  4.27 us (5%)
    all_to_all x1, blocking collectives, local(): lax.all_to_all(partial.reshape(128, 1, 128), GX_GY, split_axis=0, concat_...  24.9 us
    ppermute x7, starting transfers between devices, local(): blocks.append(lax.ppermute(routed[n + 1], GY[:2], chip_pairs(*step)))  12.7 us
    ppermute x1, waiting for transfers between devices, local(): other = lax.ppermute(attn_block, 'gx_0', [(0, 1), (1, 0)])  12.6 us
    ppermute x6, starting transfers between devices, local(): lax.ppermute(block, 'gx_1', [(y, (y + dy) % 4) for y in range(4)])  5.36 us
    pallas_call x1, Pallas kernels, local(): call(expert_state_kernel, (pltpu.HBM((ROWS, 16 * COLS), f32),) * 3, 80000...  5.31 us
    all_to_all x1, starting transfers between devices, local(): lax.all_to_all(attn_grad.reshape(8, 256, ACOLS), GX, split_axis=0, concat...  5.23 us
    all_to_all x1, starting transfers between devices, local(): lax.all_to_all(weights, GY, split_axis=0, concat_axis=0, tiled=True)  4.37 us
    unnamed x14, local copies, waits for them, and re-layouts  4.27 us
  transfers between devices with their start and end apart: 17, of which 3 were waited for; matrix products, arithmetic and copies ran while one was open for 0% of the time, Pallas kernels for 9%

profile of v7, /device:TPU:1, one launch (start us, length us, event | category | flops | bytes accessed | tf_op | source)
XLA Modules:
  0.0 88.4 jit_solution(18101144929636804941)
XLA Ops:
  0.6 0.0 copy-start
  0.6 0.9 %copy-done = f32[16,4096]{1,0:T(8,128)S(1)} copy-done((f32[16,4096]{1,0:T(8,128)S(1)}, f32[16,4096]{1,0:T(8,128)}, u32[]{:S(2)}) %copy-start) | copy-done | bytes 262168
  1.6 0.0 copy-start.2
  1.6 0.9 %copy-done.2 = f32[16,4096]{1,0:T(8,128)S(1)} copy-done((f32[16,4096]{1,0:T(8,128)S(1)}, f32[16,4096]{1,0:T(8,128)}, u32[]{:S(2)}) %copy-start.2) | copy-done | bytes 262168
  2.5 0.0 copy-start.4
  2.5 0.9 %copy-done.4 = f32[16,4096]{1,0:T(8,128)S(1)} copy-done((f32[16,4096]{1,0:T(8,128)S(1)}, f32[16,4096]{1,0:T(8,128)}, u32[]{:S(2)}) %copy-start.4) | copy-done | bytes 262168
  3.5 0.0 copy-start.6
  3.5 1.2 %copy-done.6 = bf16[1,512,896]{2,1,0:T(8,128)(2,1)S(1)} copy-done((bf16[1,512,896]{2,1,0:T(8,128)(2,1)S(1)}, bf16[1,512,896]{2,1,0:T(8,128)(2,1)}, u32[]{:S(2)}) %copy-start.6) | copy-done | bytes 917528
  4.7 1.1 %shard_map.143 = (bf16[8,32,1664]{2,1,0:T(8,128)(2,1)S(1)}, bf16[8,32,1664]{2,1,0:T(8,128)(2,1)}, f32[1,128]{1,0:T(1,128)S(1)}) custom-call(bf16[16,32,896]{2,1,0:T(8,128)(2,1)S(1)} %bitcast.12, f32[16,4096]{1,0:T(8,128)S(1)} %copy-done, f32[16,4096]{1,0:T(8,128)S(1)} %copy-done.2, f32[16,4096]{1,0:T(8,128)S(1)} %copy-done.4), custom_call_target="tpu_custom_call" | custom-call | flops 4000000 | bytes 4096 | tf_op jit(solution)/shard_map/pallas_call | solution.py:342
  5.8 1.4 %collective-permute-start = (bf16[8,32,1664]{2,1,0:T(8,128)(2,1)}, bf16[8,32,1664]{2,1,0:T(8,128)(2,1)S(1)}, u32[]{:S(2)}, u32[]{:S(2)}) collective-permute-start(bf16[8,32,1664]{2,1,0:T(8,128)(2,1)} %get-tuple-element.33), channel_id=1, source_target_pairs={{0,1},{1,0},{2,3},{3,2},{4,5},{5,4},{6,7},{7,6},{8,9},{9,8},{10,11... | collective-permute-start | bytes 2555912 | tf_op jit(solution)/shard_map/ppermute | solution.py:347
  7.2 5.2 %all-to-all-start = ((bf16[8,256,256]{2,1,0:T(8,128)(2,1)}), bf16[8,256,256]{2,1,0:T(8,128)(2,1)S(1)}, u32[]{:S(2)}, u32[]{:S(2)}) async-start(bf16[8,256,256]{2,1,0:T(8,128)(2,1)} %bitcast.14), calls=%async_computation | async-start | bytes 2097152 | tf_op jit(solution)/shard_map/all_to_all | solution.py:338
  12.4 0.0 collective-permute-done.swapped
  12.4 0.9 %shard_map.145 = (bf16[2,32,1664]{2,1,0:T(8,128)(2,1)S(1)}, bf16[2,32,1664]{2,1,0:T(8,128)(2,1)S(1)}, bf16[2,32,1664]{2,1,0:T(8,128)(2,1)S(1)}, bf16[2,32,1664]{...) custom-call(bf16[8,32,1664]{2,1,0:T(8,128)(2,1)S(1)} %get-tuple-elem, ...), custom_call_target="tpu_custom_call" | custom-call | flops 1000000 | bytes 4096 | tf_op jit(solution)/shard_map/pallas_call | solution.py:348
  13.3 1.6 %collective-permute-start.1 = (bf16[2,32,1664]{2,1,0:T(8,128)(2,1)S(1)}, bf16[2,32,1664]{2,1,0:T(8,128)(2,1)S(1)}, u32[]{:S(2)}, u32[]{:S(2)}) collective-permute-start(bf16[2,32,1664]{2,1,0:T(8,128)(2,1)S(1)} %get-tuple-element.35), channel_id=1, source_target_pairs={{0,4},{2,6},{4,8},{6,10},{8,12},{10,14},{12,0},{14,2},{1,5},{3,7},... | collective-permute-start | bytes 638984 | tf_op jit(solution)/shard_map/ppermute | solution.py:351
  15.0 2.1 %collective-permute-start.2 = (bf16[2,32,1664]{2,1,0:T(8,128)(2,1)S(1)}, bf16[2,32,1664]{2,1,0:T(8,128)(2,1)S(1)}, u32[]{:S(2)}, u32[]{:S(2)}) collective-permute-start(bf16[2,32,1664]{2,1,0:T(8,128)(2,1)S(1)} %get-tuple-element.36), channel_id=1, source_target_pairs={{0,12},{2,14},{4,0},{6,2},{8,4},{10,6},{12,8},{14,10},{1,13},{3,15... | collective-permute-start | bytes 638984 | tf_op jit(solution)/shard_map/ppermute | solution.py:351
  17.1 1.3 %collective-permute-start.3 = (bf16[2,32,1664]{2,1,0:T(8,128)(2,1)}, bf16[2,32,1664]{2,1,0:T(8,128)(2,1)S(1)}, u32[]{:S(2)}, u32[]{:S(2)}) collective-permute-start(bf16[2,32,1664]{2,1,0:T(8,128)(2,1)} %get-tuple-element.37), channel_id=1, source_target_pairs={{0,8},{2,10},{4,12},{6,14},{8,0},{10,2},{12,4},{14,6},{1,9},{3,11}... | collective-permute-start | bytes 638984 | tf_op jit(solution)/shard_map/ppermute | solution.py:351
  18.4 2.5 %collective-permute-start.4 = (bf16[2,32,1664]{2,1,0:T(8,128)(2,1)}, bf16[2,32,1664]{2,1,0:T(8,128)(2,1)S(1)}, u32[]{:S(2)}, u32[]{:S(2)}) collective-permute-start(bf16[2,32,1664]{2,1,0:T(8,128)(2,1)} %get-tuple-element.38), channel_id=1, source_target_pairs={{0,2},{2,0},{4,6},{6,4},{8,10},{10,8},{12,14},{14,12},{1,3},{3,1},... | collective-permute-start | bytes 638984 | tf_op jit(solution)/shard_map/ppermute | solution.py:351
  20.8 1.0 %collective-permute-start.5 = (bf16[2,32,1664]{2,1,0:T(8,128)(2,1)}, bf16[2,32,1664]{2,1,0:T(8,128)(2,1)S(1)}, u32[]{:S(2)}, u32[]{:S(2)}) collective-permute-start(bf16[2,32,1664]{2,1,0:T(8,128)(2,1)} %get-tuple-element.39), channel_id=1, source_target_pairs={{0,6},{2,4},{4,10},{6,8},{8,14},{10,12},{12,2},{14,0},{1,7},{3,5},... | collective-permute-start | bytes 638984 | tf_op jit(solution)/shard_map/ppermute | solution.py:351
  21.8 0.6 collective-permute-done.1.refs_1_
  22.4 3.5 %collective-permute-start.6 = (bf16[2,32,1664]{2,1,0:T(8,128)(2,1)S(1)}, bf16[2,32,1664]{2,1,0:T(8,128)(2,1)S(1)}, u32[]{:S(2)}, u32[]{:S(2)}) collective-permute-start(bf16[2,32,1664]{2,1,0:T(8,128)(2,1)S(1)} %get-tuple-element.40), channel_id=1, source_target_pairs={{0,14},{2,12},{4,2},{6,0},{8,6},{10,4},{12,10},{14,8},{1,15},{3,13... | collective-permute-start | bytes 638984 | tf_op jit(solution)/shard_map/ppermute | solution.py:351
  25.9 0.0 collective-permute-done.2.refs_2_
  25.9 0.8 collective-permute-start.7
  26.7 0.7 all-to-all-done.arrived
  27.4 0.3 shard_map.144
  27.6 24.9 %all_to_all.15 = f32[128,1,128]{2,1,0:T(1,128)S(1)} all-to-all(f32[128,1,128]{2,1,0:T(1,128)S(1)} %bitcast.13), channel_id=1, replica_groups=mesh['gx_0'=2,'gx_1'=4,'gy_0'=4,'gy_1'=2,'gy_2'=2] {'gx_0','gx_1','gy_0'..., dimensions={0} | all-to-all | bytes 131072 | tf_op jit(solution)/shard_map/all_to_all | solution.py:356
  52.5 0.0 collective-permute-done.3.refs_3_
  52.5 0.0 collective-permute-done.4.refs_4_
  52.5 0.0 collective-permute-done.5.refs_5_
  52.5 0.0 collective-permute-done.6.refs_6_
  52.5 0.0 collective-permute-done.7.refs_7_
  52.6 1.2 %shard_map.147 = (bf16[256,256]{1,0:T(8,128)(2,1)S(1)}, f32[3,1,32,1792]{3,2,1,0:T(8,128)S(1)}) custom-call(f32[128,128]{1,0:T(8,128)S(1)} %bitcast.8, f32[256,256]{1,0:T(8,128)S(1)} %get-tuple-element.45.attn, bf16[2,32,1664]{2,1,0:T(8,128)(2,1)S(1)} %get-tuple-element.34.refs_0_, bf16[2,32,1664]{2,1,0:T(8,128)(2,1)S(1)} %collective-permute-done.1.refs_1_, ...), custom_call_target="tpu_custom_call" | custom-call | flops 2000000 | bytes 4096 | tf_op jit(solution)/shard_map/pallas_call | solution.py:363
  53.8 3.7 %shard_map.148 = bf16[16,32,1024]{2,1,0:T(8,128)(2,1)} custom-call(f32[128,128]{1,0:T(8,128)S(1)} %bitcast.9, f32[256,256]{1,0:T(8,128)S(1)} %get-tuple-element.45.attn, bf16[2,32,1664]{2,1,0:T(8,128)(2,1)S(1)} %get-tuple-element.34.refs_0_, bf16[2,32,1664]{2,1,0:T(8,128)(2,1)S(1)} %collective-permute-done.1.refs_1_, ...), custom_call_target="tpu_custom_call" | custom-call | flops 8000000 | bytes 4096 | tf_op jit(solution)/shard_map/pallas_call | solution.py:372
  57.5 4.4 %all-to-all-start.2 = ((bf16[16,32,1024]{2,1,0:T(8,128)(2,1)}), bf16[16,32,1024]{2,1,0:T(8,128)(2,1)S(1)}, u32[]{:S(2)}, u32[]{:S(2)}) async-start(bf16[16,32,1024]{2,1,0:T(8,128)(2,1)} %shard_map.148), calls=%async_computation.2 | async-start | bytes 2097152 | tf_op jit(solution)/shard_map/all_to_all | solution.py:385
  61.8 0.5 collective-permute-start.11
  62.3 0.4 collective-permute-start.8
  62.7 2.2 %collective-permute-start.9 = (bf16[256,256]{1,0:T(8,128)(2,1)S(1)}, bf16[256,256]{1,0:T(8,128)(2,1)S(1)}, u32[]{:S(2)}, u32[]{:S(2)}) collective-permute-start(bf16[256,256]{1,0:T(8,128)(2,1)S(1)} %get-tuple-element.51.refs_0_), channel_id=1, source_target_pairs={{0,48},{16,0},{32,16},{48,32},{1,49},{17,1},{33,17},{49,33},{2,50}... | collective-permute-start | bytes 393224 | tf_op jit(solution)/shard_map/ppermute | solution.py:391
  65.0 0.0 collective-permute-start.10
  65.0 12.6 %collective-permute-done.11.refs_4_ = bf16[256,256]{1,0:T(8,128)(2,1)S(1)} collective-permute-done((bf16[256,256]{1,0:T(8,128)(2,1)S(1)}, bf16[256,256]{1,0:T(8,128)(2,1)S(1)}, u32[]{:S(2)}, u32[]{:S(2)}) %collective-permute-start.11) | collective-permute-done | bytes 131104 | tf_op jit(solution)/shard_map/ppermute | solution.py:371
  77.6 0.5 collective-permute-start.12
  78.0 2.2 %collective-permute-start.13 = (bf16[256,256]{1,0:T(8,128)(2,1)S(1)}, bf16[256,256]{1,0:T(8,128)(2,1)S(1)}, u32[]{:S(2)}, u32[]{:S(2)}) collective-permute-start(bf16[256,256]{1,0:T(8,128)(2,1)S(1)} %collective-permute-done.11.refs_4_), channel_id=1, source_target_pairs={{0,48},{16,0},{32,16},{48,32},{1,49},{17,1},{33,17},{49,33},{2,50}... | collective-permute-start | bytes 393224 | tf_op jit(solution)/shard_map/ppermute | solution.py:391
  80.2 0.0 collective-permute-done.8.refs_1_
  80.2 0.0 collective-permute-start.14
  80.2 5.3 %shard_map.146 = (f32[32,14336]{1,0:T(8,128)}, f32[32,14336]{1,0:T(8,128)}, f32[32,14336]{1,0:T(8,128)}) custom-call(f32[128,128]{1,0:T(8,128)S(1)} %bitcast.10, bf16[2,32,1664]{2,1,0:T(8,128)(2,1)S(1)} %get-tuple-element.34.refs_0_, bf16[2,32,1664]{2,1,0:T(8,128)(2,1)S(1)} %collective-permute-done.1.refs_1_, ...), custom_call_target="tpu_custom_call" | custom-call | flops 8000000 | bytes 4096 | tf_op jit(solution)/shard_map/pallas_call | solution.py:393
  85.6 0.0 copy-start.1
  85.6 0.0 copy-start.3
  85.6 0.0 copy-start.5
  85.6 0.0 collective-permute-done.9.refs_2_
  85.6 0.0 collective-permute-done.10.refs_3_
  85.6 0.0 collective-permute-done.12.refs_5_
  85.6 0.0 collective-permute-done.13.refs_6_
  85.6 0.0 collective-permute-done.14.refs_7_
  85.7 1.0 %shard_map.150 = bf16[8,256,256]{2,1,0:T(8,128)(2,1)} custom-call(bf16[256,256]{1,0:T(8,128)(2,1)S(1)} %get-tuple-element.51.refs_0_, bf16[256,256]{1,0:T(8,128)(2,1)S(1)} %collective-permute-done.8.refs_1_, bf16[256,256]{1,0:T(8,128)(2,1)S(1)} %collective-permute-done.9.refs_2_, bf16[256,256]{1,0:T(8,128)(2,1)S(1)} %collective-permute-done.10.refs_3_, ...), custom_call_target="tpu_custom_call" | custom-call | flops 1000000 | bytes 4096 | tf_op jit(solution)/shard_map/pallas_call | solution.py:408
  86.7 0.0 all-to-all-done.2.arrived
  86.7 0.0 copy-done.1
  86.7 0.0 copy-done.3
  86.7 0.2 copy-done.5
  87.0 1.5 %shard_map.149 = (bf16[16,32,896]{2,1,0:T(8,128)(2,1)}, f32[16,4096]{1,0:T(8,128)}, f32[16,4096]{1,0:T(8,128)}, f32[16,4096]{1,0:T(8,128)}) custom-call(f32[128,128]{1,0:T(8,128)S(1)} %bitcast.11, bf16[16,32,1024]{2,1,0:T(8,128)(2,1)S(1)} %all-to-all-done.2.arrived, f32[16,4096]{1,0:T(8,128)S(1)} %copy-done.1, f32[16,4096]{1,0:T(8,128)S(1)} %copy-done.3, ...), custom_call_target="tpu_custom_call" | custom-call | flops 2000000 | bytes 4096 | tf_op jit(solution)/shard_map/pallas_call | solution.py:416
Async XLA Ops:
  0.6 1.0 %copy-start = (f32[16,4096]{1,0:T(8,128)S(1)}, f32[16,4096]{1,0:T(8,128)}, u32[]{:S(2)}) copy-start(f32[16,4096]{1,0:T(8,128)} %refs_0_.1) | copy-start | bytes 786436
  1.6 0.9 %copy-start.2 = (f32[16,4096]{1,0:T(8,128)S(1)}, f32[16,4096]{1,0:T(8,128)}, u32[]{:S(2)}) copy-start(f32[16,4096]{1,0:T(8,128)} %refs_1_.1) | copy-start | bytes 786436
  2.5 0.9 %copy-start.4 = (f32[16,4096]{1,0:T(8,128)S(1)}, f32[16,4096]{1,0:T(8,128)}, u32[]{:S(2)}) copy-start(f32[16,4096]{1,0:T(8,128)} %refs_2_.1) | copy-start | bytes 786436
  3.5 1.2 %copy-start.6 = (bf16[1,512,896]{2,1,0:T(8,128)(2,1)S(1)}, bf16[1,512,896]{2,1,0:T(8,128)(2,1)}, u32[]{:S(2)}) copy-start(bf16[1,512,896]{2,1,0:T(8,128)(2,1)} %param.8) | copy-start | bytes 2752516
  5.8 6.6 %collective-permute-start = (bf16[8,32,1664]{2,1,0:T(8,128)(2,1)}, bf16[8,32,1664]{2,1,0:T(8,128)(2,1)S(1)}, u32[]{:S(2)}, u32[]{:S(2)}) collective-permute-start(bf16[8,32,1664]{2,1,0:T(8,128)(2,1)} %get-tuple-element.33), channel_id=1, source_target_pairs={{0,1},{1,0},{2,3},{3,2},{4,5},{5,4},{6,7},{7,6},{8,9},{9,8},{10,11... | collective-permute-start | bytes 2555912 | tf_op jit(solution)/shard_map/ppermute | solution.py:347
  7.2 20.2 %all-to-all-start = ((bf16[8,256,256]{2,1,0:T(8,128)(2,1)}), bf16[8,256,256]{2,1,0:T(8,128)(2,1)S(1)}, u32[]{:S(2)}, u32[]{:S(2)}) async-start(bf16[8,256,256]{2,1,0:T(8,128)(2,1)} %bitcast.14), calls=%async_computation | async-start | bytes 2097152 | tf_op jit(solution)/shard_map/all_to_all | solution.py:338
  13.3 9.1 %collective-permute-start.1 = (bf16[2,32,1664]{2,1,0:T(8,128)(2,1)S(1)}, bf16[2,32,1664]{2,1,0:T(8,128)(2,1)S(1)}, u32[]{:S(2)}, u32[]{:S(2)}) collective-permute-start(bf16[2,32,1664]{2,1,0:T(8,128)(2,1)S(1)} %get-tuple-element.35), channel_id=1, source_target_pairs={{0,4},{2,6},{4,8},{6,10},{8,12},{10,14},{12,0},{14,2},{1,5},{3,7},... | collective-permute-start | bytes 638984 | tf_op jit(solution)/shard_map/ppermute | solution.py:351
  15.0 11.0 %collective-permute-start.2 = (bf16[2,32,1664]{2,1,0:T(8,128)(2,1)S(1)}, bf16[2,32,1664]{2,1,0:T(8,128)(2,1)S(1)}, u32[]{:S(2)}, u32[]{:S(2)}) collective-permute-start(bf16[2,32,1664]{2,1,0:T(8,128)(2,1)S(1)} %get-tuple-element.36), channel_id=1, source_target_pairs={{0,12},{2,14},{4,0},{6,2},{8,4},{10,6},{12,8},{14,10},{1,13},{3,15... | collective-permute-start | bytes 638984 | tf_op jit(solution)/shard_map/ppermute | solution.py:351
  17.1 35.4 %collective-permute-start.3 = (bf16[2,32,1664]{2,1,0:T(8,128)(2,1)}, bf16[2,32,1664]{2,1,0:T(8,128)(2,1)S(1)}, u32[]{:S(2)}, u32[]{:S(2)}) collective-permute-start(bf16[2,32,1664]{2,1,0:T(8,128)(2,1)} %get-tuple-element.37), channel_id=1, source_target_pairs={{0,8},{2,10},{4,12},{6,14},{8,0},{10,2},{12,4},{14,6},{1,9},{3,11}... | collective-permute-start | bytes 638984 | tf_op jit(solution)/shard_map/ppermute | solution.py:351
  18.4 34.1 %collective-permute-start.4 = (bf16[2,32,1664]{2,1,0:T(8,128)(2,1)}, bf16[2,32,1664]{2,1,0:T(8,128)(2,1)S(1)}, u32[]{:S(2)}, u32[]{:S(2)}) collective-permute-start(bf16[2,32,1664]{2,1,0:T(8,128)(2,1)} %get-tuple-element.38), channel_id=1, source_target_pairs={{0,2},{2,0},{4,6},{6,4},{8,10},{10,8},{12,14},{14,12},{1,3},{3,1},... | collective-permute-start | bytes 638984 | tf_op jit(solution)/shard_map/ppermute | solution.py:351
  20.8 31.7 %collective-permute-start.5 = (bf16[2,32,1664]{2,1,0:T(8,128)(2,1)}, bf16[2,32,1664]{2,1,0:T(8,128)(2,1)S(1)}, u32[]{:S(2)}, u32[]{:S(2)}) collective-permute-start(bf16[2,32,1664]{2,1,0:T(8,128)(2,1)} %get-tuple-element.39), channel_id=1, source_target_pairs={{0,6},{2,4},{4,10},{6,8},{8,14},{10,12},{12,2},{14,0},{1,7},{3,5},... | collective-permute-start | bytes 638984 | tf_op jit(solution)/shard_map/ppermute | solution.py:351
  22.4 30.1 %collective-permute-start.6 = (bf16[2,32,1664]{2,1,0:T(8,128)(2,1)S(1)}, bf16[2,32,1664]{2,1,0:T(8,128)(2,1)S(1)}, u32[]{:S(2)}, u32[]{:S(2)}) collective-permute-start(bf16[2,32,1664]{2,1,0:T(8,128)(2,1)S(1)} %get-tuple-element.40), channel_id=1, source_target_pairs={{0,14},{2,12},{4,2},{6,0},{8,6},{10,4},{12,10},{14,8},{1,15},{3,13... | collective-permute-start | bytes 638984 | tf_op jit(solution)/shard_map/ppermute | solution.py:351
  25.9 26.6 %collective-permute-start.7 = (bf16[2,32,1664]{2,1,0:T(8,128)(2,1)S(1)}, bf16[2,32,1664]{2,1,0:T(8,128)(2,1)S(1)}, u32[]{:S(2)}, u32[]{:S(2)}) collective-permute-start(bf16[2,32,1664]{2,1,0:T(8,128)(2,1)S(1)} %get-tuple-element.41), channel_id=1, source_target_pairs={{0,10},{2,8},{4,14},{6,12},{8,2},{10,0},{12,6},{14,4},{1,11},{3,9}... | collective-permute-start | bytes 638984 | tf_op jit(solution)/shard_map/ppermute | solution.py:351
  57.5 29.2 %all-to-all-start.2 = ((bf16[16,32,1024]{2,1,0:T(8,128)(2,1)}), bf16[16,32,1024]{2,1,0:T(8,128)(2,1)S(1)}, u32[]{:S(2)}, u32[]{:S(2)}) async-start(bf16[16,32,1024]{2,1,0:T(8,128)(2,1)} %shard_map.148), calls=%async_computation.2 | async-start | bytes 2097152 | tf_op jit(solution)/shard_map/all_to_all | solution.py:385
  61.8 15.7 %collective-permute-start.11 = (bf16[256,256]{1,0:T(8,128)(2,1)S(1)}, bf16[256,256]{1,0:T(8,128)(2,1)S(1)}, u32[]{:S(2)}, u32[]{:S(2)}) collective-permute-start(bf16[256,256]{1,0:T(8,128)(2,1)S(1)} %get-tuple-element.51.refs_0_), channel_id=1, source_target_pairs={{0,64},{64,0},{1,65},{65,1},{2,66},{66,2},{3,67},{67,3},{4,68},{68... | collective-permute-start | bytes 393224 | tf_op jit(solution)/shard_map/ppermute | solution.py:371
  62.3 18.0 %collective-permute-start.8 = (bf16[256,256]{1,0:T(8,128)(2,1)S(1)}, bf16[256,256]{1,0:T(8,128)(2,1)S(1)}, u32[]{:S(2)}, u32[]{:S(2)}) collective-permute-start(bf16[256,256]{1,0:T(8,128)(2,1)S(1)} %get-tuple-element.51.refs_0_), channel_id=1, source_target_pairs={{0,16},{16,32},{32,48},{48,0},{1,17},{17,33},{33,49},{49,1},{2,18}... | collective-permute-start | bytes 393224 | tf_op jit(solution)/shard_map/ppermute | solution.py:391
  62.7 22.9 %collective-permute-start.9 = (bf16[256,256]{1,0:T(8,128)(2,1)S(1)}, bf16[256,256]{1,0:T(8,128)(2,1)S(1)}, u32[]{:S(2)}, u32[]{:S(2)}) collective-permute-start(bf16[256,256]{1,0:T(8,128)(2,1)S(1)} %get-tuple-element.51.refs_0_), channel_id=1, source_target_pairs={{0,48},{16,0},{32,16},{48,32},{1,49},{17,1},{33,17},{49,33},{2,50}... | collective-permute-start | bytes 393224 | tf_op jit(solution)/shard_map/ppermute | solution.py:391
  65.0 20.7 %collective-permute-start.10 = (bf16[256,256]{1,0:T(8,128)(2,1)S(1)}, bf16[256,256]{1,0:T(8,128)(2,1)S(1)}, u32[]{:S(2)}, u32[]{:S(2)}) collective-permute-start(bf16[256,256]{1,0:T(8,128)(2,1)S(1)} %get-tuple-element.51.refs_0_), channel_id=1, source_target_pairs={{0,32},{16,48},{32,0},{48,16},{1,33},{17,49},{33,1},{49,17},{2,34}... | collective-permute-start | bytes 393224 | tf_op jit(solution)/shard_map/ppermute | solution.py:391
  77.6 8.1 %collective-permute-start.12 = (bf16[256,256]{1,0:T(8,128)(2,1)S(1)}, bf16[256,256]{1,0:T(8,128)(2,1)S(1)}, u32[]{:S(2)}, u32[]{:S(2)}) collective-permute-start(bf16[256,256]{1,0:T(8,128)(2,1)S(1)} %collective-permute-done.11.refs_4_), channel_id=1, source_target_pairs={{0,16},{16,32},{32,48},{48,0},{1,17},{17,33},{33,49},{49,1},{2,18}... | collective-permute-start | bytes 393224 | tf_op jit(solution)/shard_map/ppermute | solution.py:391
  78.0 7.6 %collective-permute-start.13 = (bf16[256,256]{1,0:T(8,128)(2,1)S(1)}, bf16[256,256]{1,0:T(8,128)(2,1)S(1)}, u32[]{:S(2)}, u32[]{:S(2)}) collective-permute-start(bf16[256,256]{1,0:T(8,128)(2,1)S(1)} %collective-permute-done.11.refs_4_), channel_id=1, source_target_pairs={{0,48},{16,0},{32,16},{48,32},{1,49},{17,1},{33,17},{49,33},{2,50}... | collective-permute-start | bytes 393224 | tf_op jit(solution)/shard_map/ppermute | solution.py:391
  80.2 5.4 %collective-permute-start.14 = (bf16[256,256]{1,0:T(8,128)(2,1)S(1)}, bf16[256,256]{1,0:T(8,128)(2,1)S(1)}, u32[]{:S(2)}, u32[]{:S(2)}) collective-permute-start(bf16[256,256]{1,0:T(8,128)(2,1)S(1)} %collective-permute-done.11.refs_4_), channel_id=1, source_target_pairs={{0,32},{16,48},{32,0},{48,16},{1,33},{17,49},{33,1},{49,17},{2,34}... | collective-permute-start | bytes 393224 | tf_op jit(solution)/shard_map/ppermute | solution.py:391
  85.6 1.1 %copy-start.1 = (f32[16,4096]{1,0:T(8,128)S(1)}, f32[16,4096]{1,0:T(8,128)}, u32[]{:S(2)}) copy-start(f32[16,4096]{1,0:T(8,128)} %refs_0_.1) | copy-start | bytes 786436
  85.6 1.1 %copy-start.3 = (f32[16,4096]{1,0:T(8,128)S(1)}, f32[16,4096]{1,0:T(8,128)}, u32[]{:S(2)}) copy-start(f32[16,4096]{1,0:T(8,128)} %refs_1_.1) | copy-start | bytes 786436
  85.6 1.4 %copy-start.5 = (f32[16,4096]{1,0:T(8,128)S(1)}, f32[16,4096]{1,0:T(8,128)}, u32[]{:S(2)}) copy-start(f32[16,4096]{1,0:T(8,128)} %refs_2_.1) | copy-start | bytes 786436

commit v8 on v7

--- a/solution.py
+++ b/solution.py
@@ -24,12 +24,13 @@
 
 ROWS, COLS = 32, 896
 AROWS, ACOLS = 16, 256
-STATE = 3 * ACOLS
+STATE = 2 * ACOLS + ACOLS // 2
 WIDE = COLS + STATE
 BACK = COLS + ACOLS // 2
 EARLY = 1
 TOP = 87.0
 POWER = 12.0
+MIDDLE = -0.458
 
 CHIP_STEPS = ((1, 0), (3, 0), (2, 0), (0, 1), (1, 1), (3, 1), (2, 1))
 REPLICA_STEPS = (1, 3, 2)
@@ -76,6 +77,14 @@
     y = y.astype(f32)
     size = most * jnp.exp((jnp.log(jnp.maximum(jnp.abs(y), 1e-37)) - TOP) * (1.0 / POWER))
     return jnp.where(y == 0.0, 0.0, jnp.where(y < 0.0, -size, size))
+
+
+def code_second(x):
+    return jnp.exp(40.0 * (jnp.log(x) - MIDDLE)).astype(bf16)
+
+
+def decode_second(y):
+    return jnp.exp(jnp.log(y.astype(f32)) * (1.0 / 40.0) + MIDDLE)
 
 
 def adam_update(gradient, master, moment, second, clip_factor):
@@ -120,11 +129,14 @@
             wide = rows.astype(f32)
             total = total + jnp.sum((wide * wide).reshape(ROWS // 8, 8, COLS), axis=0)
             cols = pl.ds(pl.multiple_of((2 * chip + which) * ACOLS, ACOLS), ACOLS)
-            for n, state in enumerate((master, moment, second)):
+            for n, state in enumerate((master, moment)):
                 high, low = halves(state[:, cols])
                 at = COLS + n * ACOLS
                 out[chip, :AROWS, at : at + ACOLS] = high
                 out[chip, AROWS:, at : at + ACOLS] = low
+            coded = code_second(second[:, cols])
+            out[chip, :AROWS, COLS + 2 * ACOLS :] = coded[:, :128]
+            out[chip, AROWS:, COLS + 2 * ACOLS :] = coded[:, 128:]
     part[...] = fold_lanes(total)
 
 
@@ -261,15 +273,18 @@
     for chip, block in zip(sources(), blocks):
         for core in range(2):
             rows = pl.ds(pl.multiple_of((chip * 2 + core) * AROWS, AROWS), AROWS)
-            came = block[core, :AROWS, COLS:].astype(f32) + block[core, AROWS:, COLS:].astype(f32)
-            new = adam_weight(
-                attn[rows, :],
-                came[:, :ACOLS],
-                came[:, ACOLS : 2 * ACOLS],
-                came[:, 2 * ACOLS :],
-                clip,
-            )
-            out[rows, :] = new.astype(bf16)
+            pair = COLS + 2 * ACOLS
+            came = block[core, :AROWS, COLS:pair].astype(f32) + block[core, AROWS:, COLS:pair].astype(f32)
+            for half in range(2):
+                cols = lanes(half)
+                new = adam_weight(
+                    attn[rows, cols],
+                    came[:, cols],
+                    came[:, lanes(2 + half)],
+                    decode_second(block[core, half * AROWS : (half + 1) * AROWS, pair:]),
+                    clip,
+                )
+                out[rows, cols] = new.astype(bf16)
     for copy in loads:
         copy.wait()
 

time: 90.1 us -> 88.6 us (0.983)
  blocking collectives: 24.9 us -> 23.5 us
    all_to_all x1, blocking collectives: 24.9 us -> 23.5 us  [local(): lax.all_to_all(partial.reshape(128, 1, 128), GX_GY, split_axis=0, concat_...]
where the time goes in v8:
time: 88.6 us; the launch traced here: 87 us
  starting transfers between devices  29.8 us (34%)
  blocking collectives  23.5 us (27%)
  Pallas kernels  14.9 us (17%)
  waiting for transfers between devices  13.7 us (15%)
  local copies, waits for them, and re-layouts  4.27 us (5%)
    all_to_all x1, blocking collectives, local(): lax.all_to_all(partial.reshape(128, 1, 128), GX_GY, split_axis=0, concat_...  23.5 us
    ppermute x7, starting transfers between devices, local(): blocks.append(lax.ppermute(routed[n + 1], GY[:2], chip_pairs(*step)))  13 us
    ppermute x1, waiting for transfers between devices, local(): other = lax.ppermute(attn_block, 'gx_0', [(0, 1), (1, 0)])  12.6 us
    ppermute x6, starting transfers between devices, local(): lax.ppermute(block, 'gx_1', [(y, (y + dy) % 4) for y in range(4)])  5.36 us
    pallas_call x1, Pallas kernels, local(): call(expert_state_kernel, (pltpu.HBM((ROWS, 16 * COLS), f32),) * 3, 80000...  5.31 us
    all_to_all x1, starting transfers between devices, local(): lax.all_to_all(attn_grad.reshape(8, 256, ACOLS), GX, split_axis=0, concat...  5.23 us
    all_to_all x1, starting transfers between devices, local(): lax.all_to_all(weights, GY, split_axis=0, concat_axis=0, tiled=True)  4.38 us
    unnamed x14, local copies, waits for them, and re-layouts  4.27 us
  transfers between devices with their start and end apart: 17, of which 3 were waited for; matrix products, arithmetic and copies ran while one was open for 0% of the time, Pallas kernels for 9%

profile of v8, /device:TPU:1, one launch (start us, length us, event | category | flops | bytes accessed | tf_op | source)
XLA Modules:
  0.0 87.0 jit_solution(8763696284733612419)
XLA Ops:
  0.6 0.0 copy-start
  0.6 0.9 %copy-done = f32[16,4096]{1,0:T(8,128)S(1)} copy-done((f32[16,4096]{1,0:T(8,128)S(1)}, f32[16,4096]{1,0:T(8,128)}, u32[]{:S(2)}) %copy-start) | copy-done | bytes 262168
  1.6 0.0 copy-start.2
  1.6 0.9 %copy-done.2 = f32[16,4096]{1,0:T(8,128)S(1)} copy-done((f32[16,4096]{1,0:T(8,128)S(1)}, f32[16,4096]{1,0:T(8,128)}, u32[]{:S(2)}) %copy-start.2) | copy-done | bytes 262168
  2.5 0.0 copy-start.4
  2.5 0.9 %copy-done.4 = f32[16,4096]{1,0:T(8,128)S(1)} copy-done((f32[16,4096]{1,0:T(8,128)S(1)}, f32[16,4096]{1,0:T(8,128)}, u32[]{:S(2)}) %copy-start.4) | copy-done | bytes 262168
  3.5 0.0 copy-start.6
  3.5 1.2 %copy-done.6 = bf16[1,512,896]{2,1,0:T(8,128)(2,1)S(1)} copy-done((bf16[1,512,896]{2,1,0:T(8,128)(2,1)S(1)}, bf16[1,512,896]{2,1,0:T(8,128)(2,1)}, u32[]{:S(2)}) %copy-start.6) | copy-done | bytes 917528
  4.7 1.1 %shard_map.143 = (bf16[8,32,1536]{2,1,0:T(8,128)(2,1)S(1)}, bf16[8,32,1536]{2,1,0:T(8,128)(2,1)}, f32[1,128]{1,0:T(1,128)S(1)}) custom-call(bf16[16,32,896]{2,1,0:T(8,128)(2,1)S(1)} %bitcast.12, f32[16,4096]{1,0:T(8,128)S(1)} %copy-done, f32[16,4096]{1,0:T(8,128)S(1)} %copy-done.2, f32[16,4096]{1,0:T(8,128)S(1)} %copy-done.4), custom_call_target="tpu_custom_call" | custom-call | flops 4000000 | bytes 4096 | tf_op jit(solution)/shard_map/pallas_call | solution.py:357
  5.8 1.4 %collective-permute-start = (bf16[8,32,1536]{2,1,0:T(8,128)(2,1)}, bf16[8,32,1536]{2,1,0:T(8,128)(2,1)S(1)}, u32[]{:S(2)}, u32[]{:S(2)}) collective-permute-start(bf16[8,32,1536]{2,1,0:T(8,128)(2,1)} %get-tuple-element.33), channel_id=1, source_target_pairs={{0,1},{1,0},{2,3},{3,2},{4,5},{5,4},{6,7},{7,6},{8,9},{9,8},{10,11... | collective-permute-start | bytes 2359304 | tf_op jit(solution)/shard_map/ppermute | solution.py:362
  7.2 5.2 %all-to-all-start = ((bf16[8,256,256]{2,1,0:T(8,128)(2,1)}), bf16[8,256,256]{2,1,0:T(8,128)(2,1)S(1)}, u32[]{:S(2)}, u32[]{:S(2)}) async-start(bf16[8,256,256]{2,1,0:T(8,128)(2,1)} %bitcast.14), calls=%async_computation | async-start | bytes 2097152 | tf_op jit(solution)/shard_map/all_to_all | solution.py:353
  12.4 0.0 collective-permute-done.swapped
  12.4 0.9 shard_map.145
  13.3 1.6 %collective-permute-start.1 = (bf16[2,32,1536]{2,1,0:T(8,128)(2,1)S(1)}, bf16[2,32,1536]{2,1,0:T(8,128)(2,1)S(1)}, u32[]{:S(2)}, u32[]{:S(2)}) collective-permute-start(bf16[2,32,1536]{2,1,0:T(8,128)(2,1)S(1)} %get-tuple-element.35), channel_id=1, source_target_pairs={{0,4},{2,6},{4,8},{6,10},{8,12},{10,14},{12,0},{14,2},{1,5},{3,7},... | collective-permute-start | bytes 589832 | tf_op jit(solution)/shard_map/ppermute | solution.py:366
  14.9 2.1 %collective-permute-start.2 = (bf16[2,32,1536]{2,1,0:T(8,128)(2,1)S(1)}, bf16[2,32,1536]{2,1,0:T(8,128)(2,1)S(1)}, u32[]{:S(2)}, u32[]{:S(2)}) collective-permute-start(bf16[2,32,1536]{2,1,0:T(8,128)(2,1)S(1)} %get-tuple-element.36), channel_id=1, source_target_pairs={{0,12},{2,14},{4,0},{6,2},{8,4},{10,6},{12,8},{14,10},{1,13},{3,15... | collective-permute-start | bytes 589832 | tf_op jit(solution)/shard_map/ppermute | solution.py:366
  17.0 1.3 %collective-permute-start.3 = (bf16[2,32,1536]{2,1,0:T(8,128)(2,1)}, bf16[2,32,1536]{2,1,0:T(8,128)(2,1)S(1)}, u32[]{:S(2)}, u32[]{:S(2)}) collective-permute-start(bf16[2,32,1536]{2,1,0:T(8,128)(2,1)} %get-tuple-element.37), channel_id=1, source_target_pairs={{0,8},{2,10},{4,12},{6,14},{8,0},{10,2},{12,4},{14,6},{1,9},{3,11}... | collective-permute-start | bytes 589832 | tf_op jit(solution)/shard_map/ppermute | solution.py:366
  18.3 2.5 %collective-permute-start.4 = (bf16[2,32,1536]{2,1,0:T(8,128)(2,1)}, bf16[2,32,1536]{2,1,0:T(8,128)(2,1)S(1)}, u32[]{:S(2)}, u32[]{:S(2)}) collective-permute-start(bf16[2,32,1536]{2,1,0:T(8,128)(2,1)} %get-tuple-element.38), channel_id=1, source_target_pairs={{0,2},{2,0},{4,6},{6,4},{8,10},{10,8},{12,14},{14,12},{1,3},{3,1},... | collective-permute-start | bytes 589832 | tf_op jit(solution)/shard_map/ppermute | solution.py:366
  20.8 1.0 %collective-permute-start.5 = (bf16[2,32,1536]{2,1,0:T(8,128)(2,1)S(1)}, bf16[2,32,1536]{2,1,0:T(8,128)(2,1)S(1)}, u32[]{:S(2)}, u32[]{:S(2)}) collective-permute-start(bf16[2,32,1536]{2,1,0:T(8,128)(2,1)S(1)} %get-tuple-element.39), channel_id=1, source_target_pairs={{0,6},{2,4},{4,10},{6,8},{8,14},{10,12},{12,2},{14,0},{1,7},{3,5},... | collective-permute-start | bytes 589832 | tf_op jit(solution)/shard_map/ppermute | solution.py:366
  21.8 0.3 collective-permute-done.1.refs_1_
  22.0 3.8 %collective-permute-start.6 = (bf16[2,32,1536]{2,1,0:T(8,128)(2,1)S(1)}, bf16[2,32,1536]{2,1,0:T(8,128)(2,1)S(1)}, u32[]{:S(2)}, u32[]{:S(2)}) collective-permute-start(bf16[2,32,1536]{2,1,0:T(8,128)(2,1)S(1)} %get-tuple-element.40), channel_id=1, source_target_pairs={{0,14},{2,12},{4,2},{6,0},{8,6},{10,4},{12,10},{14,8},{1,15},{3,13... | collective-permute-start | bytes 589832 | tf_op jit(solution)/shard_map/ppermute | solution.py:366
  25.9 0.0 collective-permute-done.2.refs_2_
  25.9 0.7 collective-permute-start.7
  26.6 0.8 all-to-all-done.arrived
  27.4 0.3 shard_map.144
  27.6 23.5 %all_to_all.15 = f32[128,1,128]{2,1,0:T(1,128)S(1)} all-to-all(f32[128,1,128]{2,1,0:T(1,128)S(1)} %bitcast.13), channel_id=1, replica_groups=mesh['gx_0'=2,'gx_1'=4,'gy_0'=4,'gy_1'=2,'gy_2'=2] {'gx_0','gx_1','gy_0'..., dimensions={0} | all-to-all | bytes 131072 | tf_op jit(solution)/shard_map/all_to_all | solution.py:371
  51.1 0.0 collective-permute-done.3.refs_3_
  51.1 0.0 collective-permute-done.4.refs_4_
  51.1 0.0 collective-permute-done.5.refs_5_
  51.1 0.0 collective-permute-done.6.refs_6_
  51.1 0.0 collective-permute-done.7.refs_7_
  51.1 1.2 %shard_map.147 = (bf16[256,256]{1,0:T(8,128)(2,1)S(1)}, f32[3,1,32,1792]{3,2,1,0:T(8,128)S(1)}) custom-call(f32[128,128]{1,0:T(8,128)S(1)} %bitcast.8, f32[256,256]{1,0:T(8,128)S(1)} %get-tuple-element.45.attn, bf16[2,32,1536]{2,1,0:T(8,128)(2,1)S(1)} %get-tuple-element.34.refs_0_, bf16[2,32,1536]{2,1,0:T(8,128)(2,1)S(1)} %collective-permute-done.1.refs_1_, ...), custom_call_target="tpu_custom_call" | custom-call | flops 2000000 | bytes 4096 | tf_op jit(solution)/shard_map/pallas_call | solution.py:378
  52.4 3.7 %shard_map.148 = bf16[16,32,1024]{2,1,0:T(8,128)(2,1)} custom-call(f32[128,128]{1,0:T(8,128)S(1)} %bitcast.9, f32[256,256]{1,0:T(8,128)S(1)} %get-tuple-element.45.attn, bf16[2,32,1536]{2,1,0:T(8,128)(2,1)S(1)} %get-tuple-element.34.refs_0_, bf16[2,32,1536]{2,1,0:T(8,128)(2,1)S(1)} %collective-permute-done.1.refs_1_, ...), custom_call_target="tpu_custom_call" | custom-call | flops 8000000 | bytes 4096 | tf_op jit(solution)/shard_map/pallas_call | solution.py:387
  56.0 4.4 %all-to-all-start.2 = ((bf16[16,32,1024]{2,1,0:T(8,128)(2,1)}), bf16[16,32,1024]{2,1,0:T(8,128)(2,1)S(1)}, u32[]{:S(2)}, u32[]{:S(2)}) async-start(bf16[16,32,1024]{2,1,0:T(8,128)(2,1)} %shard_map.148), calls=%async_computation.2 | async-start | bytes 2097152 | tf_op jit(solution)/shard_map/all_to_all | solution.py:400
  60.4 0.4 collective-permute-start.11
  60.8 0.5 collective-permute-start.8
  61.3 2.2 %collective-permute-start.9 = (bf16[256,256]{1,0:T(8,128)(2,1)S(1)}, bf16[256,256]{1,0:T(8,128)(2,1)S(1)}, u32[]{:S(2)}, u32[]{:S(2)}) collective-permute-start(bf16[256,256]{1,0:T(8,128)(2,1)S(1)} %get-tuple-element.51.refs_0_), channel_id=1, source_target_pairs={{0,48},{16,0},{32,16},{48,32},{1,49},{17,1},{33,17},{49,33},{2,50}... | collective-permute-start | bytes 393224 | tf_op jit(solution)/shard_map/ppermute | solution.py:406
  63.5 0.0 collective-permute-start.10
  63.5 12.6 %collective-permute-done.11.refs_4_ = bf16[256,256]{1,0:T(8,128)(2,1)S(1)} collective-permute-done((bf16[256,256]{1,0:T(8,128)(2,1)S(1)}, bf16[256,256]{1,0:T(8,128)(2,1)S(1)}, u32[]{:S(2)}, u32[]{:S(2)}) %collective-permute-start.11) | collective-permute-done | bytes 131104 | tf_op jit(solution)/shard_map/ppermute | solution.py:386
  76.1 0.6 collective-permute-start.12
  76.6 2.1 %collective-permute-start.13 = (bf16[256,256]{1,0:T(8,128)(2,1)S(1)}, bf16[256,256]{1,0:T(8,128)(2,1)S(1)}, u32[]{:S(2)}, u32[]{:S(2)}) collective-permute-start(bf16[256,256]{1,0:T(8,128)(2,1)S(1)} %collective-permute-done.11.refs_4_), channel_id=1, source_target_pairs={{0,48},{16,0},{32,16},{48,32},{1,49},{17,1},{33,17},{49,33},{2,50}... | collective-permute-start | bytes 393224 | tf_op jit(solution)/shard_map/ppermute | solution.py:406
  78.8 0.0 collective-permute-done.8.refs_1_
  78.8 0.0 collective-permute-start.14
  78.8 5.3 %shard_map.146 = (f32[32,14336]{1,0:T(8,128)}, f32[32,14336]{1,0:T(8,128)}, f32[32,14336]{1,0:T(8,128)}) custom-call(f32[128,128]{1,0:T(8,128)S(1)} %bitcast.10, bf16[2,32,1536]{2,1,0:T(8,128)(2,1)S(1)} %get-tuple-element.34.refs_0_, bf16[2,32,1536]{2,1,0:T(8,128)(2,1)S(1)} %collective-permute-done.1.refs_1_, ...), custom_call_target="tpu_custom_call" | custom-call | flops 8000000 | bytes 4096 | tf_op jit(solution)/shard_map/pallas_call | solution.py:408
  84.1 0.0 copy-start.1
  84.1 0.0 copy-start.3
  84.1 0.0 copy-start.5
  84.1 0.0 collective-permute-done.9.refs_2_
  84.1 0.0 collective-permute-done.10.refs_3_
  84.2 0.0 collective-permute-done.12.refs_5_
  84.2 0.0 collective-permute-done.13.refs_6_
  84.2 0.0 collective-permute-done.14.refs_7_
  84.2 1.0 %shard_map.150 = bf16[8,256,256]{2,1,0:T(8,128)(2,1)} custom-call(bf16[256,256]{1,0:T(8,128)(2,1)S(1)} %get-tuple-element.51.refs_0_, bf16[256,256]{1,0:T(8,128)(2,1)S(1)} %collective-permute-done.8.refs_1_, bf16[256,256]{1,0:T(8,128)(2,1)S(1)} %collective-permute-done.9.refs_2_, bf16[256,256]{1,0:T(8,128)(2,1)S(1)} %collective-permute-done.10.refs_3_, ...), custom_call_target="tpu_custom_call" | custom-call | flops 1000000 | bytes 4096 | tf_op jit(solution)/shard_map/pallas_call | solution.py:423
  85.2 0.0 all-to-all-done.2.arrived
  85.2 0.0 copy-done.1
  85.3 0.0 copy-done.3
  85.3 0.2 copy-done.5
  85.5 1.5 %shard_map.149 = (bf16[16,32,896]{2,1,0:T(8,128)(2,1)}, f32[16,4096]{1,0:T(8,128)}, f32[16,4096]{1,0:T(8,128)}, f32[16,4096]{1,0:T(8,128)}) custom-call(f32[128,128]{1,0:T(8,128)S(1)} %bitcast.11, bf16[16,32,1024]{2,1,0:T(8,128)(2,1)S(1)} %all-to-all-done.2.arrived, f32[16,4096]{1,0:T(8,128)S(1)} %copy-done.1, f32[16,4096]{1,0:T(8,128)S(1)} %copy-done.3, ...), custom_call_target="tpu_custom_call" | custom-call | flops 2000000 | bytes 4096 | tf_op jit(solution)/shard_map/pallas_call | solution.py:431
Async XLA Ops:
  0.6 1.0 %copy-start = (f32[16,4096]{1,0:T(8,128)S(1)}, f32[16,4096]{1,0:T(8,128)}, u32[]{:S(2)}) copy-start(f32[16,4096]{1,0:T(8,128)} %refs_0_.1) | copy-start | bytes 786436
  1.6 0.9 %copy-start.2 = (f32[16,4096]{1,0:T(8,128)S(1)}, f32[16,4096]{1,0:T(8,128)}, u32[]{:S(2)}) copy-start(f32[16,4096]{1,0:T(8,128)} %refs_1_.1) | copy-start | bytes 786436
  2.5 0.9 %copy-start.4 = (f32[16,4096]{1,0:T(8,128)S(1)}, f32[16,4096]{1,0:T(8,128)}, u32[]{:S(2)}) copy-start(f32[16,4096]{1,0:T(8,128)} %refs_2_.1) | copy-start | bytes 786436
  3.5 1.2 %copy-start.6 = (bf16[1,512,896]{2,1,0:T(8,128)(2,1)S(1)}, bf16[1,512,896]{2,1,0:T(8,128)(2,1)}, u32[]{:S(2)}) copy-start(bf16[1,512,896]{2,1,0:T(8,128)(2,1)} %param.8) | copy-start | bytes 2752516
  5.8 6.6 %collective-permute-start = (bf16[8,32,1536]{2,1,0:T(8,128)(2,1)}, bf16[8,32,1536]{2,1,0:T(8,128)(2,1)S(1)}, u32[]{:S(2)}, u32[]{:S(2)}) collective-permute-start(bf16[8,32,1536]{2,1,0:T(8,128)(2,1)} %get-tuple-element.33), channel_id=1, source_target_pairs={{0,1},{1,0},{2,3},{3,2},{4,5},{5,4},{6,7},{7,6},{8,9},{9,8},{10,11... | collective-permute-start | bytes 2359304 | tf_op jit(solution)/shard_map/ppermute | solution.py:362
  7.2 20.2 %all-to-all-start = ((bf16[8,256,256]{2,1,0:T(8,128)(2,1)}), bf16[8,256,256]{2,1,0:T(8,128)(2,1)S(1)}, u32[]{:S(2)}, u32[]{:S(2)}) async-start(bf16[8,256,256]{2,1,0:T(8,128)(2,1)} %bitcast.14), calls=%async_computation | async-start | bytes 2097152 | tf_op jit(solution)/shard_map/all_to_all | solution.py:353
  13.3 8.8 %collective-permute-start.1 = (bf16[2,32,1536]{2,1,0:T(8,128)(2,1)S(1)}, bf16[2,32,1536]{2,1,0:T(8,128)(2,1)S(1)}, u32[]{:S(2)}, u32[]{:S(2)}) collective-permute-start(bf16[2,32,1536]{2,1,0:T(8,128)(2,1)S(1)} %get-tuple-element.35), channel_id=1, source_target_pairs={{0,4},{2,6},{4,8},{6,10},{8,12},{10,14},{12,0},{14,2},{1,5},{3,7},... | collective-permute-start | bytes 589832 | tf_op jit(solution)/shard_map/ppermute | solution.py:366
  14.9 11.0 %collective-permute-start.2 = (bf16[2,32,1536]{2,1,0:T(8,128)(2,1)S(1)}, bf16[2,32,1536]{2,1,0:T(8,128)(2,1)S(1)}, u32[]{:S(2)}, u32[]{:S(2)}) collective-permute-start(bf16[2,32,1536]{2,1,0:T(8,128)(2,1)S(1)} %get-tuple-element.36), channel_id=1, source_target_pairs={{0,12},{2,14},{4,0},{6,2},{8,4},{10,6},{12,8},{14,10},{1,13},{3,15... | collective-permute-start | bytes 589832 | tf_op jit(solution)/shard_map/ppermute | solution.py:366
  17.0 34.1 %collective-permute-start.3 = (bf16[2,32,1536]{2,1,0:T(8,128)(2,1)}, bf16[2,32,1536]{2,1,0:T(8,128)(2,1)S(1)}, u32[]{:S(2)}, u32[]{:S(2)}) collective-permute-start(bf16[2,32,1536]{2,1,0:T(8,128)(2,1)} %get-tuple-element.37), channel_id=1, source_target_pairs={{0,8},{2,10},{4,12},{6,14},{8,0},{10,2},{12,4},{14,6},{1,9},{3,11}... | collective-permute-start | bytes 589832 | tf_op jit(solution)/shard_map/ppermute | solution.py:366
  18.3 32.8 %collective-permute-start.4 = (bf16[2,32,1536]{2,1,0:T(8,128)(2,1)}, bf16[2,32,1536]{2,1,0:T(8,128)(2,1)S(1)}, u32[]{:S(2)}, u32[]{:S(2)}) collective-permute-start(bf16[2,32,1536]{2,1,0:T(8,128)(2,1)} %get-tuple-element.38), channel_id=1, source_target_pairs={{0,2},{2,0},{4,6},{6,4},{8,10},{10,8},{12,14},{14,12},{1,3},{3,1},... | collective-permute-start | bytes 589832 | tf_op jit(solution)/shard_map/ppermute | solution.py:366
  20.8 30.3 %collective-permute-start.5 = (bf16[2,32,1536]{2,1,0:T(8,128)(2,1)S(1)}, bf16[2,32,1536]{2,1,0:T(8,128)(2,1)S(1)}, u32[]{:S(2)}, u32[]{:S(2)}) collective-permute-start(bf16[2,32,1536]{2,1,0:T(8,128)(2,1)S(1)} %get-tuple-element.39), channel_id=1, source_target_pairs={{0,6},{2,4},{4,10},{6,8},{8,14},{10,12},{12,2},{14,0},{1,7},{3,5},... | collective-permute-start | bytes 589832 | tf_op jit(solution)/shard_map/ppermute | solution.py:366
  22.0 29.1 %collective-permute-start.6 = (bf16[2,32,1536]{2,1,0:T(8,128)(2,1)S(1)}, bf16[2,32,1536]{2,1,0:T(8,128)(2,1)S(1)}, u32[]{:S(2)}, u32[]{:S(2)}) collective-permute-start(bf16[2,32,1536]{2,1,0:T(8,128)(2,1)S(1)} %get-tuple-element.40), channel_id=1, source_target_pairs={{0,14},{2,12},{4,2},{6,0},{8,6},{10,4},{12,10},{14,8},{1,15},{3,13... | collective-permute-start | bytes 589832 | tf_op jit(solution)/shard_map/ppermute | solution.py:366
  25.9 25.3 %collective-permute-start.7 = (bf16[2,32,1536]{2,1,0:T(8,128)(2,1)S(1)}, bf16[2,32,1536]{2,1,0:T(8,128)(2,1)S(1)}, u32[]{:S(2)}, u32[]{:S(2)}) collective-permute-start(bf16[2,32,1536]{2,1,0:T(8,128)(2,1)S(1)} %get-tuple-element.41), channel_id=1, source_target_pairs={{0,10},{2,8},{4,14},{6,12},{8,2},{10,0},{12,6},{14,4},{1,11},{3,9}... | collective-permute-start | bytes 589832 | tf_op jit(solution)/shard_map/ppermute | solution.py:366
  56.0 29.2 %all-to-all-start.2 = ((bf16[16,32,1024]{2,1,0:T(8,128)(2,1)}), bf16[16,32,1024]{2,1,0:T(8,128)(2,1)S(1)}, u32[]{:S(2)}, u32[]{:S(2)}) async-start(bf16[16,32,1024]{2,1,0:T(8,128)(2,1)} %shard_map.148), calls=%async_computation.2 | async-start | bytes 2097152 | tf_op jit(solution)/shard_map/all_to_all | solution.py:400
  60.4 15.7 %collective-permute-start.11 = (bf16[256,256]{1,0:T(8,128)(2,1)S(1)}, bf16[256,256]{1,0:T(8,128)(2,1)S(1)}, u32[]{:S(2)}, u32[]{:S(2)}) collective-permute-start(bf16[256,256]{1,0:T(8,128)(2,1)S(1)} %get-tuple-element.51.refs_0_), channel_id=1, source_target_pairs={{0,64},{64,0},{1,65},{65,1},{2,66},{66,2},{3,67},{67,3},{4,68},{68... | collective-permute-start | bytes 393224 | tf_op jit(solution)/shard_map/ppermute | solution.py:386
  60.8 17.9 %collective-permute-start.8 = (bf16[256,256]{1,0:T(8,128)(2,1)S(1)}, bf16[256,256]{1,0:T(8,128)(2,1)S(1)}, u32[]{:S(2)}, u32[]{:S(2)}) collective-permute-start(bf16[256,256]{1,0:T(8,128)(2,1)S(1)} %get-tuple-element.51.refs_0_), channel_id=1, source_target_pairs={{0,16},{16,32},{32,48},{48,0},{1,17},{17,33},{33,49},{49,1},{2,18}... | collective-permute-start | bytes 393224 | tf_op jit(solution)/shard_map/ppermute | solution.py:406
  61.3 22.8 %collective-permute-start.9 = (bf16[256,256]{1,0:T(8,128)(2,1)S(1)}, bf16[256,256]{1,0:T(8,128)(2,1)S(1)}, u32[]{:S(2)}, u32[]{:S(2)}) collective-permute-start(bf16[256,256]{1,0:T(8,128)(2,1)S(1)} %get-tuple-element.51.refs_0_), channel_id=1, source_target_pairs={{0,48},{16,0},{32,16},{48,32},{1,49},{17,1},{33,17},{49,33},{2,50}... | collective-permute-start | bytes 393224 | tf_op jit(solution)/shard_map/ppermute | solution.py:406
  63.5 20.6 %collective-permute-start.10 = (bf16[256,256]{1,0:T(8,128)(2,1)S(1)}, bf16[256,256]{1,0:T(8,128)(2,1)S(1)}, u32[]{:S(2)}, u32[]{:S(2)}) collective-permute-start(bf16[256,256]{1,0:T(8,128)(2,1)S(1)} %get-tuple-element.51.refs_0_), channel_id=1, source_target_pairs={{0,32},{16,48},{32,0},{48,16},{1,33},{17,49},{33,1},{49,17},{2,34}... | collective-permute-start | bytes 393224 | tf_op jit(solution)/shard_map/ppermute | solution.py:406
  76.1 8.1 %collective-permute-start.12 = (bf16[256,256]{1,0:T(8,128)(2,1)S(1)}, bf16[256,256]{1,0:T(8,128)(2,1)S(1)}, u32[]{:S(2)}, u32[]{:S(2)}) collective-permute-start(bf16[256,256]{1,0:T(8,128)(2,1)S(1)} %collective-permute-done.11.refs_4_), channel_id=1, source_target_pairs={{0,16},{16,32},{32,48},{48,0},{1,17},{17,33},{33,49},{49,1},{2,18}... | collective-permute-start | bytes 393224 | tf_op jit(solution)/shard_map/ppermute | solution.py:406
  76.6 7.5 %collective-permute-start.13 = (bf16[256,256]{1,0:T(8,128)(2,1)S(1)}, bf16[256,256]{1,0:T(8,128)(2,1)S(1)}, u32[]{:S(2)}, u32[]{:S(2)}) collective-permute-start(bf16[256,256]{1,0:T(8,128)(2,1)S(1)} %collective-permute-done.11.refs_4_), channel_id=1, source_target_pairs={{0,48},{16,0},{32,16},{48,32},{1,49},{17,1},{33,17},{49,33},{2,50}... | collective-permute-start | bytes 393224 | tf_op jit(solution)/shard_map/ppermute | solution.py:406
  78.8 5.4 %collective-permute-start.14 = (bf16[256,256]{1,0:T(8,128)(2,1)S(1)}, bf16[256,256]{1,0:T(8,128)(2,1)S(1)}, u32[]{:S(2)}, u32[]{:S(2)}) collective-permute-start(bf16[256,256]{1,0:T(8,128)(2,1)S(1)} %collective-permute-done.11.refs_4_), channel_id=1, source_target_pairs={{0,32},{16,48},{32,0},{48,16},{1,33},{17,49},{33,1},{49,17},{2,34}... | collective-permute-start | bytes 393224 | tf_op jit(solution)/shard_map/ppermute | solution.py:406
  84.1 1.1 %copy-start.1 = (f32[16,4096]{1,0:T(8,128)S(1)}, f32[16,4096]{1,0:T(8,128)}, u32[]{:S(2)}) copy-start(f32[16,4096]{1,0:T(8,128)} %refs_0_.1) | copy-start | bytes 786436
  84.1 1.1 %copy-start.3 = (f32[16,4096]{1,0:T(8,128)S(1)}, f32[16,4096]{1,0:T(8,128)}, u32[]{:S(2)}) copy-start(f32[16,4096]{1,0:T(8,128)} %refs_1_.1) | copy-start | bytes 786436
  84.1 1.4 %copy-start.5 = (f32[16,4096]{1,0:T(8,128)S(1)}, f32[16,4096]{1,0:T(8,128)}, u32[]{:S(2)}) copy-start(f32[16,4096]{1,0:T(8,128)} %refs_2_.1) | copy-start | bytes 786436
